TPU v7x, 256 devices: a whole 4x4x8 slice. The times are simulated.
256 devices in a mesh: row: 8 (over x, core), col: 32 (over z, y).
Axes of the slice: x: 4, y: 4, z: 8, core: 2. Of those that a mesh axis runs over, the one named last changes fastest.
Arguments:
- momentum: bfloat16 [8192, 32768], P('row', 'col'), may hold values from -240 to 240
- gradient: bfloat16 [8192, 32768], P('row', 'col'), may hold values from -6 to 6
- right_basis: float32 [32768, 256], P('col'), may hold values from -0.03125 to 0.03125
Outputs:
- new_momentum: bfloat16 [8192, 32768], P('row', 'col')
- new_basis: float32 [32768, 256], P('col')
- update: float32 [8192, 32768], P('row', 'col')
All inputs are finite; a program needn't handle non-finite values.
Results may differ from a plain program's by a relative error of at most 0.001.
Values sent between devices are 32-bit elements; how exact they have to be, the bound alone decides.
No kernel may reach another device: no remote copies, remote signals or barrier semaphores. Data moves between devices by JAX's collectives and lax.ppermute only.
A program may use at most 64 MiB of HBM per device.

v0:
```python
import math

import jax
import jax.numpy as jnp
from jax import lax
from jax.sharding import Mesh
from jax.sharding import PartitionSpec as P

ROWS = 8192
COLS = 32768
RANK = 256
COL = ("col_0", "col_1")
ROW = ("row_0", "row_1")


eps = 1e-08
momentum_decay = 0.95


def in_blocks(array, dim, length):
    shape = array.shape
    tiles = array.reshape(*shape[:dim], length, shape[dim] // length, *shape[dim + 1 :])
    return jnp.moveaxis(tiles, dim, 0)


def sent_and_summed(array, axis, dim):
    tiles = in_blocks(array, dim, lax.axis_size(axis))
    arrived = lax.all_to_all(tiles, axis, split_axis=0, concat_axis=0, tiled=True)
    return arrived.sum(axis=0)


def rows_for(lines, length):
    spare = -len(lines) % length
    return jnp.pad(lines, [(0, spare)] + [(0, 0)] * (lines.ndim - 1))


def laid_out(tiles, dim):
    shape = list(tiles.shape[1:])
    shape[dim] *= tiles.shape[0]
    return jnp.moveaxis(tiles, 0, dim).reshape(shape)


def from_everyone(array, axis):
    length = lax.axis_size(axis)
    return lax.all_to_all(
        jnp.broadcast_to(array[None], (length, *array.shape)), axis, 0, 0, tiled=True
    )


def gather_directly(array, axis, dim):
    return laid_out(from_everyone(array, axis), dim)


def total_of(array, axes):
    lines = array.reshape(-1, array.shape[-1])
    own = sent_and_summed(rows_for(lines, lax.axis_size(axes)), axes, 0)
    whole = gather_directly(own, axes, 0)
    return whole[: len(lines)].reshape(array.shape)


def taken_together(array, axis):
    return from_everyone(array, axis).sum(axis=0)


def one_axis_at_a_time(array, axes):
    far, near = axes
    nearer = taken_together(array, near)
    return taken_together(nearer, far)


def in_one_piece(arrays, axis, dim, along):
    widths = [a.shape[along] for a in arrays]
    both = jnp.concatenate(arrays, axis=along)
    result = lax.all_gather(both, axis, axis=dim, tiled=True)
    return tuple(jnp.split(result, [sum(widths[:k]) for k in range(1, len(widths))], axis=along))


def contract_first(left_side, right_side):
    return lax.dot_general(
        left_side, right_side, (((0,), (0,)), ((), ())), precision=lax.Precision.HIGHEST
    )


def contract_last(left_side, right_side):
    return lax.dot_general(
        left_side, right_side, (((1,), (1,)), ((), ())), precision=lax.Precision.HIGHEST
    )


def shards(momentum, gradient, right_basis):
    highest = lax.Precision.HIGHEST
    summed = momentum.astype(jnp.float32) + gradient.astype(jnp.float32)
    projected = total_of(jnp.dot(summed, right_basis, precision=highest), COL)
    gram_matrix = taken_together(contract_first(projected, projected), ROW)
    factor = jnp.linalg.cholesky(gram_matrix)
    orthonormal = jax.scipy.linalg.solve_triangular(factor, projected.T, lower=True).T
    transposed_share = sent_and_summed(contract_first(summed, orthonormal), ROW, 0)
    squares = one_axis_at_a_time(
        jnp.sum(transposed_share * transposed_share, axis=0), ("row_0", ("row_1", "col_0", "col_1"))
    )
    basis_share = transposed_share / (jnp.sqrt(squares)[None, :] + eps)
    new_basis, transposed = in_one_piece((basis_share, transposed_share), ROW, 0, 1)
    new_momentum = (
        summed - (1.0 - momentum_decay) * contract_last(orthonormal, transposed)
    ).astype(jnp.bfloat16)
    rms_scale = math.sqrt(ROWS * COLS / RANK)
    update = rms_scale * contract_last(orthonormal, new_basis)
    return (new_momentum, new_basis, update)


def solution(mesh):
    split = Mesh(mesh.devices.reshape(4, 2, 8, 4), ("row_0", "row_1", "col_0", "col_1"))
    placed = (P(ROW, COL), P(ROW, COL), P(COL, None))
    return jax.shard_map(
        shards,
        mesh=split,
        in_specs=placed,
        out_specs=(P(ROW, COL), P(COL, None), P(ROW, COL)),
        check_vma=False,
    )
```

profile of v0, /device:TPU:1, one launch (start us, length us, event | category | flops | bytes accessed | tf_op | source)
XLA Modules:
  0.0 292.8 jit_solution(9293507561759242949)
XLA Ops:
  7.2 0.0 copy-start
  7.2 1.2 copy-done
  8.4 5.4 %fusion.1 = f32[1024,256]{1,0:T(8,128)S(1)} fusion(f32[1024,256]{1,0:T(8,128)S(1)} %copy-done, bf16[1024,1024]{1,0:T(8,128)(2,1)} %param.4, bf16[1024,1024]{1,0:T(8,128)(2,1)} %param.3), kind=kOutput, calls=%fused_computation.5 | convolution fusion | flops 3224371200 | bytes 6291456 | tf_op jit(solution)/shard_map/dot_general | solution.py:93
  13.8 38.0 %all_to_all.32 = f32[32,32,256]{2,1,0:T(8,128)S(1)} all-to-all(f32[32,32,256]{2,1,0:T(8,128)S(1)} %bitcast.44), channel_id=1, replica_groups=mesh['row_0'=4,'row_1'=2,'col_0'=8,'col_1'=4] {'col_0','col_1'}, dimensions={0} | all-to-all | bytes 2097152 | tf_op jit(solution)/shard_map/all_to_all | solution.py:28
  51.8 0.1 reduce_sum.54
  51.9 0.1 broadcast_in_dim.10
  52.0 31.6 %all_to_all.33 = f32[32,32,256]{2,1,0:T(8,128)S(1)} all-to-all(f32[32,32,256]{2,1,0:T(8,128)S(1)} %broadcast_in_dim.10), channel_id=1, replica_groups=mesh['row_0'=4,'row_1'=2,'col_0'=8,'col_1'=4] {'col_0','col_1'}, dimensions={0} | all-to-all | bytes 2097152 | tf_op jit(solution)/shard_map/all_to_all | solution.py:45
  83.6 1.8 convolution_bitcast_fusion
  85.4 1.5 broadcast_in_dim.11
  86.9 7.9 %all-to-all-start.2 = ((f32[8,256,256]{2,1,0:T(8,128)}), f32[8,256,256]{2,1,0:T(8,128)S(1)}, u32[]{:S(2)}, u32[]{:S(2)}) async-start(f32[8,256,256]{2,1,0:T(8,128)} %broadcast_in_dim.11), calls=%async_computation.2 | async-start | bytes 4194304 | tf_op jit(solution)/shard_map/all_to_all | solution.py:45
  94.9 2.5 copy.9
  97.4 23.7 %all-to-all-done.2 = f32[8,256,256]{2,1,0:T(8,128)S(1)} async-done(((f32[8,256,256]{2,1,0:T(8,128)}), f32[8,256,256]{2,1,0:T(8,128)S(1)}, u32[]{:S(2)}, u32[]{:S(2)}) %all-to-all-start.2) | async-done | bytes 2097184 | tf_op jit(solution)/shard_map/all_to_all | solution.py:45
  121.1 0.1 reduce_sum.55
  121.2 0.0 copy-start.1
  121.2 0.8 copy.8
  122.1 1.0 fusion.5
  123.0 0.0 copy-start.12
  123.1 0.7 copy-done.12
  123.8 11.7 %cholesky.50 = f32[128,128]{1,0:T(8,128)S(1)} custom-call(f32[128,128]{1,0:T(8,128)S(1)} %cholesky.118), custom_call_target="Cholesky" | custom-call | tf_op jit(solution)/shard_map/jit(cholesky)/cholesky | solution.py:95
  135.5 9.8 %custom-call.15 = f32[1,128,128]{1,2,0:T(8,128)S(1)} custom-call(f32[1,128,128]{2,1,0:T(8,128)S(1)} %get-tuple-element.24), custom_call_target="InvertDiagBlocksLowerTriangular" | custom-call | tf_op jit(solution)/shard_map/jit(cholesky)/cholesky | solution.py:95
  145.3 1.0 constant_dynamic-update-slice_fusion.1
  146.4 1.1 convolution_subtract_fusion.1
  147.5 11.7 %cholesky.105 = f32[128,128]{1,0:T(8,128)S(1)} custom-call(f32[128,128]{1,0:T(8,128)S(1)} %convolution_subtract_fusion.1), custom_call_target="Cholesky" | custom-call | tf_op jit(solution)/shard_map/jit(cholesky)/cholesky | solution.py:95
  159.3 0.7 compare_reduce_fusion
  161.3 1.0 select_select_fusion
  162.3 0.1 triangular_solve.57
  162.4 5.4 %while.1 = (s32[]{:T(128)}, f32[256,256]{1,0:T(8,128)S(1)}, s32[2,2]{1,0:T(2,128)S(1)}, f32[2,128,128]{2,1,0:T(8,128)}, s32[]{:T(128)}) while((s32[]{:T(128)}, f32[256,256]{1,0:T(8,128)S(1)}, s32[2,2]{1,0:T(2,128)S(1)}, f32[2,128,128]{2,1,0:T(8,128)}, s32[]{:T(128)}) %tuple.27), condition=%wide.while_cond, body=%wide.while_body.sunk | while | flops 2 | bytes 132205 | solution.py:96
  162.6 0.6 fusion.24
  163.2 2.0 bitcast_dynamic-update-slice_fusion.2
  165.2 0.6 fusion.24
  165.7 2.0 bitcast_dynamic-update-slice_fusion.2
  167.8 20.5 %custom-call.16 = f32[2,128,128]{1,2,0:T(8,128)S(1)} custom-call(f32[2,128,128]{2,1,0:T(8,128)} %get-tuple-element.10), custom_call_target="InvertDiagBlocksLowerTriangular" | custom-call | tf_op jit(solution)/shard_map/jit(_solve_triangular)/triangular_solve | solution.py:96
  188.3 1.8 fusion.3
  190.1 1.8 convolution_subtract_fusion
  191.9 0.6 fusion.7
  192.6 0.0 copy-start.6
  192.6 6.8 %fusion = f32[1024,256]{1,0:T(8,128)S(1)} fusion(bf16[1024,1024]{1,0:T(8,128)(2,1)S(1)} %copy-done.1, bf16[1024,1024]{1,0:T(8,128)(2,1)S(1)} %copy-done.2, f32[128,1024]{1,0:T(8,128)S(1)} %fusion.7, f32[128,1024]{1,0:T(8,128)S(1)} %fusion.3), kind=kOutput, calls=%fused_computation.4 | convolution fusion | flops 3224633344 | bytes 6291456 | tf_op jit(solution)/shard_map/dot_general | solution.py:79
  199.4 19.0 %all_to_all.34 = f32[8,128,256]{2,1,0:T(8,128)} all-to-all(f32[8,128,256]{2,1,0:T(8,128)S(1)} %bitcast.45), channel_id=1, replica_groups=mesh['row_0'=4,'row_1'=2,'col_0'=8,'col_1'=4] {'row_0','row_1'}, dimensions={0} | all-to-all | bytes 2097152 | tf_op jit(solution)/shard_map/all_to_all | solution.py:28
  218.4 1.3 reduce_sum.56
  219.8 16.3 %all_to_all.35 = f32[64,1,256]{2,1,0:T(1,128)S(1)} all-to-all(f32[64,1,256]{2,1,0:T(1,128)S(1)} %broadcast_in_dim.12), channel_id=1, replica_groups=mesh['row_0'=4,'row_1'=2,'col_0'=8,'col_1'=4] {'row_1','col_0','col_1'}, dimensions={0} | all-to-all | bytes 131072 | tf_op jit(solution)/shard_map/all_to_all | solution.py:45
  236.1 0.1 reduce_sum.58
  236.2 6.5 %all_to_all.36 = f32[4,1,256]{2,1,0:T(1,128)S(1)} all-to-all(f32[4,1,256]{2,1,0:T(1,128)S(1)} %broadcast_in_dim.13), channel_id=1, replica_groups=mesh['row_0'=4,'row_1'=2,'col_0'=8,'col_1'=4] {'row_0'}, dimensions={0} | all-to-all | bytes 8192 | tf_op jit(solution)/shard_map/all_to_all | solution.py:45
  242.7 0.7 pad_maximum_fusion.4
  243.4 0.0 all-gather.2.cloned.1.call-update
  243.5 22.4 %all-gather.2.cloned.1.call-done = f32[1024,512]{1,0:T(8,128)} async-done(((f32[128,512]{1,0:T(8,128)}), f32[1024,512]{1,0:T(8,128)}) %all-gather.2.cloned.1.call-update) | async-done | bytes 2097168 | tf_op jit(solution)/shard_map/all_gather | solution.py:74
  265.9 1.4 split.9
  267.3 10.2 %convolution_multiply_fusion = f32[1024,1024]{1,0:T(8,128)} fusion(f32[1024,256]{1,0:T(8,128)S(1)} %split.9, f32[128,1024]{1,0:T(8,128)} %copy-done.6, f32[128,1024]{1,0:T(8,128)} %copy-done.4), kind=kOutput, calls=%fused_computation.6 | convolution fusion | flops 3222536192 | bytes 6291456 | tf_op jit(solution)/shard_map/dot_general | solution.py:85
  277.6 8.4 %subtract_convert_fusion = bf16[1024,1024]{1,0:T(8,128)(2,1)} fusion(bf16[1024,1024]{1,0:T(8,128)(2,1)S(1)} %copy-done.1, bf16[1024,1024]{1,0:T(8,128)(2,1)S(1)} %copy-done.3, f32[1024,512]{1,0:T(8,128)S(1)} %copy-done.10, f32[128,1024]{1,0:T(8,128)S(1)} %copy-done.7, f32[128,1024]{1,0:T(8,128)S(1)} %copy-done.5), kind=kOutput, calls=%fused_computation.2 | convolution fusion | flops 3227779072 | bytes 8388608 | tf_op jit(solution)/shard_map/dot_general | solution.py:85
  (35 shorter events, 0.3 us)
Async XLA Ops:
  7.2 1.2 copy-start
  83.6 3.3 %copy-start.8 = (f32[32,32,256]{2,1,0:T(8,128)}, f32[32,32,256]{2,1,0:T(8,128)S(1)}, u32[]{:S(2)}) copy-start(f32[32,32,256]{2,1,0:T(8,128)S(1)} %all_to_all.33) | copy-start | bytes 3145732
  86.9 34.1 %all-to-all-start.2 = ((f32[8,256,256]{2,1,0:T(8,128)}), f32[8,256,256]{2,1,0:T(8,128)S(1)}, u32[]{:S(2)}, u32[]{:S(2)}) async-start(f32[8,256,256]{2,1,0:T(8,128)} %broadcast_in_dim.11), calls=%async_computation.2 | async-start | bytes 4194304 | tf_op jit(solution)/shard_map/all_to_all | solution.py:45
  94.9 171.0 %all-gather.2.cloned.1.call-start = ((), (), s32[]{:S(2)}) async-start(), calls=%async_computation.6 | async-start | bytes 2359296 | tf_op jit(solution)/shard_map/all_gather | solution.py:74
  121.2 71.3 %copy-start.1 = (bf16[1024,1024]{1,0:T(8,128)(2,1)S(1)}, bf16[1024,1024]{1,0:T(8,128)(2,1)}, u32[]{:S(2)}) copy-start(bf16[1024,1024]{1,0:T(8,128)(2,1)} %param.4) | copy-start | bytes 6291460
  123.0 0.7 copy-start.12
  159.3 2.1 copy-start.11
  188.2 4.3 %copy-start.2 = (bf16[1024,1024]{1,0:T(8,128)(2,1)S(1)}, bf16[1024,1024]{1,0:T(8,128)(2,1)}, u32[]{:S(2)}) copy-start(bf16[1024,1024]{1,0:T(8,128)(2,1)} %param.3) | copy-start | bytes 6291460
  190.1 9.3 %copy-start.4 = (f32[128,1024]{1,0:T(8,128)}, f32[128,1024]{1,0:T(8,128)S(1)}, u32[]{:S(2)}) copy-start(f32[128,1024]{1,0:T(8,128)S(1)} %fusion.3) | copy-start | bytes 1572868
  192.6 6.8 %copy-start.6 = (f32[128,1024]{1,0:T(8,128)}, f32[128,1024]{1,0:T(8,128)S(1)}, u32[]{:S(2)}) copy-start(f32[128,1024]{1,0:T(8,128)S(1)} %fusion.7) | copy-start | bytes 1572868
  265.9 11.7 %copy-start.3 = (bf16[1024,1024]{1,0:T(8,128)(2,1)S(1)}, bf16[1024,1024]{1,0:T(8,128)(2,1)}, u32[]{:S(2)}) copy-start(bf16[1024,1024]{1,0:T(8,128)(2,1)} %param.3) | copy-start | bytes 6291460
  265.9 11.7 %copy-start.5 = (f32[128,1024]{1,0:T(8,128)S(1)}, f32[128,1024]{1,0:T(8,128)}, u32[]{:S(2)}) copy-start(f32[128,1024]{1,0:T(8,128)} %copy-done.4) | copy-start | bytes 1572868
  265.9 11.7 %copy-start.7 = (f32[128,1024]{1,0:T(8,128)S(1)}, f32[128,1024]{1,0:T(8,128)}, u32[]{:S(2)}) copy-start(f32[128,1024]{1,0:T(8,128)} %copy-done.6) | copy-start | bytes 1572868
  265.9 11.7 %copy-start.10 = (f32[1024,512]{1,0:T(8,128)S(1)}, f32[1024,512]{1,0:T(8,128)}, u32[]{:S(2)}) copy-start(f32[1024,512]{1,0:T(8,128)} %all-gather.2.cloned.1.call-done) | copy-start | bytes 6291460
  267.3 18.6 %copy-start.9 = (f32[1024,256]{1,0:T(8,128)}, f32[1024,256]{1,0:T(8,128)S(1)}, u32[]{:S(2)}) copy-start(f32[1024,256]{1,0:T(8,128)S(1)} %split.9) | copy-start | bytes 3145732
Sparse Core Ops, SparseCore 0:
  243.6 22.2 all-gather.1
where the time goes:
time: 294 us; the launch traced here: 293 us
  blocking collectives  111 us (38%)
  other arithmetic  58.9 us (20%)
  waiting for transfers between devices  46.1 us (16%)
  matrix products  39.1 us (13%)
  between operations  15.6 us (5%)
  local copies, waits for them, and re-layouts  13.7 us (5%)
  starting transfers between devices  7.93 us (3%)
    all_to_all x2, blocking collectives, sent_and_summed(): lax.all_to_all(tiles, axis, split_axis=0, concat_axis=0, tiled=True)  57 us
    all_to_all x3, blocking collectives, from_everyone(): lax.all_to_all(jnp.broadcast_to(array[None], (length, *array.shape)), axi...  54.3 us
    another operation x6, other arithmetic, shards(): factor = jnp.linalg.cholesky(gram_matrix)  34 us
    all_to_all x1, waiting for transfers between devices, from_everyone(): lax.all_to_all(jnp.broadcast_to(array[None], (length, *array.shape)), axi...  23.7 us
    all_gather x1, waiting for transfers between devices, in_one_piece(): result = lax.all_gather(both, axis, axis=dim, tiled=True)  22.4 us
    another operation x3, other arithmetic, shards(): jax.scipy.linalg.solve_triangular(factor, projected.T, lower=True)  21.5 us
    dot_general x2, matrix products, contract_last(): lax.dot_general(left_side, right_side, (((1,), (1,)), ((), ())), precisio...  18.6 us
    dot_general x2, matrix products, contract_first(): lax.dot_general(left_side, right_side, (((0,), (0,)), ((), ())), precisio...  8.63 us
  transfers between devices with their start and end apart: 2, of which 2 were waited for; matrix products, arithmetic and copies ran while one was open for 1% of the time, Pallas kernels for 0%

commit v1 on v0

v1 whole, which is shorter than its diff:
```python
import math

import jax
import jax.numpy as jnp
from jax import lax
from jax.sharding import Mesh
from jax.sharding import PartitionSpec as P

ROWS = 8192
COLS = 32768
RANK = 256
COL = ("z", "y")
ROW = ("x", "c")


eps = 1e-08
momentum_decay = 0.95


def scattered(array, axis):
    tiles = array.reshape(lax.axis_size(axis), -1, array.shape[-1])
    return lax.all_to_all(tiles, axis, 0, 0, tiled=True).sum(axis=0)


def from_everyone(array, axis):
    tiles = jnp.broadcast_to(array[None], (lax.axis_size(axis), *array.shape))
    return lax.all_to_all(tiles, axis, 0, 0, tiled=True)


def gathered(array, axis):
    return from_everyone(array, axis).reshape(-1, array.shape[-1])


def other_core(array):
    return lax.ppermute(array, "c", [(0, 1), (1, 0)])


def dot(left, right, left_dim, right_dim, precision):
    return lax.dot_general(
        left,
        right,
        (((left_dim,), (right_dim,)), ((), ())),
        precision=precision,
        preferred_element_type=jnp.float32,
    )


def in_core_order(core, own, other, dim=0):
    first = jnp.where(core == 0, own, other)
    second = jnp.where(core == 0, other, own)
    return jnp.concatenate((first, second), axis=dim)


def shards(momentum, gradient, right_basis):
    high, highest = lax.Precision.HIGH, lax.Precision.HIGHEST
    core = lax.axis_index("c")
    summed = momentum.astype(jnp.float32) + gradient.astype(jnp.float32)

    part = dot(summed, right_basis, 1, 0, high)
    own = scattered(scattered(part, "y"), "z")
    projected = gathered(gathered(own, "z"), "y")

    gram = dot(projected, projected, 0, 0, highest)
    wide = dot(summed, projected, 0, 0, high)
    halves = wide.reshape(2, -1, RANK)
    kept = lax.dynamic_index_in_dim(halves, core, 0, keepdims=False)
    given = lax.dynamic_index_in_dim(halves, 1 - core, 0, keepdims=False)
    wide_half = kept + other_core(given)
    gram = gram + other_core(gram)
    gram_half = lax.dynamic_slice_in_dim(gram, core * (RANK // 2), RANK // 2, 0)
    sides = lax.axis_size("x")
    tiles = jnp.concatenate(
        (
            wide_half.reshape(sides, -1, RANK),
            jnp.broadcast_to(gram_half[None], (sides, *gram_half.shape)),
        ),
        axis=1,
    )
    arrived = lax.all_to_all(tiles, "x", 0, 0, tiled=True).sum(axis=0)
    wide_own, gram_half = arrived[: -RANK // 2], arrived[-RANK // 2 :]
    gram_matrix = in_core_order(core, gram_half, other_core(gram_half))
    wide_half = gathered(wide_own, "x")
    wide = in_core_order(core, wide_half, other_core(wide_half))

    factor = jnp.linalg.cholesky(gram_matrix)
    inverse = jax.scipy.linalg.solve_triangular(
        factor, jnp.eye(RANK, dtype=jnp.float32), lower=True
    )
    orthonormal = dot(projected, inverse, 1, 1, highest)
    transposed = dot(wide, inverse, 1, 1, highest)

    squares = from_everyone(jnp.sum(transposed * transposed, axis=0)[None], COL).sum(axis=0)
    new_momentum = (
        summed - dot((1.0 - momentum_decay) * orthonormal, transposed, 1, 1, high)
    ).astype(jnp.bfloat16)
    new_basis = transposed / (jnp.sqrt(squares) + eps)
    rms_scale = math.sqrt(ROWS * COLS / RANK)
    update = dot(rms_scale * orthonormal, new_basis, 1, 1, high)
    return (new_momentum, new_basis, update)


def solution(mesh):
    split = Mesh(mesh.devices.reshape(4, 2, 8, 4), (*ROW, *COL))
    placed = (P(ROW, COL), P(ROW, COL), P(COL, None))
    return jax.shard_map(
        shards,
        mesh=split,
        in_specs=placed,
        out_specs=(P(ROW, COL), P(COL, None), P(ROW, COL)),
        check_vma=False,
    )
```

time: 294 us -> 199 us (0.68)
  blocking collectives: 111 us -> 66.8 us
  waiting for transfers between devices: 46.1 us -> 4.64 us
  between operations: 15.6 us -> 2.28 us
  matrix products: 39.1 us -> 26.5 us
  starting transfers between devices: 7.93 us -> 18.8 us
  other arithmetic: 58.9 us -> 64.1 us
    all_to_all x5 -> x4, blocking collectives: 111 us -> 66.8 us  [the longest x2 36.3 us: scattered(): return lax.all_to_all(tiles, axis, 0, 0, tiled=True).sum(axis=0)]
    all_gather x1 -> x0, waiting for transfers between devices: 22.4 us -> none  [in_one_piece(): result = lax.all_gather(both, axis, axis=dim, tiled=True)]
    all_to_all x1 -> x3, waiting for transfers between devices: 23.7 us -> 2.98 us  [from_everyone(): return lax.all_to_all(tiles, axis, 0, 0, tiled=True)]
    dot_general x5 -> x7, matrix products: 32.6 us -> 25.2 us  [dot(): lax.dot_general(left, right, (((left_dim,), (right_dim,)), ((), ())), pre...]
    ppermute x0 -> x4, starting transfers between devices: none -> 7.09 us  [other_core(): return lax.ppermute(array, 'c', [(0, 1), (1, 0)])]
    dot_general x0 -> x1, local copies, waits for them, and re-layouts: none -> 5.35 us  [dot(): lax.dot_general(left, right, (((left_dim,), (right_dim,)), ((), ())), pre...]
    dot_general x0 -> x1, other arithmetic: none -> 5.14 us  [dot(): lax.dot_general(left, right, (((left_dim,), (right_dim,)), ((), ())), pre...]
    all_to_all x1 -> x3, starting transfers between devices: 7.92 us -> 11.7 us  [from_everyone(): return lax.all_to_all(tiles, axis, 0, 0, tiled=True)]
  transfers between devices with their start and end apart: 2 -> 7, of which waited for: 2 -> 2; matrix products, arithmetic and copies ran while one was open for 1% -> 41% of each run, Pallas kernels for 0% -> 0%
where the time goes in v1:
time: 199 us; the launch traced here: 198 us
  blocking collectives  66.8 us (34%)
  other arithmetic  64.1 us (32%)
  matrix products  26.5 us (13%)
  starting transfers between devices  18.8 us (9%)
  local copies, waits for them, and re-layouts  14.4 us (7%)
  waiting for transfers between devices  4.64 us (2%)
  between operations  2.28 us (1%)
    all_to_all x2, blocking collectives, scattered(): return lax.all_to_all(tiles, axis, 0, 0, tiled=True).sum(axis=0)  36.3 us
    another operation x6, other arithmetic, shards(): factor = jnp.linalg.cholesky(gram_matrix)  34 us
    dot_general x7, matrix products, dot(): lax.dot_general(left, right, (((left_dim,), (right_dim,)), ((), ())), pre...  25.2 us
    another operation x3, other arithmetic, shards(): jax.scipy.linalg.solve_triangular(factor, jnp.eye(RANK, dtype=jnp.float32...  19.9 us
    all_to_all x1, blocking collectives, shards(): arrived = lax.all_to_all(tiles, 'x', 0, 0, tiled=True).sum(axis=0)  18.6 us
    all_to_all x1, blocking collectives, from_everyone(): return lax.all_to_all(tiles, axis, 0, 0, tiled=True)  11.9 us
    all_to_all x3, starting transfers between devices, from_everyone(): return lax.all_to_all(tiles, axis, 0, 0, tiled=True)  11.7 us
    ppermute x4, starting transfers between devices, other_core(): return lax.ppermute(array, 'c', [(0, 1), (1, 0)])  7.09 us
  transfers between devices with their start and end apart: 7, of which 2 were waited for; matrix products, arithmetic and copies ran while one was open for 41% of the time, Pallas kernels for 0%

profile of v1, /device:TPU:1, one launch (start us, length us, event | category | flops | bytes accessed | tf_op | source)
XLA Modules:
  0.0 197.6 jit_solution(11900364990374043580)
XLA Ops:
  0.6 1.2 copy-done
  1.9 4.2 %fusion.1 = f32[1024,256]{1,0:T(8,128)S(1)} fusion(f32[1024,256]{1,0:T(8,128)S(1)} %copy-done, bf16[1024,1024]{1,0:T(8,128)(2,1)} %param.4, bf16[1024,1024]{1,0:T(8,128)(2,1)} %param.3), kind=kOutput, calls=%fused_computation.5 | convolution fusion | flops 1613758464 | bytes 6291456 | tf_op jit(solution)/shard_map/dot_general | solution.py:39
  6.1 19.0 %all_to_all.35 = f32[4,256,256]{2,1,0:T(8,128)S(1)} all-to-all(f32[4,256,256]{2,1,0:T(8,128)S(1)} %bitcast.61), channel_id=1, replica_groups=mesh['x'=4,'c'=2,'z'=8,'y'=4] {'y'}, dimensions={0} | all-to-all | bytes 2097152 | tf_op jit(solution)/shard_map/all_to_all | solution.py:22
  25.2 17.2 %all_to_all.36 = f32[8,32,256]{2,1,0:T(8,128)S(1)} all-to-all(f32[8,32,256]{2,1,0:T(8,128)S(1)} %bitcast.63), channel_id=1, replica_groups=mesh['x'=4,'c'=2,'z'=8,'y'=4] {'z'}, dimensions={0} | all-to-all | bytes 524288 | tf_op jit(solution)/shard_map/all_to_all | solution.py:22
  42.5 11.9 %all_to_all.37 = f32[8,32,256]{2,1,0:T(8,128)S(1)} all-to-all(f32[8,32,256]{2,1,0:T(8,128)S(1)} %broadcast_in_dim.13), channel_id=1, replica_groups=mesh['x'=4,'c'=2,'z'=8,'y'=4] {'z'}, dimensions={0} | all-to-all | bytes 524288 | tf_op jit(solution)/shard_map/all_to_all | solution.py:27
  54.4 1.1 broadcast_in_dim.15
  55.4 3.5 %all-to-all-start.3 = ((f32[4,256,256]{2,1,0:T(8,128)}), f32[4,256,256]{2,1,0:T(8,128)S(1)}, u32[]{:S(2)}, u32[]{:S(2)}) async-start(f32[4,256,256]{2,1,0:T(8,128)} %broadcast_in_dim.15), calls=%async_computation.3 | async-start | bytes 2097152 | tf_op jit(solution)/shard_map/all_to_all | solution.py:27
  58.9 5.1 %fusion = f32[1024,1024]{0,1:T(8,128)} fusion(bf16[1024,1024]{1,0:T(8,128)(2,1)} %param.4, bf16[1024,1024]{1,0:T(8,128)(2,1)} %param.3), kind=kLoop, calls=%fused_computation.4 | loop fusion | flops 3145728 | bytes 8388608 | tf_op jit(solution)/shard_map/dot_general | solution.py:39
  64.1 5.3 %copy.24 = f32[1024,1024]{1,0:T(8,128)} copy(f32[1024,1024]{0,1:T(8,128)} %fusion) | data formatting | bytes 8388608 | tf_op jit(solution)/shard_map/dot_general | solution.py:39
  69.4 4.0 %fusion.26 = f32[2,512,256]{2,1,0:T(8,128)S(1)} fusion(f32[2,512,1024]{2,1,0:T(8,128)} %bitcast.60, f32[1024,256,1]{1,0,2:T(8,128)S(1)} %bitcast.58), kind=kOutput, calls=%fused_computation.62 | convolution fusion | flops 1610612736 | bytes 6291456 | tf_op jit(solution)/shard_map/dot_general | solution.py:39
  73.4 0.8 dynamic-slice_bitcast_fusion
  74.3 5.5 %collective-permute-start = (f32[512,256]{1,0:T(8,128)}, f32[512,256]{1,0:T(8,128)}, u32[]{:S(2)}, u32[]{:S(2)}) collective-permute-start(f32[512,256]{1,0:T(8,128)} %dynamic-slice_bitcast_fusion), channel_id=1, source_target_pairs={{0,32},{32,0},{1,33},{33,1},{2,34},{34,2},{3,35},{35,3},{4,36},{36... | collective-permute-start | bytes 1572872 | tf_op jit(solution)/shard_map/ppermute | solution.py:35
  79.8 1.8 convolution_bitcast_fusion
  81.6 0.1 collective-permute-start.1
  81.7 1.6 collective-permute-done.1
  83.4 0.9 dynamic-slice_add_fusion
  84.3 1.1 bitcast_add_fusion
  85.6 18.6 %all_to_all.38 = f32[4,256,256]{2,1,0:T(8,128)S(1)} all-to-all(f32[4,256,256]{2,1,0:T(8,128)S(1)} %pad_maximum_fusion), channel_id=1, replica_groups=mesh['x'=4,'c'=2,'z'=8,'y'=4] {'x'}, dimensions={0} | all-to-all | bytes 2097152 | tf_op jit(solution)/shard_map/all_to_all | solution.py:79
  104.3 0.1 copy.26
  104.4 1.4 collective-permute-start.2
  105.8 0.8 broadcast_in_dim.18
  106.6 4.3 %all-to-all-start.5 = ((f32[4,128,256]{2,1,0:T(8,128)}), f32[4,128,256]{2,1,0:T(8,128)}, u32[]{:S(2)}, u32[]{:S(2)}) async-start(f32[4,128,256]{2,1,0:T(8,128)} %broadcast_in_dim.18), calls=%async_computation.5 | async-start | bytes 1048576 | tf_op jit(solution)/shard_map/all_to_all | solution.py:27
  111.0 0.1 copy.21
  111.2 11.7 %cholesky.50 = f32[128,128]{1,0:T(8,128)S(1)} custom-call(f32[128,128]{1,0:T(8,128)S(1)} %cholesky.118), custom_call_target="Cholesky" | custom-call | tf_op jit(solution)/shard_map/jit(cholesky)/cholesky | solution.py:85
  123.0 9.8 %custom-call.15 = f32[1,128,128]{1,2,0:T(8,128)S(1)} custom-call(f32[1,128,128]{2,1,0:T(8,128)S(1)} %get-tuple-element.30), custom_call_target="InvertDiagBlocksLowerTriangular" | custom-call | tf_op jit(solution)/shard_map/jit(cholesky)/cholesky | solution.py:85
  132.8 0.2 constant_dynamic-update-slice_fusion
  133.0 0.3 convolution_subtract_fusion.1
  133.3 11.7 %cholesky.105 = f32[128,128]{1,0:T(8,128)S(1)} custom-call(f32[128,128]{1,0:T(8,128)S(1)} %convolution_subtract_fusion.1), custom_call_target="Cholesky" | custom-call | tf_op jit(solution)/shard_map/jit(cholesky)/cholesky | solution.py:85
  145.0 0.7 compare_reduce_fusion
  147.2 4.1 %while.1 = (s32[]{:T(128)}, f32[256,256]{1,0:T(8,128)S(1)}, s32[2,2]{1,0:T(2,128)S(1)}, f32[2,128,128]{2,1,0:T(8,128)S(1)}, s32[]{:T(128)}) while((s32[]{:T(128)}, f32[256,256]{1,0:T(8,128)S(1)}, s32[2,2]{1,0:T(2,128)S(1)}, f32[2,128,128]{2,1,0:T(8,128)S(1)}, s32[]{:T(128)}) %tuple.31), condition=%wide.while_cond, body=%wide.while_body.sunk | while | flops 2 | bytes 131181 | solution.py:86
  147.2 0.6 fusion.40
  147.8 1.4 bitcast_dynamic-update-slice_fusion.2
  149.3 0.6 fusion.40
  149.9 1.4 bitcast_dynamic-update-slice_fusion.2
  151.3 19.9 %custom-call.16 = f32[2,128,128]{1,2,0:T(8,128)S(1)} custom-call(f32[2,128,128]{2,1,0:T(8,128)S(1)} %get-tuple-element.10), custom_call_target="InvertDiagBlocksLowerTriangular" | custom-call | tf_op jit(solution)/shard_map/jit(_solve_triangular)/triangular_solve | solution.py:86
  171.2 0.3 fusion.13
  171.5 0.1 collective-permute-start.3
  171.6 0.3 convolution_subtract_fusion
  171.9 0.3 fusion.16
  172.2 2.0 %fusion.12 = f32[1024,256]{1,0:T(8,128)} fusion(f32[1024,256]{1,0:T(8,128)S(1)} %bitcast.59, f32[128,256]{1,0:T(8,128)S(1)} %fusion.16, f32[128,256]{1,0:T(8,128)S(1)} %fusion.13), kind=kOutput, calls=%fused_computation.32 | convolution fusion | flops 805371904 | bytes 2359296 | tf_op jit(solution)/shard_map/dot_general | solution.py:39
  174.2 1.3 broadcast_select_fusion.1
  175.5 2.0 %multiply_reduce_fusion = (f32[256]{0:T(256)S(1)}, f32[1024,256]{1,0:T(8,128)}) fusion(f32[128,256]{1,0:T(8,128)S(1)} %fusion.16, f32[128,256]{1,0:T(8,128)S(1)} %fusion.13, f32[512,256]{1,0:T(8,128)S(1)} %get-tuple-element.22, f32[512,256]{1,0:T(8,128)S(1)} %get-tuple-element.21), kind=kOutput, calls=%fused_computation.16 | convolution fusion | flops 806158080 | bytes 2360320 | tf_op jit(solution)/shard_map/dot_general | solution.py:39
  177.5 0.6 broadcast_in_dim.19
  178.1 3.9 %all-to-all-start.6 = ((f32[32,1,256]{2,1,0:T(1,128)}), f32[32,1,256]{2,1,0:T(1,128)S(1)}, u32[]{:S(2)}, u32[]{:S(2)}) async-start(f32[32,1,256]{2,1,0:T(1,128)} %broadcast_in_dim.19), calls=%async_computation.6 | async-start | bytes 65536 | tf_op jit(solution)/shard_map/all_to_all | solution.py:27
  182.0 5.7 %subtract_convert_fusion = bf16[1024,1024]{1,0:T(8,128)(2,1)} fusion(bf16[1024,1024]{1,0:T(8,128)(2,1)S(1)} %copy-done.1, bf16[1024,1024]{1,0:T(8,128)(2,1)} %param.3, f32[1024,256]{1,0:T(8,128)} %get-tuple-element.34, f32[1024,256]{1,0:T(8,128)} %fusion.12), kind=kOutput, calls=%fused_computation.2 | convolution fusion | flops 1616117760 | bytes 8388608 | tf_op jit(solution)/shard_map/dot_general | solution.py:39
  187.8 3.0 %all-to-all-done.6 = f32[32,1,256]{2,1,0:T(1,128)S(1)} async-done(((f32[32,1,256]{2,1,0:T(1,128)}), f32[32,1,256]{2,1,0:T(1,128)S(1)}, u32[]{:S(2)}, u32[]{:S(2)}) %all-to-all-start.6) | async-done | bytes 32800 | tf_op jit(solution)/shard_map/all_to_all | solution.py:27
  190.8 1.3 broadcast_divide_fusion
  192.1 5.5 %fusion.6 = f32[1024,1024]{1,0:T(8,128)} fusion(f32[1024,256]{1,0:T(8,128)S(1)} %broadcast_divide_fusion, f32[1024,256]{1,0:T(8,128)} %fusion.12), kind=kOutput, calls=%fused_computation.14 | convolution fusion | flops 1610874880 | bytes 6291456 | tf_op jit(solution)/shard_map/dot_general | solution.py:39
  (33 shorter events, 0.7 us)
Async XLA Ops:
  0.6 1.2 copy-start
  55.4 14.0 %all-to-all-start.3 = ((f32[4,256,256]{2,1,0:T(8,128)}), f32[4,256,256]{2,1,0:T(8,128)S(1)}, u32[]{:S(2)}, u32[]{:S(2)}) async-start(f32[4,256,256]{2,1,0:T(8,128)} %broadcast_in_dim.15), calls=%async_computation.3 | async-start | bytes 2097152 | tf_op jit(solution)/shard_map/all_to_all | solution.py:27
  74.3 10.0 %collective-permute-start = (f32[512,256]{1,0:T(8,128)}, f32[512,256]{1,0:T(8,128)}, u32[]{:S(2)}, u32[]{:S(2)}) collective-permute-start(f32[512,256]{1,0:T(8,128)} %dynamic-slice_bitcast_fusion), channel_id=1, source_target_pairs={{0,32},{32,0},{1,33},{33,1},{2,34},{34,2},{3,35},{35,3},{4,36},{36... | collective-permute-start | bytes 1572872 | tf_op jit(solution)/shard_map/ppermute | solution.py:35
  81.6 1.8 collective-permute-start.1
  104.4 6.6 %collective-permute-start.2 = (f32[128,256]{0,1:T(8,128)S(1)}, f32[128,256]{0,1:T(8,128)S(1)}, u32[]{:S(2)}, u32[]{:S(2)}) collective-permute-start(f32[128,256]{0,1:T(8,128)S(1)} %copy.26), channel_id=1, source_target_pairs={{0,32},{32,0},{1,33},{33,1},{2,34},{34,2},{3,35},{35,3},{4,36},{36... | collective-permute-start | bytes 393224 | tf_op jit(solution)/shard_map/ppermute | solution.py:35
  106.6 64.9 %all-to-all-start.5 = ((f32[4,128,256]{2,1,0:T(8,128)}), f32[4,128,256]{2,1,0:T(8,128)}, u32[]{:S(2)}, u32[]{:S(2)}) async-start(f32[4,128,256]{2,1,0:T(8,128)} %broadcast_in_dim.18), calls=%async_computation.5 | async-start | bytes 1048576 | tf_op jit(solution)/shard_map/all_to_all | solution.py:27
  171.5 2.7 %collective-permute-start.3 = (f32[512,256]{1,0:T(8,128)}, f32[512,256]{1,0:T(8,128)S(1)}, u32[]{:S(2)}, u32[]{:S(2)}) collective-permute-start(f32[512,256]{1,0:T(8,128)} %bitcast.16), channel_id=1, source_target_pairs={{0,32},{32,0},{1,33},{33,1},{2,34},{34,2},{3,35},{35,3},{4,36},{36... | collective-permute-start | bytes 1572872 | tf_op jit(solution)/shard_map/ppermute | solution.py:35
  174.2 7.8 %copy-start.1 = (bf16[1024,1024]{1,0:T(8,128)(2,1)S(1)}, bf16[1024,1024]{1,0:T(8,128)(2,1)}, u32[]{:S(2)}) copy-start(bf16[1024,1024]{1,0:T(8,128)(2,1)} %param.4) | copy-start | bytes 6291460
  178.1 12.6 %all-to-all-start.6 = ((f32[32,1,256]{2,1,0:T(1,128)}), f32[32,1,256]{2,1,0:T(1,128)S(1)}, u32[]{:S(2)}, u32[]{:S(2)}) async-start(f32[32,1,256]{2,1,0:T(1,128)} %broadcast_in_dim.19), calls=%async_computation.6 | async-start | bytes 65536 | tf_op jit(solution)/shard_map/all_to_all | solution.py:27
  192.1 5.5 %copy-start.2 = (f32[1024,256]{1,0:T(8,128)}, f32[1024,256]{1,0:T(8,128)S(1)}, u32[]{:S(2)}) copy-start(f32[1024,256]{1,0:T(8,128)S(1)} %broadcast_divide_fusion) | copy-start | bytes 3145732

commit v2 on v1

--- a/solution.py
+++ b/solution.py
@@ -3,6 +3,8 @@
 import jax
 import jax.numpy as jnp
 from jax import lax
+from jax.experimental import pallas as pl
+from jax.experimental.pallas import tpu as pltpu
 from jax.sharding import Mesh
 from jax.sharding import PartitionSpec as P
 
@@ -51,6 +53,75 @@
     return jnp.concatenate((first, second), axis=dim)
 
 
+def mxu(left, right, dims):
+    return lax.dot_general(left, right, (dims, ((), ())), preferred_element_type=jnp.float32)
+
+def parts(array):
+    top = array.astype(jnp.bfloat16)
+    return top, (array - top.astype(jnp.float32)).astype(jnp.bfloat16)
+
+def dot3(left, right, dims):
+    (a, b), (c, d) = parts(left), parts(right)
+    return mxu(a, c, dims) + (mxu(a, d, dims) + mxu(b, c, dims))
+
+def dot1(left, right, dims):
+    return mxu(left.astype(jnp.bfloat16), right.astype(jnp.bfloat16), dims)
+
+PLAIN = ((1,), (0,))
+FLIPPED = ((1,), (1,))
+
+def inverse_factor(gram_ref, out_ref, work):
+    shape = (RANK, RANK)
+    row, column = (lax.broadcasted_iota(jnp.int32, shape, d) for d in (0, 1))
+    eye = (row == column).astype(jnp.float32)
+    lower = jnp.where(row > column, 1.0, 0.5 * eye)
+    gram = gram_ref[...]
+    diagonal = gram * eye
+    along = lax.rsqrt(jnp.sum(diagonal, axis=0, keepdims=True))
+    down = lax.rsqrt(jnp.sum(diagonal, axis=1, keepdims=True))
+    scaled = gram * down * along
+
+    def step(guess, dot):
+        error = dot(dot(guess, scaled, PLAIN), guess, FLIPPED) - eye
+        return guess - dot1(error * lower, guess, PLAIN), error
+
+    guess = eye - (scaled - eye) * lower
+    guess, _ = step(guess, dot1)
+    guess, _ = step(guess, dot3)
+    guess, error = step(guess, dot3)
+    out_ref[...] = guess * along
+
+    @pl.when(jnp.logical_not(jnp.sum(error * error) < 1e-4))
+    def _():
+        work[:, :RANK] = gram
+        work[:, RANK:] = eye
+        rows = lax.broadcasted_iota(jnp.int32, (RANK, 1), 0)
+        lanes = lax.broadcasted_iota(jnp.int32, (1, RANK), 1)
+
+        def eliminate(i, carry):
+            line = work[pl.ds(i, 1), :]
+            pivot = jnp.sum(jnp.where(lanes == i, line[:, :RANK], 0.0), axis=1, keepdims=True)
+            root = lax.rsqrt(pivot)
+            line = line * root
+            whole = work[...]
+            beneath = jnp.sum(jnp.where(lanes == i, whole[:, :RANK], 0.0), axis=1, keepdims=True) * root
+            rest = whole - jnp.where(rows > i, beneath, 0.0) * line
+            work[...] = jnp.where(rows == i, line, rest)
+            return carry
+
+        lax.fori_loop(0, RANK, eliminate, 0)
+        out_ref[...] = jnp.where(row >= column, work[:, RANK:], 0.0)
+
+def inverted(gram):
+    return pl.pallas_call(
+        inverse_factor,
+        out_shape=jax.ShapeDtypeStruct((RANK, RANK), jnp.float32),
+        scratch_shapes=[pltpu.VMEM((RANK, 2 * RANK), jnp.float32)],
+        cost_estimate=pl.CostEstimate(flops=2*9*3*RANK**3, bytes_accessed=8*RANK**2, transcendentals=0),
+        name="inverse_factor",
+    )(gram)
+
+
 def shards(momentum, gradient, right_basis):
     high, highest = lax.Precision.HIGH, lax.Precision.HIGHEST
     core = lax.axis_index("c")
@@ -82,10 +153,7 @@
     wide_half = gathered(wide_own, "x")
     wide = in_core_order(core, wide_half, other_core(wide_half))
 
-    factor = jnp.linalg.cholesky(gram_matrix)
-    inverse = jax.scipy.linalg.solve_triangular(
-        factor, jnp.eye(RANK, dtype=jnp.float32), lower=True
-    )
+    inverse = inverted(gram_matrix)
     orthonormal = dot(projected, inverse, 1, 1, highest)
     transposed = dot(wide, inverse, 1, 1, highest)
 

time: 199 us -> 190 us (0.955)
  other arithmetic: 64.1 us -> 9.59 us
  Pallas kernels: 0 us -> 46.8 us
  blocking collectives: 66.8 us -> 79.1 us
  local copies, waits for them, and re-layouts: 14.4 us -> 9.21 us
  matrix products: 26.5 us -> 22.7 us
  starting transfers between devices: 18.8 us -> 15.6 us
    another operation x9 -> x0, other arithmetic: 54 us -> none  [the longest x6 34 us: shards(): factor = jnp.linalg.cholesky(gram_matrix)]
    pallas_call x0 -> x1, Pallas kernels: none -> 46.8 us  [inverted(): pl.pallas_call(inverse_factor, out_shape=jax.ShapeDtypeStruct((RANK, RANK...]
    all_to_all x1 -> x2, blocking collectives: 11.9 us -> 24.2 us  [from_everyone(): return lax.all_to_all(tiles, axis, 0, 0, tiled=True)]
    all_to_all x3 -> x2, starting transfers between devices: 11.7 us -> 7.42 us  [from_everyone(): return lax.all_to_all(tiles, axis, 0, 0, tiled=True)]
    another operation x9 -> x0, local copies, waits for them, and re-layouts: 4.16 us -> none
    dot_general x7, matrix products: 25.2 us -> 22.7 us  [dot(): lax.dot_general(left, right, (((left_dim,), (right_dim,)), ((), ())), pre...]
  transfers between devices with their start and end apart: 7 -> 6, of which waited for: 2 -> 3; matrix products, arithmetic and copies ran while one was open for 41% -> 11% of each run, Pallas kernels for 0% -> 25%
where the time goes in v2:
time: 190 us
  blocking collectives  79.1 us (42%)
  Pallas kernels  46.8 us (25%)
  matrix products  22.7 us (12%)
  starting transfers between devices  15.6 us (8%)
  other arithmetic  9.59 us (5%)
  local copies, waits for them, and re-layouts  9.21 us (5%)
  waiting for transfers between devices  5.79 us (3%)
    pallas_call x1, Pallas kernels, inverted(): pl.pallas_call(inverse_factor, out_shape=jax.ShapeDtypeStruct((RANK, RANK...  46.8 us
    all_to_all x2, blocking collectives, scattered(): return lax.all_to_all(tiles, axis, 0, 0, tiled=True).sum(axis=0)  36.3 us
    all_to_all x2, blocking collectives, from_everyone(): return lax.all_to_all(tiles, axis, 0, 0, tiled=True)  24.2 us
    dot_general x7, matrix products, dot(): lax.dot_general(left, right, (((left_dim,), (right_dim,)), ((), ())), pre...  22.7 us
    all_to_all x1, blocking collectives, shards(): arrived = lax.all_to_all(tiles, 'x', 0, 0, tiled=True).sum(axis=0)  18.6 us
    ppermute x4, starting transfers between devices, other_core(): return lax.ppermute(array, 'c', [(0, 1), (1, 0)])  8.19 us
    all_to_all x2, starting transfers between devices, from_everyone(): return lax.all_to_all(tiles, axis, 0, 0, tiled=True)  7.42 us
    dot_general x1, local copies, waits for them, and re-layouts, dot(): lax.dot_general(left, right, (((left_dim,), (right_dim,)), ((), ())), pre...  5.35 us
  transfers between devices with their start and end apart: 6, of which 3 were waited for; matrix products, arithmetic and copies ran while one was open for 11% of the time, Pallas kernels for 25%

profile of v2, /device:TPU:1, one launch (start us, length us, event | category | flops | bytes accessed | tf_op | source)
XLA Modules:
  0.0 189.6 jit_solution(6006833658918851497)
XLA Ops:
  0.6 0.0 copy-start
  0.6 1.2 copy-done
  1.9 4.2 %fusion.1 = f32[1024,256]{1,0:T(8,128)S(1)} fusion(f32[1024,256]{1,0:T(8,128)S(1)} %copy-done, bf16[1024,1024]{1,0:T(8,128)(2,1)} %param.4, bf16[1024,1024]{1,0:T(8,128)(2,1)} %param.3), kind=kOutput, calls=%fused_computation.3 | convolution fusion | flops 1613758464 | bytes 6291456 | tf_op jit(solution)/shard_map/dot_general | solution.py:41
  6.1 19.0 %all_to_all.35 = f32[4,256,256]{2,1,0:T(8,128)S(1)} all-to-all(f32[4,256,256]{2,1,0:T(8,128)S(1)} %bitcast.32), channel_id=1, replica_groups=mesh['x'=4,'c'=2,'z'=8,'y'=4] {'y'}, dimensions={0} | all-to-all | bytes 2097152 | tf_op jit(solution)/shard_map/all_to_all | solution.py:24
  25.1 0.1 reduce_sum.45
  25.2 17.2 %all_to_all.36 = f32[8,32,256]{2,1,0:T(8,128)S(1)} all-to-all(f32[8,32,256]{2,1,0:T(8,128)S(1)} %bitcast.34), channel_id=1, replica_groups=mesh['x'=4,'c'=2,'z'=8,'y'=4] {'z'}, dimensions={0} | all-to-all | bytes 524288 | tf_op jit(solution)/shard_map/all_to_all | solution.py:24
  42.5 11.9 %all_to_all.37 = f32[8,32,256]{2,1,0:T(8,128)S(1)} all-to-all(f32[8,32,256]{2,1,0:T(8,128)S(1)} %broadcast_in_dim.12), channel_id=1, replica_groups=mesh['x'=4,'c'=2,'z'=8,'y'=4] {'z'}, dimensions={0} | all-to-all | bytes 524288 | tf_op jit(solution)/shard_map/all_to_all | solution.py:29
  54.4 1.1 broadcast_in_dim.14
  55.4 3.5 %all-to-all-start.3 = ((f32[4,256,256]{2,1,0:T(8,128)}), f32[4,256,256]{2,1,0:T(8,128)S(1)}, u32[]{:S(2)}, u32[]{:S(2)}) async-start(f32[4,256,256]{2,1,0:T(8,128)} %broadcast_in_dim.14), calls=%async_computation.3 | async-start | bytes 2097152 | tf_op jit(solution)/shard_map/all_to_all | solution.py:29
  58.9 5.1 %fusion = f32[1024,1024]{0,1:T(8,128)} fusion(bf16[1024,1024]{1,0:T(8,128)(2,1)} %param.4, bf16[1024,1024]{1,0:T(8,128)(2,1)} %param.3), kind=kLoop, calls=%fused_computation.2 | loop fusion | flops 3145728 | bytes 8388608 | tf_op jit(solution)/shard_map/dot_general | solution.py:41
  64.1 5.3 %copy.14 = f32[1024,1024]{1,0:T(8,128)} copy(f32[1024,1024]{0,1:T(8,128)} %fusion) | data formatting | bytes 8388608 | tf_op jit(solution)/shard_map/dot_general | solution.py:41
  69.4 0.0 all-to-all-done.3
  69.4 4.0 %fusion.14 = f32[2,512,256]{2,1,0:T(8,128)S(1)} fusion(f32[2,512,1024]{2,1,0:T(8,128)} %bitcast.31, f32[1024,256,1]{1,0,2:T(8,128)S(1)} %bitcast.29), kind=kOutput, calls=%fused_computation.29 | convolution fusion | flops 1610612736 | bytes 6291456 | tf_op jit(solution)/shard_map/dot_general | solution.py:41
  73.4 0.8 dynamic-slice_bitcast_fusion
  74.3 5.5 %collective-permute-start = (f32[512,256]{1,0:T(8,128)}, f32[512,256]{1,0:T(8,128)}, u32[]{:S(2)}, u32[]{:S(2)}) collective-permute-start(f32[512,256]{1,0:T(8,128)} %dynamic-slice_bitcast_fusion), channel_id=1, source_target_pairs={{0,32},{32,0},{1,33},{33,1},{2,34},{34,2},{3,35},{35,3},{4,36},{36... | collective-permute-start | bytes 1572872 | tf_op jit(solution)/shard_map/ppermute | solution.py:37
  79.8 1.8 convolution_bitcast_fusion
  81.6 0.1 collective-permute-start.1
  81.7 1.6 collective-permute-done.1
  83.4 0.9 dynamic-slice_add_fusion
  84.3 0.0 collective-permute-done
  84.3 1.1 bitcast_add_fusion
  85.5 0.1 pad_maximum_fusion
  85.6 18.6 %all_to_all.38 = f32[4,256,256]{2,1,0:T(8,128)S(1)} all-to-all(f32[4,256,256]{2,1,0:T(8,128)S(1)} %pad_maximum_fusion), channel_id=1, replica_groups=mesh['x'=4,'c'=2,'z'=8,'y'=4] {'x'}, dimensions={0} | all-to-all | bytes 2097152 | tf_op jit(solution)/shard_map/all_to_all | solution.py:150
  104.2 0.1 reduce_sum.47
  104.3 1.4 collective-permute-start.2
  105.6 1.0 collective-permute-done.2
  106.7 12.3 %all_to_all.39 = f32[4,128,256]{2,1,0:T(8,128)} all-to-all(f32[4,128,256]{2,1,0:T(8,128)S(1)} %broadcast_in_dim.16), channel_id=1, replica_groups=mesh['x'=4,'c'=2,'z'=8,'y'=4] {'x'}, dimensions={0} | all-to-all | bytes 1048576 | tf_op jit(solution)/shard_map/all_to_all | solution.py:29
  119.0 1.2 collective-permute-start.3
  120.2 0.7 pad_maximum_fusion.1.gram_ref
  120.9 46.8 %inverse_factor.1 = f32[256,256]{1,0:T(8,128)} custom-call(f32[256,256]{1,0:T(8,128)} %pad_maximum_fusion.1.gram_ref), custom_call_target="tpu_custom_call" | custom-call | flops 905969664 | bytes 524288 | tf_op jit(solution)/shard_map/inverse_factor/pallas_call | solution.py:116
  167.8 0.0 copy-start.2
  167.8 2.0 %fusion.15 = f32[1024,256]{1,0:T(8,128)S(1)} fusion(f32[1024,256]{1,0:T(8,128)S(1)} %bitcast.30, f32[256,256]{1,0:T(8,128)} %inverse_factor.1), kind=kOutput, calls=%fused_computation.30 | convolution fusion | flops 805306368 | bytes 2359296 | tf_op jit(solution)/shard_map/dot_general | solution.py:41
  169.8 0.0 collective-permute-done.3
  169.8 1.3 broadcast_select_fusion.1
  171.1 0.0 copy-done.2
  171.1 1.0 multiply_reduce_fusion
  172.2 0.6 broadcast_in_dim.17
  172.8 3.9 %all-to-all-start.6 = ((f32[32,1,256]{2,1,0:T(1,128)}), f32[32,1,256]{2,1,0:T(1,128)S(1)}, u32[]{:S(2)}, u32[]{:S(2)}) async-start(f32[32,1,256]{2,1,0:T(1,128)} %broadcast_in_dim.17), calls=%async_computation.6 | async-start | bytes 65536 | tf_op jit(solution)/shard_map/all_to_all | solution.py:29
  176.7 5.7 %subtract_convert_fusion = bf16[1024,1024]{1,0:T(8,128)(2,1)} fusion(bf16[1024,1024]{1,0:T(8,128)(2,1)} %param.4, bf16[1024,1024]{1,0:T(8,128)(2,1)} %param.3, f32[1024,256]{1,0:T(8,128)S(1)} %get-tuple-element.9, f32[1024,256]{1,0:T(8,128)S(1)} %fusion.15), kind=kOutput, calls=%fused_computation | convolution fusion | flops 1616117760 | bytes 8388608 | tf_op jit(solution)/shard_map/dot_general | solution.py:41
  182.4 3.1 %all-to-all-done.6 = f32[32,1,256]{2,1,0:T(1,128)S(1)} async-done(((f32[32,1,256]{2,1,0:T(1,128)}), f32[32,1,256]{2,1,0:T(1,128)S(1)}, u32[]{:S(2)}, u32[]{:S(2)}) %all-to-all-start.6) | async-done | bytes 32800 | tf_op jit(solution)/shard_map/all_to_all | solution.py:29
  185.6 0.1 reduce_sum.49
  185.6 0.1 broadcast_divide_fusion
  185.7 0.0 copy-start.1
  185.7 3.9 %fusion.6 = f32[1024,1024]{1,0:T(8,128)} fusion(f32[1024,256]{1,0:T(8,128)S(1)} %broadcast_divide_fusion, f32[1024,256]{1,0:T(8,128)S(1)} %fusion.15), kind=kOutput, calls=%fused_computation.10 | convolution fusion | flops 1610874880 | bytes 6291456 | tf_op jit(solution)/shard_map/dot_general | solution.py:41
  189.6 0.0 copy-done.1
  (7 shorter events, 0.2 us)
Async XLA Ops:
  0.6 1.2 copy-start
  55.4 14.0 %all-to-all-start.3 = ((f32[4,256,256]{2,1,0:T(8,128)}), f32[4,256,256]{2,1,0:T(8,128)S(1)}, u32[]{:S(2)}, u32[]{:S(2)}) async-start(f32[4,256,256]{2,1,0:T(8,128)} %broadcast_in_dim.14), calls=%async_computation.3 | async-start | bytes 2097152 | tf_op jit(solution)/shard_map/all_to_all | solution.py:29
  74.3 10.0 %collective-permute-start = (f32[512,256]{1,0:T(8,128)}, f32[512,256]{1,0:T(8,128)}, u32[]{:S(2)}, u32[]{:S(2)}) collective-permute-start(f32[512,256]{1,0:T(8,128)} %dynamic-slice_bitcast_fusion), channel_id=1, source_target_pairs={{0,32},{32,0},{1,33},{33,1},{2,34},{34,2},{3,35},{35,3},{4,36},{36... | collective-permute-start | bytes 1572872 | tf_op jit(solution)/shard_map/ppermute | solution.py:37
  81.6 1.8 collective-permute-start.1
  104.3 2.3 %collective-permute-start.2 = (f32[128,256]{1,0:T(8,128)S(1)}, f32[128,256]{1,0:T(8,128)S(1)}, u32[]{:S(2)}, u32[]{:S(2)}) collective-permute-start(f32[128,256]{1,0:T(8,128)S(1)} %slice.8), channel_id=1, source_target_pairs={{0,32},{32,0},{1,33},{33,1},{2,34},{34,2},{3,35},{35,3},{4,36},{36... | collective-permute-start | bytes 393224 | tf_op jit(solution)/shard_map/ppermute | solution.py:37
  119.0 50.8 %collective-permute-start.3 = (f32[512,256]{1,0:T(8,128)}, f32[512,256]{1,0:T(8,128)}, u32[]{:S(2)}, u32[]{:S(2)}) collective-permute-start(f32[512,256]{1,0:T(8,128)} %bitcast.11), channel_id=1, source_target_pairs={{0,32},{32,0},{1,33},{33,1},{2,34},{34,2},{3,35},{35,3},{4,36},{36... | collective-permute-start | bytes 1572872 | tf_op jit(solution)/shard_map/ppermute | solution.py:37
  167.8 3.3 %copy-start.2 = (f32[256,256]{1,0:T(8,128)S(1)}, f32[256,256]{1,0:T(8,128)}, u32[]{:S(2)}) copy-start(f32[256,256]{1,0:T(8,128)} %inverse_factor.1) | copy-start | bytes 786436
  172.8 12.8 %all-to-all-start.6 = ((f32[32,1,256]{2,1,0:T(1,128)}), f32[32,1,256]{2,1,0:T(1,128)S(1)}, u32[]{:S(2)}, u32[]{:S(2)}) async-start(f32[32,1,256]{2,1,0:T(1,128)} %broadcast_in_dim.17), calls=%async_computation.6 | async-start | bytes 65536 | tf_op jit(solution)/shard_map/all_to_all | solution.py:29
  185.7 3.9 %copy-start.1 = (f32[1024,256]{1,0:T(8,128)}, f32[1024,256]{1,0:T(8,128)S(1)}, u32[]{:S(2)}) copy-start(f32[1024,256]{1,0:T(8,128)S(1)} %broadcast_divide_fusion) | copy-start | bytes 3145732

commit v3 on v2

v3 whole, which is shorter than its diff:
```python
import math

import jax
import jax.numpy as jnp
from jax import lax
from jax.experimental import pallas as pl
from jax.experimental.pallas import tpu as pltpu
from jax.sharding import Mesh
from jax.sharding import PartitionSpec as P

ROWS = 8192
COLS = 32768
RANK = 256
COL = ("z", "y")
ROW = ("x", "c")


eps = 1e-08
momentum_decay = 0.95


def scattered(array, axis):
    tiles = array.reshape(lax.axis_size(axis), -1, array.shape[-1])
    return lax.all_to_all(tiles, axis, 0, 0, tiled=True).sum(axis=0)


def from_everyone(array, axis):
    tiles = jnp.broadcast_to(array[None], (lax.axis_size(axis), *array.shape))
    return lax.all_to_all(tiles, axis, 0, 0, tiled=True)


def gathered(array, axis):
    return from_everyone(array, axis).reshape(-1, array.shape[-1])


def other_core(array):
    return lax.ppermute(array, "c", [(0, 1), (1, 0)])


def mxu(left, right, dims):
    return lax.dot_general(left, right, (dims, ((), ())), preferred_element_type=jnp.float32)

def parts(array):
    top = array.astype(jnp.bfloat16)
    return top, (array - top.astype(jnp.float32)).astype(jnp.bfloat16)

def dot3(left, right, dims):
    (a, b), (c, d) = parts(left), parts(right)
    return mxu(a, c, dims) + (mxu(a, d, dims) + mxu(b, c, dims))

def dot1(left, right, dims):
    return mxu(left.astype(jnp.bfloat16), right.astype(jnp.bfloat16), dims)

PLAIN = ((1,), (0,))
FLIPPED = ((1,), (1,))

def core_number():
    return lax.axis_index("c").astype(jnp.int32)[None]


def cost(flops):
    return pl.CostEstimate(flops=flops, bytes_accessed=0, transcendentals=0)


IN_VMEM = pl.BlockSpec(memory_space=pltpu.VMEM)
IN_SMEM = pl.BlockSpec(memory_space=pltpu.SMEM)
TILE = 256
HALF = RANK // 2
PACKED = 3 * HALF // 4


def wider(tile):
    return tile.astype(jnp.float32)


def split_dot(left, right, dims):
    (a, b), (c, d) = left, right
    return mxu(a, c, dims) + (mxu(a, d, dims) + mxu(b, c, dims))


def limit(mib):
    return pltpu.CompilerParams(vmem_limit_bytes=mib << 20)


def project_kernel(momentum, gradient, basis, out, top, low):
    a, b = parts(wider(momentum[...]) + wider(gradient[...]))
    top[...], low[...] = a, b
    right = parts(basis[...])
    rows = out.shape[0]

    @pl.when(pl.program_id(0) == 0)
    def _():
        out[...] = split_dot((a, b), right, PLAIN)

    @pl.when(pl.program_id(0) > 0)
    def _():
        out[...] += split_dot((a, b), right, PLAIN)


def project(momentum, gradient, basis):
    rows, columns = momentum.shape
    block = pl.BlockSpec((rows, TILE), lambda t: (0, t))
    split = jax.ShapeDtypeStruct((rows, columns), jnp.bfloat16)
    return pl.pallas_call(
        project_kernel,
        grid=(columns // TILE,),
        in_specs=[block, block, pl.BlockSpec((TILE, RANK), lambda t: (t, 0))],
        out_specs=[pl.BlockSpec((rows, RANK), lambda t: (0, 0)), block, block],
        out_shape=[jax.ShapeDtypeStruct((rows, RANK), jnp.float32), split, split],
        cost_estimate=cost(6 * rows * columns * RANK),
        compiler_params=limit(61),
        name="project",
    )(momentum, gradient, basis)


def widen_kernel(core, top, low, projected, outgoing, kept, flat_top, flat_low):
    half = kept.shape[0]
    across = parts(projected[...].T)
    flat_top[...], flat_low[...] = across

    for place, target in ((1 - core[0], outgoing), (core[0], kept)):

        @pl.loop(0, half // TILE)
        def _(t):
            span = pl.ds(pl.multiple_of(place * half + t * TILE, TILE), TILE)
            tile = split_dot(
                (flat_top[...], flat_low[...]), (top[:, span], low[:, span]), PLAIN
            )
            target[pl.ds(pl.multiple_of(t * TILE, TILE), TILE), :] = tile.T

    outgoing[half:, :] = split_dot(
        (flat_top[...], flat_low[...]), parts(projected[...]), PLAIN
    )


def widen(core, top, low, projected):
    rows, columns = top.shape
    return pl.pallas_call(
        widen_kernel,
        in_specs=[IN_SMEM, IN_VMEM, IN_VMEM, IN_VMEM],
        out_specs=[IN_VMEM, IN_VMEM],
        out_shape=[
            jax.ShapeDtypeStruct((columns // 2 + RANK, RANK), jnp.float32),
            jax.ShapeDtypeStruct((columns // 2, RANK), jnp.float32),
        ],
        scratch_shapes=[pltpu.VMEM((RANK, rows), jnp.bfloat16)] * 2,
        cost_estimate=cost(6 * rows * (columns + RANK) * RANK),
        compiler_params=limit(20),
        name="widen",
    )(core, top, low, projected)


def folded(block):
    half = block.shape[0] // 2
    return jnp.concatenate((block[:half], block[half:]), axis=1)


def unfolded(block):
    return jnp.concatenate((block[:, :HALF], block[:, HALF:]), axis=0)


def merge_kernel(core, outgoing, received, kept, out):
    sides = out.shape[0]
    each = kept.shape[0] // sides
    for side in range(sides):
        span = pl.ds(side * each, each)
        out[side, :each, :] = kept[span, :] + received[span, :]
    gram = outgoing[kept.shape[0] :, :] + received[kept.shape[0] :, :]
    corner = gram[HALF:, :HALF]

    def put(square, strip):
        for side in range(sides):
            out[side, each : each + HALF // 2, :] = folded(square)
            out[side, each + HALF // 2 :, :] = folded(strip)

    @pl.when(core[0] == 0)
    def _():
        put(gram[:HALF, :HALF], corner[: HALF // 2])

    @pl.when(core[0] == 1)
    def _():
        put(gram[HALF:, HALF:], corner[HALF // 2 :])


def merge(core, outgoing, received, kept, sides):
    each = kept.shape[0] // sides
    return pl.pallas_call(
        merge_kernel,
        in_specs=[IN_SMEM, IN_VMEM, IN_VMEM, IN_VMEM],
        out_specs=IN_VMEM,
        out_shape=jax.ShapeDtypeStruct((sides, each + PACKED, RANK), jnp.float32),
        cost_estimate=cost(kept.size),
        compiler_params=pltpu.CompilerParams(vmem_limit_bytes=8 << 20),
        name="merge",
    )(core, outgoing, received, kept)


def spread_kernel(arrived, tiles, gram_half):
    sides, each, _ = tiles.shape
    wide = arrived[0, :each, :]
    gram = arrived[0, each:, :]
    for side in range(1, sides):
        wide = wide + arrived[side, :each, :]
        gram = gram + arrived[side, each:, :]
    for side in range(sides):
        tiles[side] = wide
    gram_half[...] = gram


def spread(arrived):
    sides, lines, _ = arrived.shape
    return pl.pallas_call(
        spread_kernel,
        in_specs=[IN_VMEM],
        out_specs=[IN_VMEM, IN_VMEM],
        out_shape=[
            jax.ShapeDtypeStruct((sides, lines - PACKED, RANK), jnp.float32),
            jax.ShapeDtypeStruct((PACKED, RANK), jnp.float32),
        ],
        cost_estimate=cost(arrived.size),
        compiler_params=limit(6),
        name="spread",
    )(arrived)


def inverse_factor(core, own, other, projected, out_ref, orthonormal, work):
    first = jnp.where(core[0] == 0, own[...], other[...])
    second = jnp.where(core[0] == 0, other[...], own[...])
    corner = jnp.concatenate((unfolded(first[HALF // 2 :]), unfolded(second[HALF // 2 :])), axis=0)
    gram = jnp.concatenate(
        (
            jnp.concatenate((unfolded(first[: HALF // 2]), corner.T), axis=1),
            jnp.concatenate((corner, unfolded(second[: HALF // 2])), axis=1),
        ),
        axis=0,
    )
    shape = (RANK, RANK)
    row, column = (lax.broadcasted_iota(jnp.int32, shape, d) for d in (0, 1))
    eye = (row == column).astype(jnp.float32)
    lower = jnp.where(row > column, 1.0, 0.5 * eye)
    diagonal = gram * eye
    along = lax.rsqrt(jnp.sum(diagonal, axis=0, keepdims=True))
    down = lax.rsqrt(jnp.sum(diagonal, axis=1, keepdims=True))
    scaled = gram * down * along

    def step(guess, dot):
        error = dot(dot(guess, scaled, PLAIN), guess, FLIPPED) - eye
        return guess - dot1(error * lower, guess, PLAIN), error

    guess = eye - (scaled - eye) * lower
    guess, _ = step(guess, dot1)
    guess, _ = step(guess, dot3)
    guess, error = step(guess, dot3)
    out_ref[...] = guess * along

    @pl.when(jnp.logical_not(jnp.sum(error * error) < 1e-4))
    def _():
        work[:, :RANK] = gram
        work[:, RANK:] = eye
        rows = lax.broadcasted_iota(jnp.int32, (RANK, 1), 0)
        lanes = lax.broadcasted_iota(jnp.int32, (1, RANK), 1)

        def eliminate(i, carry):
            line = work[pl.ds(i, 1), :]
            pivot = jnp.sum(jnp.where(lanes == i, line[:, :RANK], 0.0), axis=1, keepdims=True)
            root = lax.rsqrt(pivot)
            line = line * root
            whole = work[...]
            beneath = jnp.sum(jnp.where(lanes == i, whole[:, :RANK], 0.0), axis=1, keepdims=True) * root
            rest = whole - jnp.where(rows > i, beneath, 0.0) * line
            work[...] = jnp.where(rows == i, line, rest)
            return carry

        lax.fori_loop(0, RANK, eliminate, 0)
        out_ref[...] = jnp.where(row >= column, work[:, RANK:], 0.0)

    right = parts(out_ref[...])

    @pl.loop(0, projected.shape[0] // TILE)
    def _(t):
        span = pl.ds(pl.multiple_of(t * TILE, TILE), TILE)
        orthonormal[span, :] = split_dot(parts(projected[span, :]), right, FLIPPED)


def inverted(core, own, other, projected):
    return pl.pallas_call(
        inverse_factor,
        in_specs=[IN_SMEM, IN_VMEM, IN_VMEM, IN_VMEM],
        out_specs=[IN_VMEM, IN_VMEM],
        out_shape=[
            jax.ShapeDtypeStruct((RANK, RANK), jnp.float32),
            jax.ShapeDtypeStruct(projected.shape, jnp.float32),
        ],
        scratch_shapes=[pltpu.VMEM((RANK, 2 * RANK), jnp.float32)],
        cost_estimate=cost(1 << 32),
        compiler_params=limit(12),
        name="inverse_factor",
    )(core, own, other, projected)


def transposed_kernel(wide, inverse, out, squares):
    c, d = parts(inverse[...])
    total = jnp.zeros((1, RANK), jnp.float32)
    for t in range(wide.shape[0] // TILE):
        span = slice(t * TILE, (t + 1) * TILE)
        a, b = parts(wide[span, :])
        tile = mxu(a, c, FLIPPED) + (mxu(a, d, FLIPPED) + mxu(b, c, FLIPPED))
        out[span, :] = tile
        total += jnp.sum(tile * tile, axis=0, keepdims=True)
    squares[...] = jnp.broadcast_to(total[None], squares.shape)


def transpose_of(wide, inverse, copies):
    return pl.pallas_call(
        transposed_kernel,
        in_specs=[IN_VMEM, IN_VMEM],
        out_specs=[IN_VMEM, IN_VMEM],
        out_shape=[
            jax.ShapeDtypeStruct(wide.shape, jnp.float32),
            jax.ShapeDtypeStruct((copies, 1, RANK), jnp.float32),
        ],
        cost_estimate=cost(6 * wide.size * RANK),
        compiler_params=pltpu.CompilerParams(vmem_limit_bytes=8 << 20),
        name="transposed",
    )(wide, inverse)


SPAN = 512


def momentum_kernel(core, momentum, gradient, orthonormal, own, other, out, top, low):
    @pl.when(pl.program_id(1) == 0)
    def _():
        top[...], low[...] = parts(jnp.where(pl.program_id(0) == 0, own[...], other[...]))

    left = parts((1.0 - momentum_decay) * orthonormal[...])
    product = split_dot(left, (top[...], low[...]), FLIPPED)
    out[...] = (wider(momentum[...]) + wider(gradient[...]) - product).astype(jnp.bfloat16)


def side_of(h, core):
    return h + core[0] - 2 * h * core[0]


def remembered(core, momentum, gradient, orthonormal, own, other):
    rows, half = orthonormal.shape[0], own.shape[0]
    block = pl.BlockSpec((SPAN, half), lambda h, t, core: (t, side_of(h, core)))
    whole = pl.BlockSpec((half, RANK), lambda h, t, core: (0, 0))
    split = pl.BlockSpec((half, RANK), lambda h, t, core: (h, 0))
    return pl.pallas_call(
        momentum_kernel,
        grid_spec=pltpu.PrefetchScalarGridSpec(
            num_scalar_prefetch=1,
            grid=(2, rows // SPAN),
            in_specs=[
                block,
                block,
                pl.BlockSpec((SPAN, RANK), lambda h, t, core: (t, 0)),
                whole,
                whole,
            ],
            out_specs=[block, split, split],
        ),
        out_shape=[
            jax.ShapeDtypeStruct((rows, 2 * half), jnp.bfloat16),
            jax.ShapeDtypeStruct((2 * half, RANK), jnp.bfloat16),
            jax.ShapeDtypeStruct((2 * half, RANK), jnp.bfloat16),
        ],
        cost_estimate=cost(1 << 32),
        compiler_params=pltpu.CompilerParams(vmem_limit_bytes=20 << 20),
        name="new_momentum",
    )(core, momentum, gradient, orthonormal, own, other)


def update_kernel(core, orthonormal, own, other, top, low, squares, update, basis):
    norms = jnp.sqrt(jnp.sum(squares[...], axis=0)) + eps

    @pl.when(pl.program_id(1) == 0)
    def _():
        basis[...] = jnp.where(pl.program_id(0) == 0, own[...], other[...]) / norms

    left = parts(orthonormal[...] * (math.sqrt(ROWS * COLS / RANK) / norms))
    update[...] = split_dot(left, (top[...], low[...]), FLIPPED)


def updated(core, orthonormal, own, other, top, low, squares):
    rows, half = orthonormal.shape[0], own.shape[0]
    whole = pl.BlockSpec((half, RANK), lambda h, t, core: (0, 0))
    split = pl.BlockSpec((half, RANK), lambda h, t, core: (h, 0))
    return pl.pallas_call(
        update_kernel,
        grid_spec=pltpu.PrefetchScalarGridSpec(
            num_scalar_prefetch=1,
            grid=(2, rows // SPAN),
            in_specs=[
                pl.BlockSpec((SPAN, RANK), lambda h, t, core: (t, 0)),
                whole,
                whole,
                split,
                split,
                pl.BlockSpec(squares.shape, lambda h, t, core: (0, 0, 0)),
            ],
            out_specs=[
                pl.BlockSpec((SPAN, half), lambda h, t, core: (t, side_of(h, core))),
                pl.BlockSpec((half, RANK), lambda h, t, core: (side_of(h, core), 0)),
            ],
        ),
        out_shape=[
            jax.ShapeDtypeStruct((rows, 2 * half), jnp.float32),
            jax.ShapeDtypeStruct((2 * half, RANK), jnp.float32),
        ],
        cost_estimate=cost(6 * rows * 2 * half * RANK),
        compiler_params=limit(20),
        name="update",
    )(core, orthonormal, own, other, top, low, squares)


def shards(momentum, gradient, right_basis):
    core = core_number()
    sides = lax.axis_size("x")

    part, top, low = project(momentum, gradient, right_basis)
    part, core = lax.optimization_barrier((part, core))
    own = scattered(scattered(part, "y"), "z")
    projected = gathered(gathered(own, "z"), "y")

    outgoing, kept = widen(core, top, low, projected)
    tiles = merge(core, outgoing, other_core(outgoing), kept, sides)
    tiles, gram_half = spread(lax.all_to_all(tiles, "x", 0, 0, tiled=True))
    wide_half = lax.all_to_all(tiles, "x", 0, 0, tiled=True).reshape(-1, RANK)

    inverse, orthonormal = inverted(core, gram_half, other_core(gram_half), projected)
    own, own_squares = transpose_of(wide_half, inverse, lax.axis_size(COL))
    squares = own_squares + other_core(own_squares)
    squares = lax.all_to_all(squares, COL, 0, 0, tiled=True)
    other = other_core(own)
    new_momentum, top, low = remembered(core, momentum, gradient, orthonormal, own, other)
    update, new_basis = updated(core, orthonormal, own, other, top, low, squares)
    return (new_momentum, new_basis, update)


def solution(mesh):
    split = Mesh(mesh.devices.reshape(4, 2, 8, 4), (*ROW, *COL))
    placed = (P(ROW, COL), P(ROW, COL), P(COL, None))
    return jax.shard_map(
        shards,
        mesh=split,
        in_specs=placed,
        out_specs=(P(ROW, COL), P(COL, None), P(ROW, COL)),
        check_vma=False,
    )
```

time: 190 us -> 171 us (0.900)
  matrix products: 22.7 us -> 0 us
  Pallas kernels: 46.8 us -> 66.4 us
  other arithmetic: 9.59 us -> 0.75 us
  local copies, waits for them, and re-layouts: 9.21 us -> 5.12 us
    dot_general x7 -> x0, matrix products: 22.7 us -> none  [dot(): lax.dot_general(left, right, (((left_dim,), (right_dim,)), ((), ())), pre...]
    pallas_call x1 -> x8, Pallas kernels: 46.8 us -> 66.4 us  [the longest x1 46.4 us: inverted(): pl.pallas_call(inverse_factor, in_specs=[IN_SMEM, IN_VMEM, IN_VMEM, IN_VM...]
    dot_general x1 -> x0, local copies, waits for them, and re-layouts: 5.35 us -> none  [dot(): lax.dot_general(left, right, (((left_dim,), (right_dim,)), ((), ())), pre...]
    dot_general x1 -> x0, other arithmetic: 5.14 us -> none  [dot(): lax.dot_general(left, right, (((left_dim,), (right_dim,)), ((), ())), pre...]
    unnamed x6 -> x12, local copies, waits for them, and re-layouts: 1.23 us -> 5.02 us
    all_to_all x2, waiting for transfers between devices: 3.14 us -> 0.75 us  [the longest x1 0.74 us: shards(): squares = lax.all_to_all(squares, COL, 0, 0, tiled=True)]
    all_to_all x1, blocking collectives: 18.6 us -> 16.7 us  [shards(): tiles, gram_half = spread(lax.all_to_all(tiles, 'x', 0, 0, tiled=True))]
  transfers between devices with their start and end apart: 6 -> 6, of which waited for: 3 -> 3; matrix products, arithmetic and copies ran while one was open for 11% -> 0% of each run, Pallas kernels for 25% -> 29%
where the time goes in v3:
time: 171 us
  blocking collectives  78.4 us (46%)
  Pallas kernels  66.4 us (39%)
  starting transfers between devices  15.2 us (9%)
  local copies, waits for them, and re-layouts  5.12 us (3%)
  waiting for transfers between devices  4.11 us (2%)
    pallas_call x1, Pallas kernels, inverted(): pl.pallas_call(inverse_factor, in_specs=[IN_SMEM, IN_VMEM, IN_VMEM, IN_VM...  46.4 us
    all_to_all x2, blocking collectives, scattered(): return lax.all_to_all(tiles, axis, 0, 0, tiled=True).sum(axis=0)  36.5 us
    all_to_all x2, blocking collectives, from_everyone(): return lax.all_to_all(tiles, axis, 0, 0, tiled=True)  25.2 us
    all_to_all x1, blocking collectives, shards(): tiles, gram_half = spread(lax.all_to_all(tiles, 'x', 0, 0, tiled=True))  16.7 us
    ppermute x4, starting transfers between devices, other_core(): return lax.ppermute(array, 'c', [(0, 1), (1, 0)])  7.9 us
    pallas_call x1, Pallas kernels, project(): pl.pallas_call(project_kernel, grid=(columns // TILE,), in_specs=[block,...  7.04 us
    unnamed x12, local copies, waits for them, and re-layouts  5.02 us
    pallas_call x1, Pallas kernels, updated(): pl.pallas_call(update_kernel, grid_spec=pltpu.PrefetchScalarGridSpec(num_...  4.06 us
  transfers between devices with their start and end apart: 6, of which 3 were waited for; matrix products, arithmetic and copies ran while one was open for 0% of the time, Pallas kernels for 29%

profile of v3, /device:TPU:1, one launch (start us, length us, event | category | flops | bytes accessed | tf_op | source)
XLA Modules:
  0.0 170.7 jit_solution(437739131972183092)
XLA Ops:
  0.6 7.0 %project.1 = (f32[1024,256]{1,0:T(8,128)}, bf16[1024,1024]{1,0:T(8,128)(2,1)}, bf16[1024,1024]{1,0:T(8,128)(2,1)}) custom-call(bf16[1024,1024]{1,0:T(8,128)(2,1)} %momentum.3, bf16[1024,1024]{1,0:T(8,128)(2,1)} %gradient.3, f32[1024,256]{1,0:T(8,128)} %basis.1), custom_call_target="tpu_custom_call" | custom-call | flops 1610612736 | tf_op jit(solution)/shard_map/project/pallas_call | solution.py:104
  7.7 18.5 %all_to_all.35 = f32[4,256,256]{2,1,0:T(8,128)S(1)} all-to-all(f32[4,256,256]{2,1,0:T(8,128)} %bitcast.11), channel_id=1, replica_groups=mesh['x'=4,'c'=2,'z'=8,'y'=4] {'y'}, dimensions={0} | all-to-all | bytes 2097152 | tf_op jit(solution)/shard_map/all_to_all | solution.py:24
  26.2 0.1 reduce_sum.18
  26.3 18.0 %all_to_all.36 = f32[8,32,256]{2,1,0:T(8,128)S(1)} all-to-all(f32[8,32,256]{2,1,0:T(8,128)S(1)} %bitcast.9), channel_id=1, replica_groups=mesh['x'=4,'c'=2,'z'=8,'y'=4] {'z'}, dimensions={0} | all-to-all | bytes 524288 | tf_op jit(solution)/shard_map/all_to_all | solution.py:24
  44.2 0.0 copy-start.2
  44.3 0.0 copy-start.3
  44.3 12.2 %all_to_all.37 = f32[8,32,256]{2,1,0:T(8,128)S(1)} all-to-all(f32[8,32,256]{2,1,0:T(8,128)S(1)} %broadcast_in_dim.17), channel_id=1, replica_groups=mesh['x'=4,'c'=2,'z'=8,'y'=4] {'z'}, dimensions={0} | all-to-all | bytes 524288 | tf_op jit(solution)/shard_map/all_to_all | solution.py:29
  56.5 0.1 broadcast_in_dim.19
  56.6 13.1 %all_to_all.38 = f32[4,256,256]{2,1,0:T(8,128)S(1)} all-to-all(f32[4,256,256]{2,1,0:T(8,128)S(1)} %broadcast_in_dim.19), channel_id=1, replica_groups=mesh['x'=4,'c'=2,'z'=8,'y'=4] {'y'}, dimensions={0} | all-to-all | bytes 2097152 | tf_op jit(solution)/shard_map/all_to_all | solution.py:29
  69.6 0.0 copy-done.2
  69.6 0.0 copy-done.3
  69.6 3.6 %widen.1 = (f32[768,256]{1,0:T(8,128)S(1)}, f32[512,256]{1,0:T(8,128)S(1)}) custom-call(s32[1]{0:T(128)} %bitcast.core, bf16[1024,1024]{1,0:T(8,128)(2,1)S(1)} %copy-done.2, bf16[1024,1024]{1,0:T(8,128)(2,1)S(1)} %copy-done.3, f32[1024,256]{1,0:T(8,128)S(1)} %bitcast.7), custom_call_target="tpu_custom_call" | custom-call | flops 2013265920 | tf_op jit(solution)/shard_map/widen/pallas_call | solution.py:138
  73.2 5.5 %collective-permute-start = (f32[768,256]{1,0:T(8,128)S(1)}, f32[768,256]{1,0:T(8,128)S(1)}, u32[]{:S(2)}, u32[]{:S(2)}) collective-permute-start(f32[768,256]{1,0:T(8,128)S(1)} %get-tuple-element.26.outgoing), channel_id=1, source_target_pairs={{0,32},{32,0},{1,33},{33,1},{2,34},{34,2},{3,35},{35,3},{4,36},{36... | collective-permute-start | bytes 2359304 | tf_op jit(solution)/shard_map/ppermute | solution.py:37
  78.7 1.9 %collective-permute-done.received = f32[768,256]{1,0:T(8,128)S(1)} collective-permute-done((f32[768,256]{1,0:T(8,128)S(1)}, f32[768,256]{1,0:T(8,128)S(1)}, u32[]{:S(2)}, u32[]{:S(2)}) %collective-permute-start) | collective-permute-done | bytes 786464 | tf_op jit(solution)/shard_map/ppermute | solution.py:37
  80.7 0.1 merge.1
  80.8 16.7 %all_to_all.39.arrived = f32[4,224,256]{2,1,0:T(8,128)S(1)} all-to-all(f32[4,224,256]{2,1,0:T(8,128)S(1)} %merge.1), channel_id=1, replica_groups=mesh['x'=4,'c'=2,'z'=8,'y'=4] {'x'}, dimensions={0} | all-to-all | bytes 1835008 | tf_op jit(solution)/shard_map/all_to_all | solution.py:429
  97.4 0.8 spread.1
  98.3 1.8 %collective-permute-start.1 = (f32[96,256]{1,0:T(8,128)S(1)}, f32[96,256]{1,0:T(8,128)S(1)}, u32[]{:S(2)}, u32[]{:S(2)}) collective-permute-start(f32[96,256]{1,0:T(8,128)S(1)} %get-tuple-element.28.own), channel_id=1, source_target_pairs={{0,32},{32,0},{1,33},{33,1},{2,34},{34,2},{3,35},{35,3},{4,36},{36... | collective-permute-start | bytes 294920 | tf_op jit(solution)/shard_map/ppermute | solution.py:37
  100.1 3.5 %all-to-all-start.5 = ((f32[4,128,256]{2,1,0:T(8,128)}), f32[4,128,256]{2,1,0:T(8,128)S(1)}, u32[]{:S(2)}, u32[]{:S(2)}) async-start(f32[4,128,256]{2,1,0:T(8,128)} %get-tuple-element.30), calls=%async_computation.5 | async-start | bytes 1048576 | tf_op jit(solution)/shard_map/all_to_all | solution.py:430
  103.6 0.0 collective-permute-done.1.other
  103.6 46.4 %inverse_factor.1 = (f32[256,256]{1,0:T(8,128)S(1)}, f32[1024,256]{1,0:T(8,128)S(1)}) custom-call(s32[1]{0:T(128)} %bitcast.core, f32[96,256]{1,0:T(8,128)S(1)} %get-tuple-element.28.own, f32[96,256]{1,0:T(8,128)S(1)} %collective-permute-done.1.other, f32[1024,256]{1,0:T(8,128)S(1)} %bitcast.8), custom_call_target="tpu_custom_call" | custom-call | flops 4294967296 | tf_op jit(solution)/shard_map/inverse_factor/pallas_call | solution.py:286
  149.9 0.0 all-to-all-done.5
  149.9 0.4 transposed.1
  150.4 0.1 collective-permute-start.2
  150.5 0.5 collective-permute-start.3
  151.0 1.4 collective-permute-done.3
  152.4 0.6 add.3
  153.1 3.9 %all-to-all-start.6 = ((f32[32,1,256]{2,1,0:T(1,128)}), f32[32,1,256]{2,1,0:T(1,128)S(1)}, u32[]{:S(2)}, u32[]{:S(2)}) async-start(f32[32,1,256]{2,1,0:T(1,128)} %add.3), calls=%async_computation.6 | async-start | bytes 65536 | tf_op jit(solution)/shard_map/all_to_all | solution.py:435
  156.9 0.0 collective-permute-done.2.other
  157.0 0.0 copy-start
  157.0 1.6 copy-done
  158.5 0.0 copy-start.1
  158.6 1.6 copy-done.1
  160.1 4.0 %new_momentum.1 = (bf16[1024,1024]{1,0:T(8,128)(2,1)}, bf16[1024,256]{1,0:T(8,128)(2,1)S(1)}, bf16[1024,256]{1,0:T(8,128)(2,1)S(1)}) custom-call(s32[1]{0:T(128)} %bitcast.core, bf16[1024,1024]{1,0:T(8,128)(2,1)S(1)} %copy-done, bf16[1024,1024]{1,0:T(8,128)(2,1)S(1)} %copy-done.1, f32[1024,256]{1,0:T(8,128)S(1)} %get-tuple-element.29.orthonormal, ...), custom_call_target="tpu_custom_call" | custom-call | flops 4294967296 | tf_op jit(solution)/shard_map/new_momentum/pallas_call | solution.py:350
  164.1 0.0 copy-start.4
  164.1 0.8 copy-done.4
  164.9 0.7 all-to-all-done.6.squares
  165.6 0.0 copy-start.5
  165.6 1.0 copy-done.5
  166.7 4.1 %update.1 = (f32[1024,1024]{1,0:T(8,128)}, f32[1024,256]{1,0:T(8,128)}) custom-call(s32[1]{0:T(128)} %bitcast.core, f32[1024,256]{1,0:T(8,128)S(1)} %get-tuple-element.29.orthonormal, f32[512,256]{1,0:T(8,128)S(1)} %get-tuple-element.32.own, f32[512,256]{1,0:T(8,128)S(1)} %collective-permute-done.2.other, bf16[1024,256]{1,0:T(8,128)(2,1)S(1)} %get-tuple-element.34.top, ...), custom_call_target="tpu_custom_call" | custom-call | flops 1610612736 | tf_op jit(solution)/shard_map/update/pallas_call | solution.py:390
  (2 shorter events, 0.0 us)
Async XLA Ops:
  44.2 25.4 %copy-start.2 = (bf16[1024,1024]{1,0:T(8,128)(2,1)S(1)}, bf16[1024,1024]{1,0:T(8,128)(2,1)}, u32[]{:S(2)}) copy-start(bf16[1024,1024]{1,0:T(8,128)(2,1)} %get-tuple-element.23.top) | copy-start | bytes 6291460
  44.3 25.4 %copy-start.3 = (bf16[1024,1024]{1,0:T(8,128)(2,1)S(1)}, bf16[1024,1024]{1,0:T(8,128)(2,1)}, u32[]{:S(2)}) copy-start(bf16[1024,1024]{1,0:T(8,128)(2,1)} %get-tuple-element.24.low) | copy-start | bytes 6291460
  73.2 7.4 %collective-permute-start = (f32[768,256]{1,0:T(8,128)S(1)}, f32[768,256]{1,0:T(8,128)S(1)}, u32[]{:S(2)}, u32[]{:S(2)}) collective-permute-start(f32[768,256]{1,0:T(8,128)S(1)} %get-tuple-element.26.outgoing), channel_id=1, source_target_pairs={{0,32},{32,0},{1,33},{33,1},{2,34},{34,2},{3,35},{35,3},{4,36},{36... | collective-permute-start | bytes 2359304 | tf_op jit(solution)/shard_map/ppermute | solution.py:37
  98.3 5.3 %collective-permute-start.1 = (f32[96,256]{1,0:T(8,128)S(1)}, f32[96,256]{1,0:T(8,128)S(1)}, u32[]{:S(2)}, u32[]{:S(2)}) collective-permute-start(f32[96,256]{1,0:T(8,128)S(1)} %get-tuple-element.28.own), channel_id=1, source_target_pairs={{0,32},{32,0},{1,33},{33,1},{2,34},{34,2},{3,35},{35,3},{4,36},{36... | collective-permute-start | bytes 294920 | tf_op jit(solution)/shard_map/ppermute | solution.py:37
  100.1 49.9 %all-to-all-start.5 = ((f32[4,128,256]{2,1,0:T(8,128)}), f32[4,128,256]{2,1,0:T(8,128)S(1)}, u32[]{:S(2)}, u32[]{:S(2)}) async-start(f32[4,128,256]{2,1,0:T(8,128)} %get-tuple-element.30), calls=%async_computation.5 | async-start | bytes 1048576 | tf_op jit(solution)/shard_map/all_to_all | solution.py:430
  150.4 6.6 %collective-permute-start.2 = (f32[512,256]{1,0:T(8,128)S(1)}, f32[512,256]{1,0:T(8,128)S(1)}, u32[]{:S(2)}, u32[]{:S(2)}) collective-permute-start(f32[512,256]{1,0:T(8,128)S(1)} %get-tuple-element.32.own), channel_id=1, source_target_pairs={{0,32},{32,0},{1,33},{33,1},{2,34},{34,2},{3,35},{35,3},{4,36},{36... | collective-permute-start | bytes 1572872 | tf_op jit(solution)/shard_map/ppermute | solution.py:37
  150.5 1.9 %collective-permute-start.3 = (f32[32,1,256]{2,1,0:T(1,128)S(1)}, f32[32,1,256]{2,1,0:T(1,128)S(1)}, u32[]{:S(2)}, u32[]{:S(2)}) collective-permute-start(f32[32,1,256]{2,1,0:T(1,128)S(1)} %get-tuple-element.36), channel_id=1, source_target_pairs={{0,32},{32,0},{1,33},{33,1},{2,34},{34,2},{3,35},{35,3},{4,36},{36... | collective-permute-start | bytes 98312 | tf_op jit(solution)/shard_map/ppermute | solution.py:37
  153.1 12.6 %all-to-all-start.6 = ((f32[32,1,256]{2,1,0:T(1,128)}), f32[32,1,256]{2,1,0:T(1,128)S(1)}, u32[]{:S(2)}, u32[]{:S(2)}) async-start(f32[32,1,256]{2,1,0:T(1,128)} %add.3), calls=%async_computation.6 | async-start | bytes 65536 | tf_op jit(solution)/shard_map/all_to_all | solution.py:435
  157.0 1.6 copy-start
  158.5 1.6 copy-start.1
  164.1 0.8 copy-start.4
  165.6 1.0 copy-start.5

commit v4 on v3

--- a/solution.py
+++ b/solution.py
@@ -1,3 +1,4 @@
+import functools
 import math
 
 import jax
@@ -78,76 +79,102 @@
     return mxu(a, c, dims) + (mxu(a, d, dims) + mxu(b, c, dims))
 
 
+def in_hbm(*arrays):
+    return [pltpu.with_memory_space_constraint(a, pltpu.HBM) for a in arrays]
+
+
 def limit(mib):
     return pltpu.CompilerParams(vmem_limit_bytes=mib << 20)
 
 
-def project_kernel(momentum, gradient, basis, out, top, low):
-    a, b = parts(wider(momentum[...]) + wider(gradient[...]))
-    top[...], low[...] = a, b
-    right = parts(basis[...])
-    rows = out.shape[0]
-
-    @pl.when(pl.program_id(0) == 0)
-    def _():
-        out[...] = split_dot((a, b), right, PLAIN)
-
-    @pl.when(pl.program_id(0) > 0)
-    def _():
-        out[...] += split_dot((a, b), right, PLAIN)
+def both(left, right, dims):
+    (a, b), (c, d) = left, right
+    return (mxu(a, c, dims) + mxu(b, c, dims)) + (mxu(a, d, dims) + mxu(b, d, dims))
+
+
+def project_kernel(momentum, gradient, basis, out, m, g, r, top, low, arrived):
+    chunks = momentum.shape[0] // TILE
+    first = pltpu.make_async_copy(basis, r, arrived.at[0])
+    first.start()
+    copies = []
+    for t in range(chunks):
+        span = pl.ds(t * TILE, TILE)
+        pair = (
+            pltpu.make_async_copy(momentum.at[span, :], m.at[span, :], arrived.at[2 * t + 1]),
+            pltpu.make_async_copy(gradient.at[span, :], g.at[span, :], arrived.at[2 * t + 2]),
+        )
+        for copy in pair:
+            copy.start()
+        copies.append(pair)
+    first.wait()
+    top[...], low[...] = parts(r[...])
+    for t in range(chunks):
+        for copy in copies[t]:
+            copy.wait()
+        span = slice(t * TILE, (t + 1) * TILE)
+        out[span, :] = both((m[span, :], g[span, :]), (top[...], low[...]), PLAIN)
 
 
 def project(momentum, gradient, basis):
     rows, columns = momentum.shape
-    block = pl.BlockSpec((rows, TILE), lambda t: (0, t))
-    split = jax.ShapeDtypeStruct((rows, columns), jnp.bfloat16)
     return pl.pallas_call(
         project_kernel,
-        grid=(columns // TILE,),
-        in_specs=[block, block, pl.BlockSpec((TILE, RANK), lambda t: (t, 0))],
-        out_specs=[pl.BlockSpec((rows, RANK), lambda t: (0, 0)), block, block],
-        out_shape=[jax.ShapeDtypeStruct((rows, RANK), jnp.float32), split, split],
-        cost_estimate=cost(6 * rows * columns * RANK),
-        compiler_params=limit(61),
+        in_specs=[pl.BlockSpec(memory_space=pltpu.HBM)] * 3,
+        out_specs=IN_VMEM,
+        out_shape=jax.ShapeDtypeStruct((rows, RANK), jnp.float32),
+        scratch_shapes=[
+            pltpu.VMEM((rows, columns), jnp.bfloat16),
+            pltpu.VMEM((rows, columns), jnp.bfloat16),
+            pltpu.VMEM((columns, RANK), jnp.float32),
+            pltpu.VMEM((columns, RANK), jnp.bfloat16),
+            pltpu.VMEM((columns, RANK), jnp.bfloat16),
+            pltpu.SemaphoreType.DMA((2 * rows // TILE + 1,)),
+        ],
+        cost_estimate=cost(8 * rows * columns * RANK),
+        compiler_params=limit(16),
         name="project",
-    )(momentum, gradient, basis)
-
-
-def widen_kernel(core, top, low, projected, outgoing, kept, flat_top, flat_low):
-    half = kept.shape[0]
-    across = parts(projected[...].T)
-    flat_top[...], flat_low[...] = across
-
-    for place, target in ((1 - core[0], outgoing), (core[0], kept)):
-
-        @pl.loop(0, half // TILE)
-        def _(t):
-            span = pl.ds(pl.multiple_of(place * half + t * TILE, TILE), TILE)
-            tile = split_dot(
-                (flat_top[...], flat_low[...]), (top[:, span], low[:, span]), PLAIN
-            )
-            target[pl.ds(pl.multiple_of(t * TILE, TILE), TILE), :] = tile.T
-
-    outgoing[half:, :] = split_dot(
-        (flat_top[...], flat_low[...]), parts(projected[...]), PLAIN
-    )
-
-
-def widen(core, top, low, projected):
-    rows, columns = top.shape
-    return pl.pallas_call(
-        widen_kernel,
+    )(*in_hbm(momentum, gradient, basis))
+
+
+def widen_kernel(with_gram, core, momentum, gradient, projected, out, top, low):
+    half = momentum.shape[1] // 2
+    top[...], low[...] = parts(projected[...].T)
+    place = 1 - core[0] if with_gram else core[0]
+
+    @pl.loop(0, half // TILE)
+    def _(t):
+        span = pl.ds(pl.multiple_of(place * half + t * TILE, TILE), TILE)
+        pair = (momentum[:, span], gradient[:, span])
+        tile = both((top[...], low[...]), pair, PLAIN)
+        out[pl.ds(pl.multiple_of(t * TILE, TILE), TILE), :] = tile.T
+
+    if with_gram:
+        out[half:, :] = split_dot((top[...], low[...]), parts(projected[...]), PLAIN)
+
+
+def widen(with_gram, core, momentum, gradient, projected):
+    rows, columns = momentum.shape
+    return pl.pallas_call(
+        functools.partial(widen_kernel, with_gram),
         in_specs=[IN_SMEM, IN_VMEM, IN_VMEM, IN_VMEM],
-        out_specs=[IN_VMEM, IN_VMEM],
-        out_shape=[
-            jax.ShapeDtypeStruct((columns // 2 + RANK, RANK), jnp.float32),
-            jax.ShapeDtypeStruct((columns // 2, RANK), jnp.float32),
-        ],
+        out_specs=IN_VMEM,
+        out_shape=jax.ShapeDtypeStruct(
+            (columns // 2 + (RANK if with_gram else 0), RANK), jnp.float32
+        ),
         scratch_shapes=[pltpu.VMEM((RANK, rows), jnp.bfloat16)] * 2,
-        cost_estimate=cost(6 * rows * (columns + RANK) * RANK),
-        compiler_params=limit(20),
-        name="widen",
-    )(core, top, low, projected)
+        cost_estimate=cost(4 * rows * columns * RANK),
+        compiler_params=limit(16),
+        name="widen_given" if with_gram else "widen_kept",
+    )(core, momentum, gradient, projected)
+
+
+def split_dot(left, right, dims):
+    (a, b), (c, d) = left, right
+    return mxu(a, c, dims) + (mxu(a, d, dims) + mxu(b, c, dims))
+
+
+def limit(mib):
+    return pltpu.CompilerParams(vmem_limit_bytes=mib << 20)
 
 
 def folded(block):
@@ -214,7 +241,7 @@
         in_specs=[IN_VMEM],
         out_specs=[IN_VMEM, IN_VMEM],
         out_shape=[
-            jax.ShapeDtypeStruct((sides, lines - PACKED, RANK), jnp.float32),
+            pltpu.HBM((sides, lines - PACKED, RANK), jnp.float32),
             jax.ShapeDtypeStruct((PACKED, RANK), jnp.float32),
         ],
         cost_estimate=cost(arrived.size),
@@ -346,7 +373,6 @@
     rows, half = orthonormal.shape[0], own.shape[0]
     block = pl.BlockSpec((SPAN, half), lambda h, t, core: (t, side_of(h, core)))
     whole = pl.BlockSpec((half, RANK), lambda h, t, core: (0, 0))
-    split = pl.BlockSpec((half, RANK), lambda h, t, core: (h, 0))
     return pl.pallas_call(
         momentum_kernel,
         grid_spec=pltpu.PrefetchScalarGridSpec(
@@ -359,34 +385,32 @@
                 whole,
                 whole,
             ],
-            out_specs=[block, split, split],
+            out_specs=block,
+            scratch_shapes=[pltpu.VMEM((half, RANK), jnp.bfloat16)] * 2,
         ),
-        out_shape=[
-            jax.ShapeDtypeStruct((rows, 2 * half), jnp.bfloat16),
-            jax.ShapeDtypeStruct((2 * half, RANK), jnp.bfloat16),
-            jax.ShapeDtypeStruct((2 * half, RANK), jnp.bfloat16),
-        ],
+        out_shape=jax.ShapeDtypeStruct((rows, 2 * half), jnp.bfloat16),
         cost_estimate=cost(1 << 32),
         compiler_params=pltpu.CompilerParams(vmem_limit_bytes=20 << 20),
         name="new_momentum",
-    )(core, momentum, gradient, orthonormal, own, other)
-
-
-def update_kernel(core, orthonormal, own, other, top, low, squares, update, basis):
+    )(core, *in_hbm(momentum, gradient), orthonormal, own, other)
+
+
+def update_kernel(core, orthonormal, own, other, squares, update, basis, top, low):
     norms = jnp.sqrt(jnp.sum(squares[...], axis=0)) + eps
 
     @pl.when(pl.program_id(1) == 0)
     def _():
-        basis[...] = jnp.where(pl.program_id(0) == 0, own[...], other[...]) / norms
+        side = jnp.where(pl.program_id(0) == 0, own[...], other[...])
+        top[...], low[...] = parts(side)
+        basis[...] = side / norms
 
     left = parts(orthonormal[...] * (math.sqrt(ROWS * COLS / RANK) / norms))
     update[...] = split_dot(left, (top[...], low[...]), FLIPPED)
 
 
-def updated(core, orthonormal, own, other, top, low, squares):
+def updated(core, orthonormal, own, other, squares):
     rows, half = orthonormal.shape[0], own.shape[0]
     whole = pl.BlockSpec((half, RANK), lambda h, t, core: (0, 0))
-    split = pl.BlockSpec((half, RANK), lambda h, t, core: (h, 0))
     return pl.pallas_call(
         update_kernel,
         grid_spec=pltpu.PrefetchScalarGridSpec(
@@ -396,14 +420,13 @@
                 pl.BlockSpec((SPAN, RANK), lambda h, t, core: (t, 0)),
                 whole,
                 whole,
-                split,
-                split,
                 pl.BlockSpec(squares.shape, lambda h, t, core: (0, 0, 0)),
             ],
             out_specs=[
                 pl.BlockSpec((SPAN, half), lambda h, t, core: (t, side_of(h, core))),
                 pl.BlockSpec((half, RANK), lambda h, t, core: (side_of(h, core), 0)),
             ],
+            scratch_shapes=[pltpu.VMEM((half, RANK), jnp.bfloat16)] * 2,
         ),
         out_shape=[
             jax.ShapeDtypeStruct((rows, 2 * half), jnp.float32),
@@ -412,20 +435,22 @@
         cost_estimate=cost(6 * rows * 2 * half * RANK),
         compiler_params=limit(20),
         name="update",
-    )(core, orthonormal, own, other, top, low, squares)
+    )(core, orthonormal, own, other, squares)
 
 
 def shards(momentum, gradient, right_basis):
     core = core_number()
     sides = lax.axis_size("x")
 
-    part, top, low = project(momentum, gradient, right_basis)
+    part = project(momentum, gradient, right_basis)
     part, core = lax.optimization_barrier((part, core))
     own = scattered(scattered(part, "y"), "z")
     projected = gathered(gathered(own, "z"), "y")
 
-    outgoing, kept = widen(core, top, low, projected)
-    tiles = merge(core, outgoing, other_core(outgoing), kept, sides)
+    outgoing = widen(True, core, momentum, gradient, projected)
+    received = other_core(outgoing)
+    kept = widen(False, core, momentum, gradient, projected)
+    tiles = merge(core, outgoing, received, kept, sides)
     tiles, gram_half = spread(lax.all_to_all(tiles, "x", 0, 0, tiled=True))
     wide_half = lax.all_to_all(tiles, "x", 0, 0, tiled=True).reshape(-1, RANK)
 
@@ -434,8 +459,8 @@
     squares = own_squares + other_core(own_squares)
     squares = lax.all_to_all(squares, COL, 0, 0, tiled=True)
     other = other_core(own)
-    new_momentum, top, low = remembered(core, momentum, gradient, orthonormal, own, other)
-    update, new_basis = updated(core, orthonormal, own, other, top, low, squares)
+    new_momentum = remembered(core, momentum, gradient, orthonormal, own, other)
+    update, new_basis = updated(core, orthonormal, own, other, squares)
     return (new_momentum, new_basis, update)
 
 

time: 171 us -> 169 us (0.988)
  local copies, waits for them, and re-layouts: 5.12 us -> 0.11 us
  Pallas kernels: 66.4 us -> 68.4 us
    unnamed x12 -> x4, local copies, waits for them, and re-layouts: 5.02 us -> 0.01 us
    all_to_all x1, waiting for transfers between devices: 0.74 us -> 3.17 us  [shards(): squares = lax.all_to_all(squares, COL, 0, 0, tiled=True)]
    ppermute x4, waiting for transfers between devices: 3.36 us -> 1.45 us  [other_core(): return lax.ppermute(array, 'c', [(0, 1), (1, 0)])]
    pallas_call x2 -> x3, Pallas kernels: 10.7 us -> 11 us  [the longest x1 6.51 us: project(): pl.pallas_call(project_kernel, in_specs=[pl.BlockSpec(memory_space=pltpu....]
  transfers between devices with their start and end apart: 6 -> 6, of which waited for: 3 -> 2; matrix products, arithmetic and copies ran while one was open for 0% -> 0% of each run, Pallas kernels for 29% -> 32%
where the time goes in v4:
time: 169 us; the launch traced here: 168 us
  blocking collectives  78.5 us (46%)
  Pallas kernels  68.4 us (40%)
  starting transfers between devices  14.9 us (9%)
  waiting for transfers between devices  4.63 us (3%)
    pallas_call x1, Pallas kernels, inverted(): pl.pallas_call(inverse_factor, in_specs=[IN_SMEM, IN_VMEM, IN_VMEM, IN_VM...  46.3 us
    all_to_all x2, blocking collectives, scattered(): return lax.all_to_all(tiles, axis, 0, 0, tiled=True).sum(axis=0)  36.3 us
    all_to_all x2, blocking collectives, from_everyone(): return lax.all_to_all(tiles, axis, 0, 0, tiled=True)  25.2 us
    all_to_all x1, blocking collectives, shards(): tiles, gram_half = spread(lax.all_to_all(tiles, 'x', 0, 0, tiled=True))  17 us
    ppermute x4, starting transfers between devices, other_core(): return lax.ppermute(array, 'c', [(0, 1), (1, 0)])  7.53 us
    pallas_call x1, Pallas kernels, project(): pl.pallas_call(project_kernel, in_specs=[pl.BlockSpec(memory_space=pltpu....  6.51 us
    pallas_call x1, Pallas kernels, remembered(): pl.pallas_call(momentum_kernel, grid_spec=pltpu.PrefetchScalarGridSpec(nu...  5.51 us
    pallas_call x2, Pallas kernels, widen(): pl.pallas_call(functools.partial(widen_kernel, with_gram), in_specs=[IN_S...  4.49 us
  transfers between devices with their start and end apart: 6, of which 2 were waited for; matrix products, arithmetic and copies ran while one was open for 0% of the time, Pallas kernels for 32%

profile of v4, /device:TPU:1, one launch (start us, length us, event | category | flops | bytes accessed | tf_op | source)
XLA Modules:
  0.0 168.1 jit_solution(1801568986212129048)
XLA Ops:
  0.6 6.5 %project.1 = f32[1024,256]{1,0:T(8,128)S(1)} custom-call(bf16[1024,1024]{1,0:T(8,128)(2,1)} %momentum.7, bf16[1024,1024]{1,0:T(8,128)(2,1)} %gradient.7, f32[1024,256]{1,0:T(8,128)} %basis.1), custom_call_target="tpu_custom_call" | custom-call | flops 2147483648 | tf_op jit(solution)/shard_map/project/pallas_call | solution.py:120
  7.2 19.0 %all_to_all.35 = f32[4,256,256]{2,1,0:T(8,128)S(1)} all-to-all(f32[4,256,256]{2,1,0:T(8,128)S(1)} %bitcast.10), channel_id=1, replica_groups=mesh['x'=4,'c'=2,'z'=8,'y'=4] {'y'}, dimensions={0} | all-to-all | bytes 2097152 | tf_op jit(solution)/shard_map/all_to_all | solution.py:25
  26.2 0.1 reduce_sum.18
  26.3 17.2 %all_to_all.36 = f32[8,32,256]{2,1,0:T(8,128)S(1)} all-to-all(f32[8,32,256]{2,1,0:T(8,128)S(1)} %bitcast.11), channel_id=1, replica_groups=mesh['x'=4,'c'=2,'z'=8,'y'=4] {'z'}, dimensions={0} | all-to-all | bytes 524288 | tf_op jit(solution)/shard_map/all_to_all | solution.py:25
  43.5 0.0 copy-start
  43.5 0.0 copy-start.1
  43.6 12.2 %all_to_all.37 = f32[8,32,256]{2,1,0:T(8,128)S(1)} all-to-all(f32[8,32,256]{2,1,0:T(8,128)S(1)} %broadcast_in_dim.17), channel_id=1, replica_groups=mesh['x'=4,'c'=2,'z'=8,'y'=4] {'z'}, dimensions={0} | all-to-all | bytes 524288 | tf_op jit(solution)/shard_map/all_to_all | solution.py:30
  55.7 0.1 broadcast_in_dim.19
  55.8 13.1 %all_to_all.38 = f32[4,256,256]{2,1,0:T(8,128)S(1)} all-to-all(f32[4,256,256]{2,1,0:T(8,128)S(1)} %broadcast_in_dim.19), channel_id=1, replica_groups=mesh['x'=4,'c'=2,'z'=8,'y'=4] {'y'}, dimensions={0} | all-to-all | bytes 2097152 | tf_op jit(solution)/shard_map/all_to_all | solution.py:30
  68.9 0.0 copy-done
  68.9 0.0 copy-done.1
  68.9 2.5 %widen_given.1.outgoing = f32[768,256]{1,0:T(8,128)S(1)} custom-call(s32[1]{0:T(128)} %bitcast.core, bf16[1024,1024]{1,0:T(8,128)(2,1)S(1)} %copy-done, bf16[1024,1024]{1,0:T(8,128)(2,1)S(1)} %copy-done.1, f32[1024,256]{1,0:T(8,128)S(1)} %bitcast.6), custom_call_target="tpu_custom_call" | custom-call | flops 1073741824 | tf_op jit(solution)/shard_map/widen_given/pallas_call | solution.py:157
  71.4 5.5 %collective-permute-start = (f32[768,256]{1,0:T(8,128)S(1)}, f32[768,256]{1,0:T(8,128)S(1)}, u32[]{:S(2)}, u32[]{:S(2)}) collective-permute-start(f32[768,256]{1,0:T(8,128)S(1)} %widen_given.1.outgoing), channel_id=1, source_target_pairs={{0,32},{32,0},{1,33},{33,1},{2,34},{34,2},{3,35},{35,3},{4,36},{36... | collective-permute-start | bytes 2359304 | tf_op jit(solution)/shard_map/ppermute | solution.py:38
  76.9 2.0 %widen_kept.1.kept = f32[512,256]{1,0:T(8,128)S(1)} custom-call(s32[1]{0:T(128)} %bitcast.core, bf16[1024,1024]{1,0:T(8,128)(2,1)S(1)} %copy-done, bf16[1024,1024]{1,0:T(8,128)(2,1)S(1)} %copy-done.1, f32[1024,256]{1,0:T(8,128)S(1)} %bitcast.7), custom_call_target="tpu_custom_call" | custom-call | flops 1073741824 | tf_op jit(solution)/shard_map/widen_kept/pallas_call | solution.py:157
  78.9 0.0 collective-permute-done.received
  78.9 0.1 merge.1
  79.0 17.0 %all_to_all.39.arrived = f32[4,224,256]{2,1,0:T(8,128)S(1)} all-to-all(f32[4,224,256]{2,1,0:T(8,128)S(1)} %merge.1), channel_id=1, replica_groups=mesh['x'=4,'c'=2,'z'=8,'y'=4] {'x'}, dimensions={0} | all-to-all | bytes 1835008 | tf_op jit(solution)/shard_map/all_to_all | solution.py:454
  96.1 0.8 spread.1
  96.9 1.4 collective-permute-start.1
  98.3 3.5 %all-to-all-start.5 = ((f32[4,128,256]{2,1,0:T(8,128)}), f32[4,128,256]{2,1,0:T(8,128)S(1)}, u32[]{:S(2)}, u32[]{:S(2)}) async-start(f32[4,128,256]{2,1,0:T(8,128)} %get-tuple-element.17), calls=%async_computation.5 | async-start | bytes 1048576 | tf_op jit(solution)/shard_map/all_to_all | solution.py:455
  101.8 0.0 collective-permute-done.1.other
  101.8 46.3 %inverse_factor.1 = (f32[256,256]{1,0:T(8,128)S(1)}, f32[1024,256]{1,0:T(8,128)S(1)}) custom-call(s32[1]{0:T(128)} %bitcast.core, f32[96,256]{1,0:T(8,128)S(1)} %get-tuple-element.15.own, f32[96,256]{1,0:T(8,128)S(1)} %collective-permute-done.1.other, f32[1024,256]{1,0:T(8,128)S(1)} %bitcast.8), custom_call_target="tpu_custom_call" | custom-call | flops 4294967296 | tf_op jit(solution)/shard_map/inverse_factor/pallas_call | solution.py:313
  148.2 0.0 all-to-all-done.5
  148.2 0.4 transposed.1
  148.6 0.1 collective-permute-start.2
  148.7 0.5 collective-permute-start.3
  149.2 1.4 collective-permute-done.3
  150.7 0.6 add.3
  151.3 3.9 %all-to-all-start.6 = ((f32[32,1,256]{2,1,0:T(1,128)}), f32[32,1,256]{2,1,0:T(1,128)S(1)}, u32[]{:S(2)}, u32[]{:S(2)}) async-start(f32[32,1,256]{2,1,0:T(1,128)} %add.3), calls=%async_computation.6 | async-start | bytes 65536 | tf_op jit(solution)/shard_map/all_to_all | solution.py:460
  155.2 0.0 collective-permute-done.2.other
  155.2 5.5 %new_momentum.1 = bf16[1024,1024]{1,0:T(8,128)(2,1)} custom-call(s32[1]{0:T(128)} %bitcast.core, bf16[1024,1024]{1,0:T(8,128)(2,1)} %momentum.7, bf16[1024,1024]{1,0:T(8,128)(2,1)} %gradient.7, f32[1024,256]{1,0:T(8,128)S(1)} %get-tuple-element.16.orthonormal, f32[512,256]{1,0:T(8,128)S(1)} %get-tuple-element.19.own, f32[512,256]{1,0:T(8,128)S(1)} %collective-permute-done.2.other), custom_call_target="tpu_custom_call" | custom-call | flops 4294967296 | tf_op jit(solution)/shard_map/new_momentum/pallas_call | solution.py:376
  160.7 3.2 %all-to-all-done.6.squares = f32[32,1,256]{2,1,0:T(1,128)S(1)} async-done(((f32[32,1,256]{2,1,0:T(1,128)}), f32[32,1,256]{2,1,0:T(1,128)S(1)}, u32[]{:S(2)}, u32[]{:S(2)}) %all-to-all-start.6) | async-done | bytes 32800 | tf_op jit(solution)/shard_map/all_to_all | solution.py:460
  163.9 4.2 %update.1 = (f32[1024,1024]{1,0:T(8,128)}, f32[1024,256]{1,0:T(8,128)}) custom-call(s32[1]{0:T(128)} %bitcast.core, f32[1024,256]{1,0:T(8,128)S(1)} %get-tuple-element.16.orthonormal, f32[512,256]{1,0:T(8,128)S(1)} %get-tuple-element.19.own, f32[512,256]{1,0:T(8,128)S(1)} %collective-permute-done.2.other, f32[32,1,256]{2,1,0:T(1,128)S(1)} %all-to-all-done.6.squares), custom_call_target="tpu_custom_call" | custom-call | flops 1610612736 | tf_op jit(solution)/shard_map/update/pallas_call | solution.py:414
  (2 shorter events, 0.0 us)
Async XLA Ops:
  43.5 25.4 %copy-start = (bf16[1024,1024]{1,0:T(8,128)(2,1)S(1)}, bf16[1024,1024]{1,0:T(8,128)(2,1)}, u32[]{:S(2)}) copy-start(bf16[1024,1024]{1,0:T(8,128)(2,1)} %momentum.7) | copy-start | bytes 6291460
  43.5 25.4 %copy-start.1 = (bf16[1024,1024]{1,0:T(8,128)(2,1)S(1)}, bf16[1024,1024]{1,0:T(8,128)(2,1)}, u32[]{:S(2)}) copy-start(bf16[1024,1024]{1,0:T(8,128)(2,1)} %gradient.7) | copy-start | bytes 6291460
  71.4 7.5 %collective-permute-start = (f32[768,256]{1,0:T(8,128)S(1)}, f32[768,256]{1,0:T(8,128)S(1)}, u32[]{:S(2)}, u32[]{:S(2)}) collective-permute-start(f32[768,256]{1,0:T(8,128)S(1)} %widen_given.1.outgoing), channel_id=1, source_target_pairs={{0,32},{32,0},{1,33},{33,1},{2,34},{34,2},{3,35},{35,3},{4,36},{36... | collective-permute-start | bytes 2359304 | tf_op jit(solution)/shard_map/ppermute | solution.py:38
  96.9 4.9 %collective-permute-start.1 = (f32[96,256]{1,0:T(8,128)S(1)}, f32[96,256]{1,0:T(8,128)S(1)}, u32[]{:S(2)}, u32[]{:S(2)}) collective-permute-start(f32[96,256]{1,0:T(8,128)S(1)} %get-tuple-element.15.own), channel_id=1, source_target_pairs={{0,32},{32,0},{1,33},{33,1},{2,34},{34,2},{3,35},{35,3},{4,36},{36... | collective-permute-start | bytes 294920 | tf_op jit(solution)/shard_map/ppermute | solution.py:38
  98.3 49.9 %all-to-all-start.5 = ((f32[4,128,256]{2,1,0:T(8,128)}), f32[4,128,256]{2,1,0:T(8,128)S(1)}, u32[]{:S(2)}, u32[]{:S(2)}) async-start(f32[4,128,256]{2,1,0:T(8,128)} %get-tuple-element.17), calls=%async_computation.5 | async-start | bytes 1048576 | tf_op jit(solution)/shard_map/all_to_all | solution.py:455
  148.6 6.6 %collective-permute-start.2 = (f32[512,256]{1,0:T(8,128)S(1)}, f32[512,256]{1,0:T(8,128)S(1)}, u32[]{:S(2)}, u32[]{:S(2)}) collective-permute-start(f32[512,256]{1,0:T(8,128)S(1)} %get-tuple-element.19.own), channel_id=1, source_target_pairs={{0,32},{32,0},{1,33},{33,1},{2,34},{34,2},{3,35},{35,3},{4,36},{36... | collective-permute-start | bytes 1572872 | tf_op jit(solution)/shard_map/ppermute | solution.py:38
  148.7 1.9 %collective-permute-start.3 = (f32[32,1,256]{2,1,0:T(1,128)S(1)}, f32[32,1,256]{2,1,0:T(1,128)S(1)}, u32[]{:S(2)}, u32[]{:S(2)}) collective-permute-start(f32[32,1,256]{2,1,0:T(1,128)S(1)} %get-tuple-element.20), channel_id=1, source_target_pairs={{0,32},{32,0},{1,33},{33,1},{2,34},{34,2},{3,35},{35,3},{4,36},{36... | collective-permute-start | bytes 98312 | tf_op jit(solution)/shard_map/ppermute | solution.py:38
  151.3 12.6 %all-to-all-start.6 = ((f32[32,1,256]{2,1,0:T(1,128)}), f32[32,1,256]{2,1,0:T(1,128)S(1)}, u32[]{:S(2)}, u32[]{:S(2)}) async-start(f32[32,1,256]{2,1,0:T(1,128)} %add.3), calls=%async_computation.6 | async-start | bytes 65536 | tf_op jit(solution)/shard_map/all_to_all | solution.py:460

commit v5 on v4

--- a/solution.py
+++ b/solution.py
@@ -87,32 +87,26 @@
     return pltpu.CompilerParams(vmem_limit_bytes=mib << 20)
 
 
-def both(left, right, dims):
-    (a, b), (c, d) = left, right
-    return (mxu(a, c, dims) + mxu(b, c, dims)) + (mxu(a, d, dims) + mxu(b, d, dims))
-
-
-def project_kernel(momentum, gradient, basis, out, m, g, r, top, low, arrived):
-    chunks = momentum.shape[0] // TILE
-    first = pltpu.make_async_copy(basis, r, arrived.at[0])
-    first.start()
-    copies = []
-    for t in range(chunks):
-        span = pl.ds(t * TILE, TILE)
-        pair = (
-            pltpu.make_async_copy(momentum.at[span, :], m.at[span, :], arrived.at[2 * t + 1]),
-            pltpu.make_async_copy(gradient.at[span, :], g.at[span, :], arrived.at[2 * t + 2]),
-        )
-        for copy in pair:
-            copy.start()
-        copies.append(pair)
-    first.wait()
-    top[...], low[...] = parts(r[...])
-    for t in range(chunks):
-        for copy in copies[t]:
-            copy.wait()
-        span = slice(t * TILE, (t + 1) * TILE)
-        out[span, :] = both((m[span, :], g[span, :]), (top[...], low[...]), PLAIN)
+def added(product):
+    return product[:, :RANK] + product[:, RANK:]
+
+
+def project_kernel(momentum, gradient, basis, out, m, g, r, right, arrived):
+    loads = [
+        pltpu.make_async_copy(source, target, arrived.at[k])
+        for k, (source, target) in enumerate(((basis, r), (momentum, m), (gradient, g)))
+    ]
+    for load in loads:
+        load.start()
+    loads[0].wait()
+    right[:, :RANK], right[:, RANK:] = parts(r[...])
+    spans = [slice(t, t + SPAN) for t in range(0, out.shape[0], SPAN)]
+    loads[1].wait()
+    for span in spans:
+        out[span, :] = added(mxu(m[span, :], right[...], PLAIN))
+    loads[2].wait()
+    for span in spans:
+        out[span, :] += added(mxu(g[span, :], right[...], PLAIN))
 
 
 def project(momentum, gradient, basis):
@@ -126,9 +120,8 @@
             pltpu.VMEM((rows, columns), jnp.bfloat16),
             pltpu.VMEM((rows, columns), jnp.bfloat16),
             pltpu.VMEM((columns, RANK), jnp.float32),
-            pltpu.VMEM((columns, RANK), jnp.bfloat16),
-            pltpu.VMEM((columns, RANK), jnp.bfloat16),
-            pltpu.SemaphoreType.DMA((2 * rows // TILE + 1,)),
+            pltpu.VMEM((columns, 2 * RANK), jnp.bfloat16),
+            pltpu.SemaphoreType.DMA((3,)),
         ],
         cost_estimate=cost(8 * rows * columns * RANK),
         compiler_params=limit(16),
@@ -136,20 +129,18 @@
     )(*in_hbm(momentum, gradient, basis))
 
 
-def widen_kernel(with_gram, core, momentum, gradient, projected, out, top, low):
+def widen_kernel(with_gram, core, momentum, gradient, projected, out, left):
     half = momentum.shape[1] // 2
-    top[...], low[...] = parts(projected[...].T)
+    left[:RANK, :], left[RANK:, :] = parts(projected[...].T)
     place = 1 - core[0] if with_gram else core[0]
-
-    @pl.loop(0, half // TILE)
-    def _(t):
-        span = pl.ds(pl.multiple_of(place * half + t * TILE, TILE), TILE)
-        pair = (momentum[:, span], gradient[:, span])
-        tile = both((top[...], low[...]), pair, PLAIN)
-        out[pl.ds(pl.multiple_of(t * TILE, TILE), TILE), :] = tile.T
+    span = pl.ds(pl.multiple_of(place * half, half), half)
+    product = mxu(left[...], momentum[:, span], PLAIN) + mxu(left[...], gradient[:, span], PLAIN)
+    out[:half, :] = (product[:RANK] + product[RANK:]).T
 
     if with_gram:
-        out[half:, :] = split_dot((top[...], low[...]), parts(projected[...]), PLAIN)
+        top, low = parts(projected[...])
+        product = mxu(left[...], top, PLAIN)
+        out[half:, :] = product[:RANK] + (product[RANK:] + mxu(left[:RANK, :], low, PLAIN))
 
 
 def widen(with_gram, core, momentum, gradient, projected):
@@ -161,7 +152,7 @@
         out_shape=jax.ShapeDtypeStruct(
             (columns // 2 + (RANK if with_gram else 0), RANK), jnp.float32
         ),
-        scratch_shapes=[pltpu.VMEM((RANK, rows), jnp.bfloat16)] * 2,
+        scratch_shapes=[pltpu.VMEM((2 * RANK, rows), jnp.bfloat16)],
         cost_estimate=cost(4 * rows * columns * RANK),
         compiler_params=limit(16),
         name="widen_given" if with_gram else "widen_kept",
@@ -415,15 +406,15 @@
         update_kernel,
         grid_spec=pltpu.PrefetchScalarGridSpec(
             num_scalar_prefetch=1,
-            grid=(2, rows // SPAN),
+            grid=(2, 1),
             in_specs=[
-                pl.BlockSpec((SPAN, RANK), lambda h, t, core: (t, 0)),
+                pl.BlockSpec((rows, RANK), lambda h, t, core: (t, 0)),
                 whole,
                 whole,
                 pl.BlockSpec(squares.shape, lambda h, t, core: (0, 0, 0)),
             ],
             out_specs=[
-                pl.BlockSpec((SPAN, half), lambda h, t, core: (t, side_of(h, core))),
+                pl.BlockSpec((rows, half), lambda h, t, core: (t, side_of(h, core))),
                 pl.BlockSpec((half, RANK), lambda h, t, core: (side_of(h, core), 0)),
             ],
             scratch_shapes=[pltpu.VMEM((half, RANK), jnp.bfloat16)] * 2,
@@ -455,9 +446,9 @@
     wide_half = lax.all_to_all(tiles, "x", 0, 0, tiled=True).reshape(-1, RANK)
 
     inverse, orthonormal = inverted(core, gram_half, other_core(gram_half), projected)
-    own, own_squares = transpose_of(wide_half, inverse, lax.axis_size(COL))
-    squares = own_squares + other_core(own_squares)
-    squares = lax.all_to_all(squares, COL, 0, 0, tiled=True)
+    everyone = ("c", *COL)
+    own, squares = transpose_of(wide_half, inverse, lax.axis_size(everyone))
+    squares = lax.all_to_all(squares, everyone, 0, 0, tiled=True)
     other = other_core(own)
     new_momentum = remembered(core, momentum, gradient, orthonormal, own, other)
     update, new_basis = updated(core, orthonormal, own, other, squares)

time: 169 us -> 165 us (0.976)
  Pallas kernels: 68.4 us -> 64.9 us
    pallas_call x1, Pallas kernels: 6.51 us -> 4.34 us  [project(): pl.pallas_call(project_kernel, in_specs=[pl.BlockSpec(memory_space=pltpu....]
    ppermute x4 -> x3, starting transfers between devices: 7.53 us -> 7.33 us  [other_core(): return lax.ppermute(array, 'c', [(0, 1), (1, 0)])]
  transfers between devices with their start and end apart: 6 -> 5, of which waited for: 2 -> 2; matrix products, arithmetic and copies ran while one was open for 0% -> 0% of each run, Pallas kernels for 32% -> 32%
where the time goes in v5:
time: 165 us; the launch traced here: 164 us
  blocking collectives  78.1 us (47%)
  Pallas kernels  64.9 us (39%)
  starting transfers between devices  15.6 us (9%)
  waiting for transfers between devices  4.55 us (3%)
    pallas_call x1, Pallas kernels, inverted(): pl.pallas_call(inverse_factor, in_specs=[IN_SMEM, IN_VMEM, IN_VMEM, IN_VM...  46.4 us
    all_to_all x2, blocking collectives, scattered(): return lax.all_to_all(tiles, axis, 0, 0, tiled=True).sum(axis=0)  36.3 us
    all_to_all x2, blocking collectives, from_everyone(): return lax.all_to_all(tiles, axis, 0, 0, tiled=True)  25.2 us
    all_to_all x1, blocking collectives, shards(): tiles, gram_half = spread(lax.all_to_all(tiles, 'x', 0, 0, tiled=True))  16.7 us
    ppermute x3, starting transfers between devices, other_core(): return lax.ppermute(array, 'c', [(0, 1), (1, 0)])  7.33 us
    pallas_call x1, Pallas kernels, remembered(): pl.pallas_call(momentum_kernel, grid_spec=pltpu.PrefetchScalarGridSpec(nu...  5.51 us
    all_to_all x1, starting transfers between devices, shards(): squares = lax.all_to_all(squares, everyone, 0, 0, tiled=True)  4.77 us
    pallas_call x1, Pallas kernels, project(): pl.pallas_call(project_kernel, in_specs=[pl.BlockSpec(memory_space=pltpu....  4.34 us
  transfers between devices with their start and end apart: 5, of which 2 were waited for; matrix products, arithmetic and copies ran while one was open for 0% of the time, Pallas kernels for 32%

profile of v5, /device:TPU:1, one launch (start us, length us, event | category | flops | bytes accessed | tf_op | source)
XLA Modules:
  0.0 164.1 jit_solution(17842958401136583325)
XLA Ops:
  0.6 4.3 %project.1 = f32[1024,256]{1,0:T(8,128)S(1)} custom-call(bf16[1024,1024]{1,0:T(8,128)(2,1)} %momentum.7, bf16[1024,1024]{1,0:T(8,128)(2,1)} %gradient.7, f32[1024,256]{1,0:T(8,128)} %basis.1), custom_call_target="tpu_custom_call" | custom-call | flops 2147483648 | tf_op jit(solution)/shard_map/project/pallas_call | solution.py:114
  5.0 19.0 %all_to_all.35 = f32[4,256,256]{2,1,0:T(8,128)S(1)} all-to-all(f32[4,256,256]{2,1,0:T(8,128)S(1)} %bitcast.10), channel_id=1, replica_groups=mesh['x'=4,'c'=2,'z'=8,'y'=4] {'y'}, dimensions={0} | all-to-all | bytes 2097152 | tf_op jit(solution)/shard_map/all_to_all | solution.py:25
  24.0 0.1 reduce_sum.18
  24.1 17.2 %all_to_all.36 = f32[8,32,256]{2,1,0:T(8,128)S(1)} all-to-all(f32[8,32,256]{2,1,0:T(8,128)S(1)} %bitcast.11), channel_id=1, replica_groups=mesh['x'=4,'c'=2,'z'=8,'y'=4] {'z'}, dimensions={0} | all-to-all | bytes 524288 | tf_op jit(solution)/shard_map/all_to_all | solution.py:25
  41.4 0.0 copy-start
  41.4 0.0 copy-start.1
  41.4 12.2 %all_to_all.37 = f32[8,32,256]{2,1,0:T(8,128)S(1)} all-to-all(f32[8,32,256]{2,1,0:T(8,128)S(1)} %broadcast_in_dim.17), channel_id=1, replica_groups=mesh['x'=4,'c'=2,'z'=8,'y'=4] {'z'}, dimensions={0} | all-to-all | bytes 524288 | tf_op jit(solution)/shard_map/all_to_all | solution.py:30
  53.6 0.1 broadcast_in_dim.19
  53.6 13.0 %all_to_all.38 = f32[4,256,256]{2,1,0:T(8,128)S(1)} all-to-all(f32[4,256,256]{2,1,0:T(8,128)S(1)} %broadcast_in_dim.19), channel_id=1, replica_groups=mesh['x'=4,'c'=2,'z'=8,'y'=4] {'y'}, dimensions={0} | all-to-all | bytes 2097152 | tf_op jit(solution)/shard_map/all_to_all | solution.py:30
  66.7 0.0 copy-done
  66.7 0.0 copy-done.1
  66.7 1.7 %widen_given.1.outgoing = f32[768,256]{1,0:T(8,128)S(1)} custom-call(s32[1]{0:T(128)} %bitcast.core, bf16[1024,1024]{1,0:T(8,128)(2,1)S(1)} %copy-done, bf16[1024,1024]{1,0:T(8,128)(2,1)S(1)} %copy-done.1, f32[1024,256]{1,0:T(8,128)S(1)} %bitcast.6), custom_call_target="tpu_custom_call" | custom-call | flops 1073741824 | tf_op jit(solution)/shard_map/widen_given/pallas_call | solution.py:148
  68.4 5.5 %collective-permute-start = (f32[768,256]{1,0:T(8,128)S(1)}, f32[768,256]{1,0:T(8,128)S(1)}, u32[]{:S(2)}, u32[]{:S(2)}) collective-permute-start(f32[768,256]{1,0:T(8,128)S(1)} %widen_given.1.outgoing), channel_id=1, source_target_pairs={{0,32},{32,0},{1,33},{33,1},{2,34},{34,2},{3,35},{35,3},{4,36},{36... | collective-permute-start | bytes 2359304 | tf_op jit(solution)/shard_map/ppermute | solution.py:38
  74.0 1.4 widen_kept.1.kept
  75.4 0.5 collective-permute-done.received
  75.9 0.1 merge.1
  76.0 16.7 %all_to_all.39.arrived = f32[4,224,256]{2,1,0:T(8,128)S(1)} all-to-all(f32[4,224,256]{2,1,0:T(8,128)S(1)} %merge.1), channel_id=1, replica_groups=mesh['x'=4,'c'=2,'z'=8,'y'=4] {'x'}, dimensions={0} | all-to-all | bytes 1835008 | tf_op jit(solution)/shard_map/all_to_all | solution.py:445
  92.6 0.8 spread.1
  93.5 1.8 %collective-permute-start.1 = (f32[96,256]{1,0:T(8,128)S(1)}, f32[96,256]{1,0:T(8,128)S(1)}, u32[]{:S(2)}, u32[]{:S(2)}) collective-permute-start(f32[96,256]{1,0:T(8,128)S(1)} %get-tuple-element.15.own), channel_id=1, source_target_pairs={{0,32},{32,0},{1,33},{33,1},{2,34},{34,2},{3,35},{35,3},{4,36},{36... | collective-permute-start | bytes 294920 | tf_op jit(solution)/shard_map/ppermute | solution.py:38
  95.3 3.5 %all-to-all-start.5 = ((f32[4,128,256]{2,1,0:T(8,128)}), f32[4,128,256]{2,1,0:T(8,128)S(1)}, u32[]{:S(2)}, u32[]{:S(2)}) async-start(f32[4,128,256]{2,1,0:T(8,128)} %get-tuple-element.17), calls=%async_computation.5 | async-start | bytes 1048576 | tf_op jit(solution)/shard_map/all_to_all | solution.py:446
  98.8 0.0 collective-permute-done.1.other
  98.8 46.4 %inverse_factor.1 = (f32[256,256]{1,0:T(8,128)S(1)}, f32[1024,256]{1,0:T(8,128)S(1)}) custom-call(s32[1]{0:T(128)} %bitcast.core, f32[96,256]{1,0:T(8,128)S(1)} %get-tuple-element.15.own, f32[96,256]{1,0:T(8,128)S(1)} %collective-permute-done.1.other, f32[1024,256]{1,0:T(8,128)S(1)} %bitcast.8), custom_call_target="tpu_custom_call" | custom-call | flops 4294967296 | tf_op jit(solution)/shard_map/inverse_factor/pallas_call | solution.py:304
  145.1 0.0 all-to-all-done.5
  145.2 1.1 transposed.1
  146.2 0.0 collective-permute-start.2
  146.2 4.8 %all-to-all-start.6 = ((f32[64,1,256]{2,1,0:T(1,128)}), f32[64,1,256]{2,1,0:T(1,128)S(1)}, u32[]{:S(2)}, u32[]{:S(2)}) async-start(f32[64,1,256]{2,1,0:T(1,128)} %get-tuple-element.20), calls=%async_computation.6 | async-start | bytes 131072 | tf_op jit(solution)/shard_map/all_to_all | solution.py:451
  151.0 0.0 collective-permute-done.2.other
  151.0 5.5 %new_momentum.1 = bf16[1024,1024]{1,0:T(8,128)(2,1)} custom-call(s32[1]{0:T(128)} %bitcast.core, bf16[1024,1024]{1,0:T(8,128)(2,1)} %momentum.7, bf16[1024,1024]{1,0:T(8,128)(2,1)} %gradient.7, f32[1024,256]{1,0:T(8,128)S(1)} %get-tuple-element.16.orthonormal, f32[512,256]{1,0:T(8,128)S(1)} %get-tuple-element.19.own, f32[512,256]{1,0:T(8,128)S(1)} %collective-permute-done.2.other), custom_call_target="tpu_custom_call" | custom-call | flops 4294967296 | tf_op jit(solution)/shard_map/new_momentum/pallas_call | solution.py:367
  156.5 4.1 %all-to-all-done.6.squares = f32[64,1,256]{2,1,0:T(1,128)S(1)} async-done(((f32[64,1,256]{2,1,0:T(1,128)}), f32[64,1,256]{2,1,0:T(1,128)S(1)}, u32[]{:S(2)}, u32[]{:S(2)}) %all-to-all-start.6) | async-done | bytes 65568 | tf_op jit(solution)/shard_map/all_to_all | solution.py:451
  160.6 3.5 %update.1 = (f32[1024,1024]{1,0:T(8,128)}, f32[1024,256]{1,0:T(8,128)}) custom-call(s32[1]{0:T(128)} %bitcast.core, f32[1024,256]{1,0:T(8,128)S(1)} %get-tuple-element.16.orthonormal, f32[512,256]{1,0:T(8,128)S(1)} %get-tuple-element.19.own, f32[512,256]{1,0:T(8,128)S(1)} %collective-permute-done.2.other, f32[64,1,256]{2,1,0:T(1,128)S(1)} %all-to-all-done.6.squares), custom_call_target="tpu_custom_call" | custom-call | flops 1610612736 | tf_op jit(solution)/shard_map/update/pallas_call | solution.py:405
  (2 shorter events, 0.0 us)
Async XLA Ops:
  41.4 25.3 %copy-start = (bf16[1024,1024]{1,0:T(8,128)(2,1)S(1)}, bf16[1024,1024]{1,0:T(8,128)(2,1)}, u32[]{:S(2)}) copy-start(bf16[1024,1024]{1,0:T(8,128)(2,1)} %momentum.7) | copy-start | bytes 6291460
  41.4 25.3 %copy-start.1 = (bf16[1024,1024]{1,0:T(8,128)(2,1)S(1)}, bf16[1024,1024]{1,0:T(8,128)(2,1)}, u32[]{:S(2)}) copy-start(bf16[1024,1024]{1,0:T(8,128)(2,1)} %gradient.7) | copy-start | bytes 6291460
  68.4 7.4 %collective-permute-start = (f32[768,256]{1,0:T(8,128)S(1)}, f32[768,256]{1,0:T(8,128)S(1)}, u32[]{:S(2)}, u32[]{:S(2)}) collective-permute-start(f32[768,256]{1,0:T(8,128)S(1)} %widen_given.1.outgoing), channel_id=1, source_target_pairs={{0,32},{32,0},{1,33},{33,1},{2,34},{34,2},{3,35},{35,3},{4,36},{36... | collective-permute-start | bytes 2359304 | tf_op jit(solution)/shard_map/ppermute | solution.py:38
  93.5 5.3 %collective-permute-start.1 = (f32[96,256]{1,0:T(8,128)S(1)}, f32[96,256]{1,0:T(8,128)S(1)}, u32[]{:S(2)}, u32[]{:S(2)}) collective-permute-start(f32[96,256]{1,0:T(8,128)S(1)} %get-tuple-element.15.own), channel_id=1, source_target_pairs={{0,32},{32,0},{1,33},{33,1},{2,34},{34,2},{3,35},{35,3},{4,36},{36... | collective-permute-start | bytes 294920 | tf_op jit(solution)/shard_map/ppermute | solution.py:38
  95.3 49.9 %all-to-all-start.5 = ((f32[4,128,256]{2,1,0:T(8,128)}), f32[4,128,256]{2,1,0:T(8,128)S(1)}, u32[]{:S(2)}, u32[]{:S(2)}) async-start(f32[4,128,256]{2,1,0:T(8,128)} %get-tuple-element.17), calls=%async_computation.5 | async-start | bytes 1048576 | tf_op jit(solution)/shard_map/all_to_all | solution.py:446
  146.2 4.8 %collective-permute-start.2 = (f32[512,256]{1,0:T(8,128)S(1)}, f32[512,256]{1,0:T(8,128)S(1)}, u32[]{:S(2)}, u32[]{:S(2)}) collective-permute-start(f32[512,256]{1,0:T(8,128)S(1)} %get-tuple-element.19.own), channel_id=1, source_target_pairs={{0,32},{32,0},{1,33},{33,1},{2,34},{34,2},{3,35},{35,3},{4,36},{36... | collective-permute-start | bytes 1572872 | tf_op jit(solution)/shard_map/ppermute | solution.py:38
  146.2 14.4 %all-to-all-start.6 = ((f32[64,1,256]{2,1,0:T(1,128)}), f32[64,1,256]{2,1,0:T(1,128)S(1)}, u32[]{:S(2)}, u32[]{:S(2)}) async-start(f32[64,1,256]{2,1,0:T(1,128)} %get-tuple-element.20), calls=%async_computation.6 | async-start | bytes 131072 | tf_op jit(solution)/shard_map/all_to_all | solution.py:451

commit v6 on v5

--- a/solution.py
+++ b/solution.py
@@ -41,22 +41,37 @@
 def mxu(left, right, dims):
     return lax.dot_general(left, right, (dims, ((), ())), preferred_element_type=jnp.float32)
 
+
 def parts(array):
     top = array.astype(jnp.bfloat16)
     return top, (array - top.astype(jnp.float32)).astype(jnp.bfloat16)
 
+
 def dot3(left, right, dims):
     (a, b), (c, d) = parts(left), parts(right)
     return mxu(a, c, dims) + (mxu(a, d, dims) + mxu(b, c, dims))
 
+
 def dot1(left, right, dims):
     return mxu(left.astype(jnp.bfloat16), right.astype(jnp.bfloat16), dims)
 
+
 PLAIN = ((1,), (0,))
 FLIPPED = ((1,), (1,))
 
-def core_number():
-    return lax.axis_index("c").astype(jnp.int32)[None]
+
+def place_on(axis):
+    return lax.axis_index(axis).astype(jnp.int32)[None]
+
+
+def from_others(array, axis):
+    length = lax.axis_size(axis)
+    rings = ([(i, (i + k) % length) for i in range(length)] for k in range(1, length))
+    return [array, *(lax.ppermute(array, axis, ring) for ring in rings)]
+
+
+def origin(place, k, length):
+    return lax.rem(place + length - k, length)
 
 
 def cost(flops):
@@ -67,7 +82,6 @@
 IN_SMEM = pl.BlockSpec(memory_space=pltpu.SMEM)
 TILE = 256
 HALF = RANK // 2
-PACKED = 3 * HALF // 4
 
 
 def wider(tile):
@@ -129,34 +143,50 @@
     )(*in_hbm(momentum, gradient, basis))
 
 
-def widen_kernel(with_gram, core, momentum, gradient, projected, out, left):
+def widen_kernel(give, core, line, momentum, gradient, *refs):
+    *chunks, out, left = refs
     half = momentum.shape[1] // 2
-    left[:RANK, :], left[RANK:, :] = parts(projected[...].T)
-    place = 1 - core[0] if with_gram else core[0]
+    for k, chunk in enumerate(chunks):
+        top, low = parts(chunk[...].T)
+        start = origin(line[0], k, len(chunks)) * chunk.shape[0]
+        span = pl.ds(pl.multiple_of(start, TILE), chunk.shape[0])
+        left[:RANK, span] = top
+        left[RANK:, span] = low
+    place = 1 - core[0] if give else core[0]
     span = pl.ds(pl.multiple_of(place * half, half), half)
     product = mxu(left[...], momentum[:, span], PLAIN) + mxu(left[...], gradient[:, span], PLAIN)
-    out[:half, :] = (product[:RANK] + product[RANK:]).T
-
-    if with_gram:
-        top, low = parts(projected[...])
-        product = mxu(left[...], top, PLAIN)
-        out[half:, :] = product[:RANK] + (product[RANK:] + mxu(left[:RANK, :], low, PLAIN))
-
-
-def widen(with_gram, core, momentum, gradient, projected):
+    out[...] = (product[:RANK] + product[RANK:]).T
+
+
+def widen(give, core, line, momentum, gradient, chunks):
     rows, columns = momentum.shape
     return pl.pallas_call(
-        functools.partial(widen_kernel, with_gram),
-        in_specs=[IN_SMEM, IN_VMEM, IN_VMEM, IN_VMEM],
+        functools.partial(widen_kernel, give),
+        in_specs=[IN_SMEM, IN_SMEM] + [IN_VMEM] * (2 + len(chunks)),
         out_specs=IN_VMEM,
-        out_shape=jax.ShapeDtypeStruct(
-            (columns // 2 + (RANK if with_gram else 0), RANK), jnp.float32
-        ),
+        out_shape=jax.ShapeDtypeStruct((columns // 2, RANK), jnp.float32),
         scratch_shapes=[pltpu.VMEM((2 * RANK, rows), jnp.bfloat16)],
         cost_estimate=cost(4 * rows * columns * RANK),
         compiler_params=limit(16),
-        name="widen_given" if with_gram else "widen_kept",
-    )(core, momentum, gradient, projected)
+        name="widen_given" if give else "widen_kept",
+    )(core, line, momentum, gradient, *chunks)
+
+
+def gram_kernel(chunk, out):
+    flat = parts(chunk[...].T)
+    out[...] = split_dot(flat, parts(chunk[...]), PLAIN)
+
+
+def gram_of(chunk):
+    return pl.pallas_call(
+        gram_kernel,
+        in_specs=[IN_VMEM],
+        out_specs=IN_VMEM,
+        out_shape=jax.ShapeDtypeStruct((RANK, RANK), jnp.float32),
+        cost_estimate=cost(6 * chunk.size * RANK),
+        compiler_params=limit(6),
+        name="gram",
+    )(chunk)
 
 
 def split_dot(left, right, dims):
@@ -168,90 +198,9 @@
     return pltpu.CompilerParams(vmem_limit_bytes=mib << 20)
 
 
-def folded(block):
-    half = block.shape[0] // 2
-    return jnp.concatenate((block[:half], block[half:]), axis=1)
-
-
-def unfolded(block):
-    return jnp.concatenate((block[:, :HALF], block[:, HALF:]), axis=0)
-
-
-def merge_kernel(core, outgoing, received, kept, out):
-    sides = out.shape[0]
-    each = kept.shape[0] // sides
-    for side in range(sides):
-        span = pl.ds(side * each, each)
-        out[side, :each, :] = kept[span, :] + received[span, :]
-    gram = outgoing[kept.shape[0] :, :] + received[kept.shape[0] :, :]
-    corner = gram[HALF:, :HALF]
-
-    def put(square, strip):
-        for side in range(sides):
-            out[side, each : each + HALF // 2, :] = folded(square)
-            out[side, each + HALF // 2 :, :] = folded(strip)
-
-    @pl.when(core[0] == 0)
-    def _():
-        put(gram[:HALF, :HALF], corner[: HALF // 2])
-
-    @pl.when(core[0] == 1)
-    def _():
-        put(gram[HALF:, HALF:], corner[HALF // 2 :])
-
-
-def merge(core, outgoing, received, kept, sides):
-    each = kept.shape[0] // sides
-    return pl.pallas_call(
-        merge_kernel,
-        in_specs=[IN_SMEM, IN_VMEM, IN_VMEM, IN_VMEM],
-        out_specs=IN_VMEM,
-        out_shape=jax.ShapeDtypeStruct((sides, each + PACKED, RANK), jnp.float32),
-        cost_estimate=cost(kept.size),
-        compiler_params=pltpu.CompilerParams(vmem_limit_bytes=8 << 20),
-        name="merge",
-    )(core, outgoing, received, kept)
-
-
-def spread_kernel(arrived, tiles, gram_half):
-    sides, each, _ = tiles.shape
-    wide = arrived[0, :each, :]
-    gram = arrived[0, each:, :]
-    for side in range(1, sides):
-        wide = wide + arrived[side, :each, :]
-        gram = gram + arrived[side, each:, :]
-    for side in range(sides):
-        tiles[side] = wide
-    gram_half[...] = gram
-
-
-def spread(arrived):
-    sides, lines, _ = arrived.shape
-    return pl.pallas_call(
-        spread_kernel,
-        in_specs=[IN_VMEM],
-        out_specs=[IN_VMEM, IN_VMEM],
-        out_shape=[
-            pltpu.HBM((sides, lines - PACKED, RANK), jnp.float32),
-            jax.ShapeDtypeStruct((PACKED, RANK), jnp.float32),
-        ],
-        cost_estimate=cost(arrived.size),
-        compiler_params=limit(6),
-        name="spread",
-    )(arrived)
-
-
-def inverse_factor(core, own, other, projected, out_ref, orthonormal, work):
-    first = jnp.where(core[0] == 0, own[...], other[...])
-    second = jnp.where(core[0] == 0, other[...], own[...])
-    corner = jnp.concatenate((unfolded(first[HALF // 2 :]), unfolded(second[HALF // 2 :])), axis=0)
-    gram = jnp.concatenate(
-        (
-            jnp.concatenate((unfolded(first[: HALF // 2]), corner.T), axis=1),
-            jnp.concatenate((corner, unfolded(second[: HALF // 2])), axis=1),
-        ),
-        axis=0,
-    )
+def inverse_factor(line, gram_ref, *refs):
+    *chunks, out_ref, orthonormal, work = refs
+    gram = gram_ref[...]
     shape = (RANK, RANK)
     row, column = (lax.broadcasted_iota(jnp.int32, shape, d) for d in (0, 1))
     eye = (row == column).astype(jnp.float32)
@@ -293,54 +242,72 @@
         out_ref[...] = jnp.where(row >= column, work[:, RANK:], 0.0)
 
     right = parts(out_ref[...])
-
-    @pl.loop(0, projected.shape[0] // TILE)
-    def _(t):
-        span = pl.ds(pl.multiple_of(t * TILE, TILE), TILE)
-        orthonormal[span, :] = split_dot(parts(projected[span, :]), right, FLIPPED)
-
-
-def inverted(core, own, other, projected):
+    for k, chunk in enumerate(chunks):
+        start = origin(line[0], k, len(chunks)) * chunk.shape[0]
+        span = pl.ds(pl.multiple_of(start, TILE), chunk.shape[0])
+        orthonormal[span, :] = split_dot(parts(chunk[...]), right, FLIPPED)
+
+
+def inverted(line, gram, chunks):
+    rows = len(chunks) * chunks[0].shape[0]
     return pl.pallas_call(
         inverse_factor,
-        in_specs=[IN_SMEM, IN_VMEM, IN_VMEM, IN_VMEM],
+        in_specs=[IN_SMEM] + [IN_VMEM] * (1 + len(chunks)),
         out_specs=[IN_VMEM, IN_VMEM],
         out_shape=[
             jax.ShapeDtypeStruct((RANK, RANK), jnp.float32),
-            jax.ShapeDtypeStruct(projected.shape, jnp.float32),
+            jax.ShapeDtypeStruct((rows, RANK), jnp.float32),
         ],
         scratch_shapes=[pltpu.VMEM((RANK, 2 * RANK), jnp.float32)],
         cost_estimate=cost(1 << 32),
         compiler_params=limit(12),
         name="inverse_factor",
-    )(core, own, other, projected)
-
-
-def transposed_kernel(wide, inverse, out, squares):
-    c, d = parts(inverse[...])
-    total = jnp.zeros((1, RANK), jnp.float32)
-    for t in range(wide.shape[0] // TILE):
-        span = slice(t * TILE, (t + 1) * TILE)
-        a, b = parts(wide[span, :])
-        tile = mxu(a, c, FLIPPED) + (mxu(a, d, FLIPPED) + mxu(b, c, FLIPPED))
-        out[span, :] = tile
-        total += jnp.sum(tile * tile, axis=0, keepdims=True)
+    )(line, gram, *chunks)
+
+
+def transposed_kernel(arrived, inverse, out, squares):
+    wide = arrived[0]
+    for side in range(1, arrived.shape[0]):
+        wide = wide + arrived[side]
+    tile = split_dot(parts(wide), parts(inverse[...]), FLIPPED)
+    out[...] = tile
+    total = jnp.sum(tile * tile, axis=0, keepdims=True)
     squares[...] = jnp.broadcast_to(total[None], squares.shape)
 
 
-def transpose_of(wide, inverse, copies):
+def transpose_of(arrived, inverse, copies):
     return pl.pallas_call(
         transposed_kernel,
         in_specs=[IN_VMEM, IN_VMEM],
         out_specs=[IN_VMEM, IN_VMEM],
         out_shape=[
-            jax.ShapeDtypeStruct(wide.shape, jnp.float32),
-            jax.ShapeDtypeStruct((copies, 1, RANK), jnp.float32),
+            jax.ShapeDtypeStruct(arrived.shape[1:], jnp.float32),
+            pltpu.HBM((copies, 1, RANK), jnp.float32),
         ],
-        cost_estimate=cost(6 * wide.size * RANK),
-        compiler_params=pltpu.CompilerParams(vmem_limit_bytes=8 << 20),
+        cost_estimate=cost(6 * arrived.size * RANK),
+        compiler_params=limit(8),
         name="transposed",
-    )(wide, inverse)
+    )(arrived, inverse)
+
+
+def assemble_kernel(line, *refs):
+    *pieces, out = refs
+    for k, piece in enumerate(pieces):
+        start = origin(line[0], k, len(pieces)) * piece.shape[0]
+        out[pl.ds(pl.multiple_of(start, HALF), piece.shape[0]), :] = piece[...]
+
+
+def assembled(line, pieces):
+    rows = len(pieces) * pieces[0].shape[0]
+    return pl.pallas_call(
+        assemble_kernel,
+        in_specs=[IN_SMEM] + [IN_VMEM] * len(pieces),
+        out_specs=IN_VMEM,
+        out_shape=jax.ShapeDtypeStruct((rows, RANK), jnp.float32),
+        cost_estimate=cost(rows * RANK),
+        compiler_params=limit(6),
+        name="assembled",
+    )(line, *pieces)
 
 
 SPAN = 512
@@ -429,26 +396,27 @@
     )(core, orthonormal, own, other, squares)
 
 
-def shards(momentum, gradient, right_basis):
-    core = core_number()
+def step(momentum, gradient, right_basis):
+    core, line, side = place_on("c"), place_on("y"), place_on("x")
     sides = lax.axis_size("x")
 
     part = project(momentum, gradient, right_basis)
-    part, core = lax.optimization_barrier((part, core))
     own = scattered(scattered(part, "y"), "z")
-    projected = gathered(gathered(own, "z"), "y")
-
-    outgoing = widen(True, core, momentum, gradient, projected)
-    received = other_core(outgoing)
-    kept = widen(False, core, momentum, gradient, projected)
-    tiles = merge(core, outgoing, received, kept, sides)
-    tiles, gram_half = spread(lax.all_to_all(tiles, "x", 0, 0, tiled=True))
-    wide_half = lax.all_to_all(tiles, "x", 0, 0, tiled=True).reshape(-1, RANK)
-
-    inverse, orthonormal = inverted(core, gram_half, other_core(gram_half), projected)
-    everyone = ("c", *COL)
-    own, squares = transpose_of(wide_half, inverse, lax.axis_size(everyone))
-    squares = lax.all_to_all(squares, everyone, 0, 0, tiled=True)
+    chunk = gathered(own, "z")
+    chunks = from_others(chunk, "y")
+
+    piece = scattered(gram_of(chunk), ("x", "y"))
+    gram_matrix = gathered(piece + other_core(piece), ("x", "y"))
+    inverse, orthonormal = inverted(line, gram_matrix, chunks)
+
+    received = other_core(widen(True, core, line, momentum, gradient, chunks))
+    wide = widen(False, core, line, momentum, gradient, chunks) + received
+    arrived = lax.all_to_all(wide.reshape(sides, -1, RANK), "x", 0, 0, tiled=True)
+
+    piece, squares = transpose_of(arrived, inverse, lax.axis_size((*ROW, *COL)))
+    pieces = from_others(piece, "x")
+    squares = lax.all_to_all(squares, (*ROW, *COL), 0, 0, tiled=True)
+    own = assembled(side, pieces)
     other = other_core(own)
     new_momentum = remembered(core, momentum, gradient, orthonormal, own, other)
     update, new_basis = updated(core, orthonormal, own, other, squares)
@@ -459,7 +427,7 @@
     split = Mesh(mesh.devices.reshape(4, 2, 8, 4), (*ROW, *COL))
     placed = (P(ROW, COL), P(ROW, COL), P(COL, None))
     return jax.shard_map(
-        shards,
+        step,
         mesh=split,
         in_specs=placed,
         out_specs=(P(ROW, COL), P(COL, None), P(ROW, COL)),

time: 165 us -> 189 us (1.15)
  waiting for transfers between devices: 4.55 us -> 24.3 us
  blocking collectives: 78.1 us -> 61.8 us
  starting transfers between devices: 15.6 us -> 30.2 us
  local copies, waits for them, and re-layouts: 0.11 us -> 4.9 us
  other arithmetic: 0.1 us -> 2.03 us
    all_to_all x1 -> x0, blocking collectives: 16.7 us -> none  [shards(): tiles, gram_half = spread(lax.all_to_all(tiles, 'x', 0, 0, tiled=True))]
    all_to_all x2 -> x3, blocking collectives: 36.3 us -> 49.8 us  [scattered(): return lax.all_to_all(tiles, axis, 0, 0, tiled=True).sum(axis=0)]
    all_to_all x2 -> x1, blocking collectives: 25.2 us -> 12 us  [from_everyone(): return lax.all_to_all(tiles, axis, 0, 0, tiled=True)]
    ppermute x0 -> x6, waiting for transfers between devices: none -> 11.8 us  [from_others(): return [array, *(lax.ppermute(array, axis, ring) for ring in rings)]]
    ppermute x0 -> x6, starting transfers between devices: none -> 7.68 us  [from_others(): return [array, *(lax.ppermute(array, axis, ring) for ring in rings)]]
    all_to_all x2 -> x3, waiting for transfers between devices: 4.08 us -> 11.7 us  [the longest x1 9.19 us: step(): squares = lax.all_to_all(squares, (*ROW, *COL), 0, 0, tiled=True)]
    all_to_all x2 -> x3, starting transfers between devices: 8.24 us -> 12.6 us  [the longest x1 5.56 us: step(): squares = lax.all_to_all(squares, (*ROW, *COL), 0, 0, tiled=True)]
    unnamed x4 -> x10, local copies, waits for them, and re-layouts: 0.01 us -> 4.15 us
  transfers between devices with their start and end apart: 5 -> 12, of which waited for: 2 -> 7; matrix products, arithmetic and copies ran while one was open for 0% -> 1% of each run, Pallas kernels for 32% -> 28%
where the time goes in v6:
time: 189 us
  Pallas kernels  64.7 us (34%)
  blocking collectives  61.8 us (33%)
  starting transfers between devices  30.2 us (16%)
  waiting for transfers between devices  24.3 us (13%)
  local copies, waits for them, and re-layouts  4.9 us (3%)
  other arithmetic  2.03 us (1%)
    all_to_all x3, blocking collectives, scattered(): return lax.all_to_all(tiles, axis, 0, 0, tiled=True).sum(axis=0)  49.8 us
    pallas_call x1, Pallas kernels, inverted(): pl.pallas_call(inverse_factor, in_specs=[IN_SMEM] + [IN_VMEM] * (1 + len(...  45.2 us
    all_to_all x1, blocking collectives, from_everyone(): return lax.all_to_all(tiles, axis, 0, 0, tiled=True)  12 us
    ppermute x6, waiting for transfers between devices, from_others(): return [array, *(lax.ppermute(array, axis, ring) for ring in rings)]  11.8 us
    ppermute x3, starting transfers between devices, other_core(): return lax.ppermute(array, 'c', [(0, 1), (1, 0)])  9.95 us
    all_to_all x1, waiting for transfers between devices, step(): squares = lax.all_to_all(squares, (*ROW, *COL), 0, 0, tiled=True)  9.19 us
    ppermute x6, starting transfers between devices, from_others(): return [array, *(lax.ppermute(array, axis, ring) for ring in rings)]  7.68 us
    all_to_all x1, starting transfers between devices, step(): squares = lax.all_to_all(squares, (*ROW, *COL), 0, 0, tiled=True)  5.56 us
  transfers between devices with their start and end apart: 12, of which 7 were waited for; matrix products, arithmetic and copies ran while one was open for 1% of the time, Pallas kernels for 28%

profile of v6, /device:TPU:1, one launch (start us, length us, event | category | flops | bytes accessed | tf_op | source)
XLA Modules:
  0.0 188.6 jit_solution(8290796826888781645)
XLA Ops:
  0.6 4.3 %project.1 = f32[1024,256]{1,0:T(8,128)S(1)} custom-call(bf16[1024,1024]{1,0:T(8,128)(2,1)} %momentum.7, bf16[1024,1024]{1,0:T(8,128)(2,1)} %gradient.7, f32[1024,256]{1,0:T(8,128)} %basis.1), custom_call_target="tpu_custom_call" | custom-call | flops 2147483648 | tf_op jit(solution)/shard_map/project/pallas_call | solution.py:128
  5.0 0.0 copy-start
  5.0 19.2 %all_to_all.35 = f32[4,256,256]{2,1,0:T(8,128)S(1)} all-to-all(f32[4,256,256]{2,1,0:T(8,128)S(1)} %bitcast.16), channel_id=1, replica_groups=mesh['x'=4,'c'=2,'z'=8,'y'=4] {'y'}, dimensions={0} | all-to-all | bytes 2097152 | tf_op jit(solution)/shard_map/all_to_all | solution.py:25
  24.2 0.1 reduce_sum.27
  24.2 17.2 %all_to_all.36 = f32[8,32,256]{2,1,0:T(8,128)S(1)} all-to-all(f32[8,32,256]{2,1,0:T(8,128)S(1)} %bitcast.19), channel_id=1, replica_groups=mesh['x'=4,'c'=2,'z'=8,'y'=4] {'z'}, dimensions={0} | all-to-all | bytes 524288 | tf_op jit(solution)/shard_map/all_to_all | solution.py:25
  41.5 12.0 %all_to_all.37 = f32[8,32,256]{2,1,0:T(8,128)S(1)} all-to-all(f32[8,32,256]{2,1,0:T(8,128)S(1)} %broadcast_in_dim.23), channel_id=1, replica_groups=mesh['x'=4,'c'=2,'z'=8,'y'=4] {'z'}, dimensions={0} | all-to-all | bytes 524288 | tf_op jit(solution)/shard_map/all_to_all | solution.py:30
  53.5 0.3 collective-permute-start.1
  53.8 1.8 collective-permute-start.2
  55.5 0.6 collective-permute-start.3
  56.1 7.1 %collective-permute-done.1.refs_1_ = f32[256,256]{1,0:T(8,128)S(1)} collective-permute-done((f32[256,256]{1,0:T(8,128)S(1)}, f32[256,256]{1,0:T(8,128)S(1)}, u32[]{:S(2)}, u32[]{:S(2)}) %collective-permute-start.1) | collective-permute-done | bytes 262176 | tf_op jit(solution)/shard_map/ppermute | solution.py:70
  63.3 0.0 collective-permute-done.2.refs_2_
  63.3 0.8 collective-permute-done.3.refs_3_
  64.0 0.0 copy-done
  64.0 1.6 copy-done.1
  65.6 2.5 %widen_given.1 = f32[512,256]{1,0:T(8,128)} custom-call(s32[1]{0:T(128)} %bitcast.core, s32[1]{0:T(128)} %bitcast.1.line, bf16[1024,1024]{1,0:T(8,128)(2,1)S(1)} %copy-done, bf16[1024,1024]{1,0:T(8,128)(2,1)S(1)} %copy-done.1, f32[256,256]{1,0:T(8,128)S(1)} %bitcast.12, f32[256,256]{1,0:T(8,128)S(1)} %collective-permute-done.1.refs_1_, ...), custom_call_target="tpu_custom_call" | custom-call | flops 1073741824 | tf_op jit(solution)/shard_map/widen_given/pallas_call | solution.py:163
  68.1 5.7 %collective-permute-start.4 = (f32[512,256]{1,0:T(8,128)}, f32[512,256]{1,0:T(8,128)}, u32[]{:S(2)}, u32[]{:S(2)}) collective-permute-start(f32[512,256]{1,0:T(8,128)} %widen_given.1), channel_id=1, source_target_pairs={{0,32},{32,0},{1,33},{33,1},{2,34},{34,2},{3,35},{35,3},{4,36},{36... | collective-permute-start | bytes 1572872 | tf_op jit(solution)/shard_map/ppermute | solution.py:38
  73.8 0.3 gram.1
  74.1 13.4 %all_to_all.38 = f32[16,16,256]{2,1,0:T(8,128)S(1)} all-to-all(f32[16,16,256]{2,1,0:T(8,128)S(1)} %bitcast.17), channel_id=1, replica_groups=mesh['x'=4,'c'=2,'z'=8,'y'=4] {'x','y'}, dimensions={0} | all-to-all | bytes 524288 | tf_op jit(solution)/shard_map/all_to_all | solution.py:25
  87.6 1.7 collective-permute-start
  89.3 0.8 collective-permute-done
  90.2 0.7 broadcast_in_dim.24
  90.9 3.5 %all-to-all-start.4 = ((f32[16,16,256]{2,1,0:T(8,128)}), f32[16,16,256]{2,1,0:T(8,128)S(1)}, u32[]{:S(2)}, u32[]{:S(2)}) async-start(f32[16,16,256]{2,1,0:T(8,128)} %broadcast_in_dim.24), calls=%async_computation.4 | async-start | bytes 524288 | tf_op jit(solution)/shard_map/all_to_all | solution.py:30
  94.4 0.0 copy-start.2
  94.4 1.6 copy-done.2
  96.0 1.7 widen_kept.1
  97.7 0.0 collective-permute-done.4
  97.8 1.9 %add.7 = f32[512,256]{1,0:T(8,128)} add(f32[512,256]{1,0:T(8,128)S(1)} %widen_kept.1, f32[512,256]{1,0:T(8,128)} %collective-permute-done.4) | non-fusion elementwise | flops 131072 | bytes 1572864 | tf_op jit(solution)/shard_map/add | solution.py:413
  99.7 2.5 %all-to-all-done.4 = f32[16,16,256]{2,1,0:T(8,128)S(1)} async-done(((f32[16,16,256]{2,1,0:T(8,128)}), f32[16,16,256]{2,1,0:T(8,128)S(1)}, u32[]{:S(2)}, u32[]{:S(2)}) %all-to-all-start.4) | async-done | bytes 262176 | tf_op jit(solution)/shard_map/all_to_all | solution.py:30
  102.1 3.5 %all-to-all-start.5 = ((f32[4,128,256]{2,1,0:T(8,128)}), f32[4,128,256]{2,1,0:T(8,128)S(1)}, u32[]{:S(2)}, u32[]{:S(2)}) async-start(f32[4,128,256]{2,1,0:T(8,128)} %bitcast.8), calls=%async_computation.5 | async-start | bytes 1048576 | tf_op jit(solution)/shard_map/all_to_all | solution.py:414
  105.6 45.2 %inverse_factor.1 = (f32[256,256]{1,0:T(8,128)S(1)}, f32[1024,256]{1,0:T(8,128)S(1)}) custom-call(s32[1]{0:T(128)} %bitcast.1.line, f32[256,256]{1,0:T(8,128)S(1)} %bitcast.18, f32[256,256]{1,0:T(8,128)S(1)} %bitcast.15, f32[256,256]{1,0:T(8,128)S(1)} %collective-permute-done.1.refs_1_, f32[256,256]{1,0:T(8,128)S(1)} %collective-permute-done.2.refs_2_, ...), custom_call_target="tpu_custom_call" | custom-call | flops 4294967296 | tf_op jit(solution)/shard_map/inverse_factor/pallas_call | solution.py:253
  150.9 0.0 copy-start.3
  150.9 1.0 copy-done.3
  151.8 0.0 all-to-all-done.5.arrived
  151.8 0.0 copy-start.4
  151.8 1.1 transposed.1
  152.9 1.4 collective-permute-start.5
  154.3 2.4 %collective-permute-start.6 = (f32[128,256]{1,0:T(8,128)S(1)}, f32[128,256]{1,0:T(8,128)S(1)}, u32[]{:S(2)}, u32[]{:S(2)}) collective-permute-start(f32[128,256]{1,0:T(8,128)S(1)} %get-tuple-element.11.refs_0_), channel_id=1, source_target_pairs={{0,128},{64,192},{128,0},{192,64},{1,129},{65,193},{129,1},{193,65... | collective-permute-start | bytes 393224 | tf_op jit(solution)/shard_map/ppermute | solution.py:70
  156.7 1.2 collective-permute-start.7
  157.9 0.0 collective-permute-done.5.refs_1_
  158.0 3.0 %collective-permute-done.6.refs_2_ = f32[128,256]{1,0:T(8,128)S(1)} collective-permute-done((f32[128,256]{1,0:T(8,128)S(1)}, f32[128,256]{1,0:T(8,128)S(1)}, u32[]{:S(2)}, u32[]{:S(2)}) %collective-permute-start.6) | collective-permute-done | bytes 131104 | tf_op jit(solution)/shard_map/ppermute | solution.py:70
  161.0 0.9 collective-permute-done.7.refs_3_
  161.9 2.5 %collective-permute-start.8 = (f32[512,256]{1,0:T(8,128)S(1)}, f32[512,256]{1,0:T(8,128)S(1)}, u32[]{:S(2)}, u32[]{:S(2)}) collective-permute-start(f32[512,256]{1,0:T(8,128)S(1)} %assembled.1.own), channel_id=1, source_target_pairs={{0,32},{32,0},{1,33},{33,1},{2,34},{34,2},{3,35},{35,3},{4,36},{36... | collective-permute-start | bytes 1572872 | tf_op jit(solution)/shard_map/ppermute | solution.py:38
  164.4 5.6 %all-to-all-start.6 = ((f32[256,1,256]{2,1,0:T(1,128)}), f32[256,1,256]{2,1,0:T(1,128)S(1)}, u32[]{:S(2)}, u32[]{:S(2)}) async-start(f32[256,1,256]{2,1,0:T(1,128)} %get-tuple-element.12), calls=%async_computation.6 | async-start | bytes 524288 | tf_op jit(solution)/shard_map/all_to_all | solution.py:418
  170.0 0.0 collective-permute-done.8.other
  170.0 0.0 copy-done.4
  170.0 5.5 %new_momentum.1 = bf16[1024,1024]{1,0:T(8,128)(2,1)} custom-call(s32[1]{0:T(128)} %bitcast.core, bf16[1024,1024]{1,0:T(8,128)(2,1)} %momentum.7, bf16[1024,1024]{1,0:T(8,128)(2,1)} %gradient.7, f32[1024,256]{1,0:T(8,128)S(1)} %copy-done.4, f32[512,256]{1,0:T(8,128)S(1)} %assembled.1.own, f32[512,256]{1,0:T(8,128)S(1)} %collective-permute-done.8.other), custom_call_target="tpu_custom_call" | custom-call | flops 4294967296 | tf_op jit(solution)/shard_map/new_momentum/pallas_call | solution.py:334
  175.5 9.2 %all-to-all-done.6.squares = f32[256,1,256]{2,1,0:T(1,128)S(1)} async-done(((f32[256,1,256]{2,1,0:T(1,128)}), f32[256,1,256]{2,1,0:T(1,128)S(1)}, u32[]{:S(2)}, u32[]{:S(2)}) %all-to-all-start.6) | async-done | bytes 262176 | tf_op jit(solution)/shard_map/all_to_all | solution.py:418
  184.7 3.9 %update.1 = (f32[1024,1024]{1,0:T(8,128)}, f32[1024,256]{1,0:T(8,128)}) custom-call(s32[1]{0:T(128)} %bitcast.core, f32[1024,256]{1,0:T(8,128)S(1)} %copy-done.4, f32[512,256]{1,0:T(8,128)S(1)} %assembled.1.own, f32[512,256]{1,0:T(8,128)S(1)} %collective-permute-done.8.other, f32[256,1,256]{2,1,0:T(1,128)S(1)} %all-to-all-done.6.squares), custom_call_target="tpu_custom_call" | custom-call | flops 1610612736 | tf_op jit(solution)/shard_map/update/pallas_call | solution.py:372
  (6 shorter events, 0.1 us)
Async XLA Ops:
  5.0 59.0 %copy-start = (bf16[1024,1024]{1,0:T(8,128)(2,1)S(1)}, bf16[1024,1024]{1,0:T(8,128)(2,1)}, u32[]{:S(2)}) copy-start(bf16[1024,1024]{1,0:T(8,128)(2,1)} %momentum.7) | copy-start | bytes 6291460
  53.5 9.8 %collective-permute-start.1 = (f32[256,256]{1,0:T(8,128)S(1)}, f32[256,256]{1,0:T(8,128)S(1)}, u32[]{:S(2)}, u32[]{:S(2)}) collective-permute-start(f32[256,256]{1,0:T(8,128)S(1)} %bitcast.9), channel_id=1, source_target_pairs={{0,1},{1,2},{2,3},{3,0},{4,5},{5,6},{6,7},{7,4},{8,9},{9,10},{10,1... | collective-permute-start | bytes 786440 | tf_op jit(solution)/shard_map/ppermute | solution.py:70
  53.8 9.5 %collective-permute-start.2 = (f32[256,256]{1,0:T(8,128)S(1)}, f32[256,256]{1,0:T(8,128)S(1)}, u32[]{:S(2)}, u32[]{:S(2)}) collective-permute-start(f32[256,256]{1,0:T(8,128)S(1)} %bitcast.10), channel_id=1, source_target_pairs={{0,2},{1,3},{2,0},{3,1},{4,6},{5,7},{6,4},{7,5},{8,10},{9,11},{10,... | collective-permute-start | bytes 786440 | tf_op jit(solution)/shard_map/ppermute | solution.py:70
  55.5 8.5 %collective-permute-start.3 = (f32[256,256]{1,0:T(8,128)S(1)}, f32[256,256]{1,0:T(8,128)S(1)}, u32[]{:S(2)}, u32[]{:S(2)}) collective-permute-start(f32[256,256]{1,0:T(8,128)S(1)} %bitcast.11), channel_id=1, source_target_pairs={{0,3},{1,0},{2,1},{3,2},{4,7},{5,4},{6,5},{7,6},{8,11},{9,8},{10,9... | collective-permute-start | bytes 786440 | tf_op jit(solution)/shard_map/ppermute | solution.py:70
  64.0 1.6 copy-start.1
  68.1 29.6 %collective-permute-start.4 = (f32[512,256]{1,0:T(8,128)}, f32[512,256]{1,0:T(8,128)}, u32[]{:S(2)}, u32[]{:S(2)}) collective-permute-start(f32[512,256]{1,0:T(8,128)} %widen_given.1), channel_id=1, source_target_pairs={{0,32},{32,0},{1,33},{33,1},{2,34},{34,2},{3,35},{35,3},{4,36},{36... | collective-permute-start | bytes 1572872 | tf_op jit(solution)/shard_map/ppermute | solution.py:38
  87.6 2.6 %collective-permute-start = (f32[16,256]{1,0:T(8,128)S(1)}, f32[16,256]{1,0:T(8,128)S(1)}, u32[]{:S(2)}, u32[]{:S(2)}) collective-permute-start(f32[16,256]{1,0:T(8,128)S(1)} %reduce_sum.29), channel_id=1, source_target_pairs={{0,32},{32,0},{1,33},{33,1},{2,34},{34,2},{3,35},{35,3},{4,36},{36... | collective-permute-start | bytes 49160 | tf_op jit(solution)/shard_map/ppermute | solution.py:38
  90.9 11.2 %all-to-all-start.4 = ((f32[16,16,256]{2,1,0:T(8,128)}), f32[16,16,256]{2,1,0:T(8,128)S(1)}, u32[]{:S(2)}, u32[]{:S(2)}) async-start(f32[16,16,256]{2,1,0:T(8,128)} %broadcast_in_dim.24), calls=%async_computation.4 | async-start | bytes 524288 | tf_op jit(solution)/shard_map/all_to_all | solution.py:30
  94.4 1.6 copy-start.2
  102.1 49.7 %all-to-all-start.5 = ((f32[4,128,256]{2,1,0:T(8,128)}), f32[4,128,256]{2,1,0:T(8,128)S(1)}, u32[]{:S(2)}, u32[]{:S(2)}) async-start(f32[4,128,256]{2,1,0:T(8,128)} %bitcast.8), calls=%async_computation.5 | async-start | bytes 1048576 | tf_op jit(solution)/shard_map/all_to_all | solution.py:414
  150.9 1.0 copy-start.3
  151.8 18.1 %copy-start.4 = (f32[1024,256]{1,0:T(8,128)S(1)}, f32[1024,256]{1,0:T(8,128)}, u32[]{:S(2)}) copy-start(f32[1024,256]{1,0:T(8,128)} %copy-done.3) | copy-start | bytes 3145732
  152.9 5.0 %collective-permute-start.5 = (f32[128,256]{1,0:T(8,128)S(1)}, f32[128,256]{1,0:T(8,128)S(1)}, u32[]{:S(2)}, u32[]{:S(2)}) collective-permute-start(f32[128,256]{1,0:T(8,128)S(1)} %get-tuple-element.11.refs_0_), channel_id=1, source_target_pairs={{0,64},{64,128},{128,192},{192,0},{1,65},{65,129},{129,193},{193,1... | collective-permute-start | bytes 393224 | tf_op jit(solution)/shard_map/ppermute | solution.py:70
  154.3 6.6 %collective-permute-start.6 = (f32[128,256]{1,0:T(8,128)S(1)}, f32[128,256]{1,0:T(8,128)S(1)}, u32[]{:S(2)}, u32[]{:S(2)}) collective-permute-start(f32[128,256]{1,0:T(8,128)S(1)} %get-tuple-element.11.refs_0_), channel_id=1, source_target_pairs={{0,128},{64,192},{128,0},{192,64},{1,129},{65,193},{129,1},{193,65... | collective-permute-start | bytes 393224 | tf_op jit(solution)/shard_map/ppermute | solution.py:70
  156.7 5.1 %collective-permute-start.7 = (f32[128,256]{1,0:T(8,128)S(1)}, f32[128,256]{1,0:T(8,128)S(1)}, u32[]{:S(2)}, u32[]{:S(2)}) collective-permute-start(f32[128,256]{1,0:T(8,128)S(1)} %get-tuple-element.11.refs_0_), channel_id=1, source_target_pairs={{0,192},{64,0},{128,64},{192,128},{1,193},{65,1},{129,65},{193,129... | collective-permute-start | bytes 393224 | tf_op jit(solution)/shard_map/ppermute | solution.py:70
  161.9 8.1 %collective-permute-start.8 = (f32[512,256]{1,0:T(8,128)S(1)}, f32[512,256]{1,0:T(8,128)S(1)}, u32[]{:S(2)}, u32[]{:S(2)}) collective-permute-start(f32[512,256]{1,0:T(8,128)S(1)} %assembled.1.own), channel_id=1, source_target_pairs={{0,32},{32,0},{1,33},{33,1},{2,34},{34,2},{3,35},{35,3},{4,36},{36... | collective-permute-start | bytes 1572872 | tf_op jit(solution)/shard_map/ppermute | solution.py:38
  164.4 20.3 %all-to-all-start.6 = ((f32[256,1,256]{2,1,0:T(1,128)}), f32[256,1,256]{2,1,0:T(1,128)S(1)}, u32[]{:S(2)}, u32[]{:S(2)}) async-start(f32[256,1,256]{2,1,0:T(1,128)} %get-tuple-element.12), calls=%async_computation.6 | async-start | bytes 524288 | tf_op jit(solution)/shard_map/all_to_all | solution.py:418

commit v7 on v5

--- a/solution.py
+++ b/solution.py
@@ -41,22 +41,33 @@
 def mxu(left, right, dims):
     return lax.dot_general(left, right, (dims, ((), ())), preferred_element_type=jnp.float32)
 
+
 def parts(array):
     top = array.astype(jnp.bfloat16)
     return top, (array - top.astype(jnp.float32)).astype(jnp.bfloat16)
 
+
 def dot3(left, right, dims):
     (a, b), (c, d) = parts(left), parts(right)
     return mxu(a, c, dims) + (mxu(a, d, dims) + mxu(b, c, dims))
 
+
 def dot1(left, right, dims):
     return mxu(left.astype(jnp.bfloat16), right.astype(jnp.bfloat16), dims)
 
+
 PLAIN = ((1,), (0,))
 FLIPPED = ((1,), (1,))
 
-def core_number():
-    return lax.axis_index("c").astype(jnp.int32)[None]
+
+def place_on(axis):
+    return lax.axis_index(axis).astype(jnp.int32)[None]
+
+
+def from_others(array, axis):
+    length = lax.axis_size(axis)
+    rings = ([(i, (i + k) % length) for i in range(length)] for k in range(1, length))
+    return [array, *(lax.ppermute(array, axis, ring) for ring in rings)]
 
 
 def cost(flops):
@@ -213,31 +224,29 @@
     )(core, outgoing, received, kept)
 
 
-def spread_kernel(arrived, tiles, gram_half):
-    sides, each, _ = tiles.shape
+def summed_kernel(arrived, wide_out, gram_half):
+    sides, each = arrived.shape[0], wide_out.shape[0]
     wide = arrived[0, :each, :]
     gram = arrived[0, each:, :]
     for side in range(1, sides):
         wide = wide + arrived[side, :each, :]
         gram = gram + arrived[side, each:, :]
-    for side in range(sides):
-        tiles[side] = wide
+    wide_out[...] = wide
     gram_half[...] = gram
 
 
-def spread(arrived):
-    sides, lines, _ = arrived.shape
-    return pl.pallas_call(
-        spread_kernel,
+def summed_over_sides(arrived):
+    return pl.pallas_call(
+        summed_kernel,
         in_specs=[IN_VMEM],
         out_specs=[IN_VMEM, IN_VMEM],
         out_shape=[
-            pltpu.HBM((sides, lines - PACKED, RANK), jnp.float32),
+            jax.ShapeDtypeStruct((arrived.shape[1] - PACKED, RANK), jnp.float32),
             jax.ShapeDtypeStruct((PACKED, RANK), jnp.float32),
         ],
         cost_estimate=cost(arrived.size),
         compiler_params=limit(6),
-        name="spread",
+        name="summed",
     )(arrived)
 
 
@@ -316,31 +325,32 @@
     )(core, own, other, projected)
 
 
-def transposed_kernel(wide, inverse, out, squares):
-    c, d = parts(inverse[...])
+def transposed_kernel(line, *refs):
+    *pieces, inverse, out, squares = refs
+    right = parts(inverse[...])
     total = jnp.zeros((1, RANK), jnp.float32)
-    for t in range(wide.shape[0] // TILE):
-        span = slice(t * TILE, (t + 1) * TILE)
-        a, b = parts(wide[span, :])
-        tile = mxu(a, c, FLIPPED) + (mxu(a, d, FLIPPED) + mxu(b, c, FLIPPED))
-        out[span, :] = tile
+    for k, piece in enumerate(pieces):
+        tile = split_dot(parts(piece[...]), right, FLIPPED)
+        start = lax.rem(line[0] + len(pieces) - k, len(pieces)) * piece.shape[0]
+        out[pl.ds(pl.multiple_of(start, HALF), piece.shape[0]), :] = tile
         total += jnp.sum(tile * tile, axis=0, keepdims=True)
     squares[...] = jnp.broadcast_to(total[None], squares.shape)
 
 
-def transpose_of(wide, inverse, copies):
+def transpose_of(line, pieces, inverse, copies):
+    rows = len(pieces) * pieces[0].shape[0]
     return pl.pallas_call(
         transposed_kernel,
-        in_specs=[IN_VMEM, IN_VMEM],
+        in_specs=[IN_SMEM] + [IN_VMEM] * (len(pieces) + 1),
         out_specs=[IN_VMEM, IN_VMEM],
         out_shape=[
-            jax.ShapeDtypeStruct(wide.shape, jnp.float32),
+            jax.ShapeDtypeStruct((rows, RANK), jnp.float32),
             jax.ShapeDtypeStruct((copies, 1, RANK), jnp.float32),
         ],
-        cost_estimate=cost(6 * wide.size * RANK),
-        compiler_params=pltpu.CompilerParams(vmem_limit_bytes=8 << 20),
+        cost_estimate=cost(6 * rows * RANK * RANK),
+        compiler_params=limit(8),
         name="transposed",
-    )(wide, inverse)
+    )(line, *pieces, inverse)
 
 
 SPAN = 512
@@ -429,12 +439,12 @@
     )(core, orthonormal, own, other, squares)
 
 
-def shards(momentum, gradient, right_basis):
-    core = core_number()
+def step(momentum, gradient, right_basis):
+    core, line = place_on("c"), place_on("x")
     sides = lax.axis_size("x")
 
     part = project(momentum, gradient, right_basis)
-    part, core = lax.optimization_barrier((part, core))
+    part, core, line = lax.optimization_barrier((part, core, line))
     own = scattered(scattered(part, "y"), "z")
     projected = gathered(gathered(own, "z"), "y")
 
@@ -442,12 +452,12 @@
     received = other_core(outgoing)
     kept = widen(False, core, momentum, gradient, projected)
     tiles = merge(core, outgoing, received, kept, sides)
-    tiles, gram_half = spread(lax.all_to_all(tiles, "x", 0, 0, tiled=True))
-    wide_half = lax.all_to_all(tiles, "x", 0, 0, tiled=True).reshape(-1, RANK)
-
+    wide, gram_half = summed_over_sides(lax.all_to_all(tiles, "x", 0, 0, tiled=True))
+    pieces = from_others(wide, "x")
     inverse, orthonormal = inverted(core, gram_half, other_core(gram_half), projected)
+
     everyone = ("c", *COL)
-    own, squares = transpose_of(wide_half, inverse, lax.axis_size(everyone))
+    own, squares = transpose_of(line, pieces, inverse, lax.axis_size(everyone))
     squares = lax.all_to_all(squares, everyone, 0, 0, tiled=True)
     other = other_core(own)
     new_momentum = remembered(core, momentum, gradient, orthonormal, own, other)
@@ -459,7 +469,7 @@
     split = Mesh(mesh.devices.reshape(4, 2, 8, 4), (*ROW, *COL))
     placed = (P(ROW, COL), P(ROW, COL), P(COL, None))
     return jax.shard_map(
-        shards,
+        step,
         mesh=split,
         in_specs=placed,
         out_specs=(P(ROW, COL), P(COL, None), P(ROW, COL)),

time: 165 us -> 164 us (level)
    all_to_all x2 -> x1, starting transfers between devices: 8.24 us -> 4.26 us  [step(): squares = lax.all_to_all(squares, everyone, 0, 0, tiled=True)]
    ppermute x0 -> x3, starting transfers between devices: none -> 2.68 us  [from_others(): return [array, *(lax.ppermute(array, axis, ring) for ring in rings)]]
    all_to_all x2 -> x1, waiting for transfers between devices: 4.08 us -> 4.07 us  [step(): squares = lax.all_to_all(squares, everyone, 0, 0, tiled=True)]
  transfers between devices with their start and end apart: 5 -> 7, of which waited for: 2 -> 2; matrix products, arithmetic and copies ran while one was open for 0% -> 0% of each run, Pallas kernels for 32% -> 33%
where the time goes in v7:
time: 164 us; the launch traced here: 163 us
  blocking collectives  78.2 us (48%)
  Pallas kernels  64.4 us (39%)
  starting transfers between devices  15.2 us (9%)
  waiting for transfers between devices  4.56 us (3%)
    pallas_call x1, Pallas kernels, inverted(): pl.pallas_call(inverse_factor, in_specs=[IN_SMEM, IN_VMEM, IN_VMEM, IN_VM...  46.4 us
    all_to_all x2, blocking collectives, scattered(): return lax.all_to_all(tiles, axis, 0, 0, tiled=True).sum(axis=0)  36.3 us
    all_to_all x2, blocking collectives, from_everyone(): return lax.all_to_all(tiles, axis, 0, 0, tiled=True)  25.2 us
    all_to_all x1, blocking collectives, step(): lax.all_to_all(tiles, 'x', 0, 0, tiled=True)  16.7 us
    ppermute x3, starting transfers between devices, other_core(): return lax.ppermute(array, 'c', [(0, 1), (1, 0)])  8.26 us
    pallas_call x1, Pallas kernels, remembered(): pl.pallas_call(momentum_kernel, grid_spec=pltpu.PrefetchScalarGridSpec(nu...  5.51 us
    pallas_call x1, Pallas kernels, project(): pl.pallas_call(project_kernel, in_specs=[pl.BlockSpec(memory_space=pltpu....  4.34 us
    all_to_all x1, starting transfers between devices, step(): squares = lax.all_to_all(squares, everyone, 0, 0, tiled=True)  4.26 us
  transfers between devices with their start and end apart: 7, of which 2 were waited for; matrix products, arithmetic and copies ran while one was open for 0% of the time, Pallas kernels for 33%

profile of v7, /device:TPU:1, one launch (start us, length us, event | category | flops | bytes accessed | tf_op | source)
XLA Modules:
  0.0 163.3 jit_solution(17679026094143513484)
XLA Ops:
  0.6 4.3 %project.1 = f32[1024,256]{1,0:T(8,128)S(1)} custom-call(bf16[1024,1024]{1,0:T(8,128)(2,1)} %momentum.7, bf16[1024,1024]{1,0:T(8,128)(2,1)} %gradient.7, f32[1024,256]{1,0:T(8,128)} %basis.1), custom_call_target="tpu_custom_call" | custom-call | flops 2147483648 | tf_op jit(solution)/shard_map/project/pallas_call | solution.py:125
  5.0 19.1 %all_to_all.30 = f32[4,256,256]{2,1,0:T(8,128)S(1)} all-to-all(f32[4,256,256]{2,1,0:T(8,128)S(1)} %bitcast.9), channel_id=1, replica_groups=mesh['x'=4,'c'=2,'z'=8,'y'=4] {'y'}, dimensions={0} | all-to-all | bytes 2097152 | tf_op jit(solution)/shard_map/all_to_all | solution.py:25
  24.0 0.1 reduce_sum.18
  24.1 17.2 %all_to_all.31 = f32[8,32,256]{2,1,0:T(8,128)S(1)} all-to-all(f32[8,32,256]{2,1,0:T(8,128)S(1)} %bitcast.10), channel_id=1, replica_groups=mesh['x'=4,'c'=2,'z'=8,'y'=4] {'z'}, dimensions={0} | all-to-all | bytes 524288 | tf_op jit(solution)/shard_map/all_to_all | solution.py:25
  41.4 0.0 copy-start
  41.4 0.0 copy-start.1
  41.4 12.2 %all_to_all.32 = f32[8,32,256]{2,1,0:T(8,128)S(1)} all-to-all(f32[8,32,256]{2,1,0:T(8,128)S(1)} %broadcast_in_dim.21), channel_id=1, replica_groups=mesh['x'=4,'c'=2,'z'=8,'y'=4] {'z'}, dimensions={0} | all-to-all | bytes 524288 | tf_op jit(solution)/shard_map/all_to_all | solution.py:30
  53.6 0.1 broadcast_in_dim.23
  53.7 13.1 %all_to_all.33 = f32[4,256,256]{2,1,0:T(8,128)S(1)} all-to-all(f32[4,256,256]{2,1,0:T(8,128)S(1)} %broadcast_in_dim.23), channel_id=1, replica_groups=mesh['x'=4,'c'=2,'z'=8,'y'=4] {'y'}, dimensions={0} | all-to-all | bytes 2097152 | tf_op jit(solution)/shard_map/all_to_all | solution.py:30
  66.7 0.0 copy-done
  66.7 0.0 copy-done.1
  66.7 1.8 %widen_given.1.outgoing = f32[768,256]{1,0:T(8,128)S(1)} custom-call(s32[1]{0:T(128)} %bitcast.core, bf16[1024,1024]{1,0:T(8,128)(2,1)S(1)} %copy-done, bf16[1024,1024]{1,0:T(8,128)(2,1)S(1)} %copy-done.1, f32[1024,256]{1,0:T(8,128)S(1)} %bitcast.6), custom_call_target="tpu_custom_call" | custom-call | flops 1073741824 | tf_op jit(solution)/shard_map/widen_given/pallas_call | solution.py:159
  68.5 5.5 %collective-permute-start = (f32[768,256]{1,0:T(8,128)S(1)}, f32[768,256]{1,0:T(8,128)S(1)}, u32[]{:S(2)}, u32[]{:S(2)}) collective-permute-start(f32[768,256]{1,0:T(8,128)S(1)} %widen_given.1.outgoing), channel_id=1, source_target_pairs={{0,32},{32,0},{1,33},{33,1},{2,34},{34,2},{3,35},{35,3},{4,36},{36... | collective-permute-start | bytes 2359304 | tf_op jit(solution)/shard_map/ppermute | solution.py:38
  74.0 1.4 widen_kept.1.kept
  75.5 0.5 collective-permute-done.received
  75.9 0.1 merge.1
  76.0 16.7 %all_to_all.34.arrived = f32[4,224,256]{2,1,0:T(8,128)S(1)} all-to-all(f32[4,224,256]{2,1,0:T(8,128)S(1)} %merge.1), channel_id=1, replica_groups=mesh['x'=4,'c'=2,'z'=8,'y'=4] {'x'}, dimensions={0} | all-to-all | bytes 1835008 | tf_op jit(solution)/shard_map/all_to_all | solution.py:455
  92.8 1.9 %collective-permute-start.1 = (f32[96,256]{1,0:T(8,128)S(1)}, f32[96,256]{1,0:T(8,128)S(1)}, u32[]{:S(2)}, u32[]{:S(2)}) collective-permute-start(f32[96,256]{1,0:T(8,128)S(1)} %get-tuple-element.16.own), channel_id=1, source_target_pairs={{0,32},{32,0},{1,33},{33,1},{2,34},{34,2},{3,35},{35,3},{4,36},{36... | collective-permute-start | bytes 294920 | tf_op jit(solution)/shard_map/ppermute | solution.py:38
  94.6 0.3 collective-permute-start.2
  94.9 1.8 %collective-permute-start.3 = (f32[128,256]{1,0:T(8,128)S(1)}, f32[128,256]{1,0:T(8,128)S(1)}, u32[]{:S(2)}, u32[]{:S(2)}) collective-permute-start(f32[128,256]{1,0:T(8,128)S(1)} %get-tuple-element.19.refs_0_), channel_id=1, source_target_pairs={{0,128},{64,192},{128,0},{192,64},{1,129},{65,193},{129,1},{193,65... | collective-permute-start | bytes 393224 | tf_op jit(solution)/shard_map/ppermute | solution.py:70
  96.7 0.6 collective-permute-start.4
  97.3 0.0 collective-permute-done.1.other
  97.3 46.4 %inverse_factor.1 = (f32[256,256]{1,0:T(8,128)S(1)}, f32[1024,256]{1,0:T(8,128)S(1)}) custom-call(s32[1]{0:T(128)} %bitcast.core, f32[96,256]{1,0:T(8,128)S(1)} %get-tuple-element.16.own, f32[96,256]{1,0:T(8,128)S(1)} %collective-permute-done.1.other, f32[1024,256]{1,0:T(8,128)S(1)} %bitcast.8), custom_call_target="tpu_custom_call" | custom-call | flops 4294967296 | tf_op jit(solution)/shard_map/inverse_factor/pallas_call | solution.py:313
  143.7 0.0 collective-permute-done.2.refs_1_
  143.7 0.0 collective-permute-done.3.refs_2_
  143.7 0.0 collective-permute-done.4.refs_3_
  143.7 1.3 transposed.1
  145.0 0.9 collective-permute-start.5
  145.9 4.3 %all-to-all-start.5 = ((f32[64,1,256]{2,1,0:T(1,128)}), f32[64,1,256]{2,1,0:T(1,128)S(1)}, u32[]{:S(2)}, u32[]{:S(2)}) async-start(f32[64,1,256]{2,1,0:T(1,128)} %get-tuple-element.22), calls=%async_computation.5 | async-start | bytes 131072 | tf_op jit(solution)/shard_map/all_to_all | solution.py:461
  150.2 0.0 collective-permute-done.5.other
  150.2 5.5 %new_momentum.1 = bf16[1024,1024]{1,0:T(8,128)(2,1)} custom-call(s32[1]{0:T(128)} %bitcast.core, bf16[1024,1024]{1,0:T(8,128)(2,1)} %momentum.7, bf16[1024,1024]{1,0:T(8,128)(2,1)} %gradient.7, f32[1024,256]{1,0:T(8,128)S(1)} %get-tuple-element.17.orthonormal, f32[512,256]{1,0:T(8,128)S(1)} %get-tuple-element.21.own, f32[512,256]{1,0:T(8,128)S(1)} %collective-permute-done.5.other), custom_call_target="tpu_custom_call" | custom-call | flops 4294967296 | tf_op jit(solution)/shard_map/new_momentum/pallas_call | solution.py:377
  155.7 4.1 %all-to-all-done.5.squares = f32[64,1,256]{2,1,0:T(1,128)S(1)} async-done(((f32[64,1,256]{2,1,0:T(1,128)}), f32[64,1,256]{2,1,0:T(1,128)S(1)}, u32[]{:S(2)}, u32[]{:S(2)}) %all-to-all-start.5) | async-done | bytes 65568 | tf_op jit(solution)/shard_map/all_to_all | solution.py:461
  159.8 3.5 %update.1 = (f32[1024,1024]{1,0:T(8,128)}, f32[1024,256]{1,0:T(8,128)}) custom-call(s32[1]{0:T(128)} %bitcast.core, f32[1024,256]{1,0:T(8,128)S(1)} %get-tuple-element.17.orthonormal, f32[512,256]{1,0:T(8,128)S(1)} %get-tuple-element.21.own, f32[512,256]{1,0:T(8,128)S(1)} %collective-permute-done.5.other, f32[64,1,256]{2,1,0:T(1,128)S(1)} %all-to-all-done.5.squares), custom_call_target="tpu_custom_call" | custom-call | flops 1610612736 | tf_op jit(solution)/shard_map/update/pallas_call | solution.py:415
  (3 shorter events, 0.1 us)
Async XLA Ops:
  41.4 25.4 %copy-start = (bf16[1024,1024]{1,0:T(8,128)(2,1)S(1)}, bf16[1024,1024]{1,0:T(8,128)(2,1)}, u32[]{:S(2)}) copy-start(bf16[1024,1024]{1,0:T(8,128)(2,1)} %momentum.7) | copy-start | bytes 6291460
  41.4 25.4 %copy-start.1 = (bf16[1024,1024]{1,0:T(8,128)(2,1)S(1)}, bf16[1024,1024]{1,0:T(8,128)(2,1)}, u32[]{:S(2)}) copy-start(bf16[1024,1024]{1,0:T(8,128)(2,1)} %gradient.7) | copy-start | bytes 6291460
  68.5 7.4 %collective-permute-start = (f32[768,256]{1,0:T(8,128)S(1)}, f32[768,256]{1,0:T(8,128)S(1)}, u32[]{:S(2)}, u32[]{:S(2)}) collective-permute-start(f32[768,256]{1,0:T(8,128)S(1)} %widen_given.1.outgoing), channel_id=1, source_target_pairs={{0,32},{32,0},{1,33},{33,1},{2,34},{34,2},{3,35},{35,3},{4,36},{36... | collective-permute-start | bytes 2359304 | tf_op jit(solution)/shard_map/ppermute | solution.py:38
  92.8 4.6 %collective-permute-start.1 = (f32[96,256]{1,0:T(8,128)S(1)}, f32[96,256]{1,0:T(8,128)S(1)}, u32[]{:S(2)}, u32[]{:S(2)}) collective-permute-start(f32[96,256]{1,0:T(8,128)S(1)} %get-tuple-element.16.own), channel_id=1, source_target_pairs={{0,32},{32,0},{1,33},{33,1},{2,34},{34,2},{3,35},{35,3},{4,36},{36... | collective-permute-start | bytes 294920 | tf_op jit(solution)/shard_map/ppermute | solution.py:38
  94.6 49.1 %collective-permute-start.2 = (f32[128,256]{1,0:T(8,128)S(1)}, f32[128,256]{1,0:T(8,128)S(1)}, u32[]{:S(2)}, u32[]{:S(2)}) collective-permute-start(f32[128,256]{1,0:T(8,128)S(1)} %get-tuple-element.19.refs_0_), channel_id=1, source_target_pairs={{0,64},{64,128},{128,192},{192,0},{1,65},{65,129},{129,193},{193,1... | collective-permute-start | bytes 393224 | tf_op jit(solution)/shard_map/ppermute | solution.py:70
  94.9 48.8 %collective-permute-start.3 = (f32[128,256]{1,0:T(8,128)S(1)}, f32[128,256]{1,0:T(8,128)S(1)}, u32[]{:S(2)}, u32[]{:S(2)}) collective-permute-start(f32[128,256]{1,0:T(8,128)S(1)} %get-tuple-element.19.refs_0_), channel_id=1, source_target_pairs={{0,128},{64,192},{128,0},{192,64},{1,129},{65,193},{129,1},{193,65... | collective-permute-start | bytes 393224 | tf_op jit(solution)/shard_map/ppermute | solution.py:70
  96.7 47.0 %collective-permute-start.4 = (f32[128,256]{1,0:T(8,128)S(1)}, f32[128,256]{1,0:T(8,128)S(1)}, u32[]{:S(2)}, u32[]{:S(2)}) collective-permute-start(f32[128,256]{1,0:T(8,128)S(1)} %get-tuple-element.19.refs_0_), channel_id=1, source_target_pairs={{0,192},{64,0},{128,64},{192,128},{1,193},{65,1},{129,65},{193,129... | collective-permute-start | bytes 393224 | tf_op jit(solution)/shard_map/ppermute | solution.py:70
  145.0 5.1 %collective-permute-start.5 = (f32[512,256]{1,0:T(8,128)S(1)}, f32[512,256]{1,0:T(8,128)S(1)}, u32[]{:S(2)}, u32[]{:S(2)}) collective-permute-start(f32[512,256]{1,0:T(8,128)S(1)} %get-tuple-element.21.own), channel_id=1, source_target_pairs={{0,32},{32,0},{1,33},{33,1},{2,34},{34,2},{3,35},{35,3},{4,36},{36... | collective-permute-start | bytes 1572872 | tf_op jit(solution)/shard_map/ppermute | solution.py:38
  145.9 13.9 %all-to-all-start.5 = ((f32[64,1,256]{2,1,0:T(1,128)}), f32[64,1,256]{2,1,0:T(1,128)S(1)}, u32[]{:S(2)}, u32[]{:S(2)}) async-start(f32[64,1,256]{2,1,0:T(1,128)} %get-tuple-element.22), calls=%async_computation.5 | async-start | bytes 131072 | tf_op jit(solution)/shard_map/all_to_all | solution.py:461
